TPU v7x, 512 devices: a whole 4x4x16 slice. The times are simulated.
512 devices in a mesh: row: 64 (over y_hi, z, core), head: 8 (over x, y_lo).
Axes of the slice: x: 4, y: 4 (y_hi: 2, y_lo: 2; y = y_hi * 2 + y_lo), z: 16, core: 2. Of those that a mesh axis runs over, the one named last changes fastest.
Arguments:
- pair_input: bfloat16 [512, 512, 128], P(('row', 'head')), may hold values from -6 to 6
- cotangent: bfloat16 [512, 512, 128], P(('row', 'head')), may hold values from -24 to 24
- residue_mask: int32 [512], replicated, may hold values from 0 to 1, as said below
- norm_gain: float32 [2, 128], replicated, may hold values from 0.5 to 1.5
- norm_shift: float32 [2, 128], replicated, may hold values from -3 to 3
- proj_weights: bfloat16 [2, 4, 128, 128], replicated, may hold values from -0.5 to 0.5
- gate_bias: float32 [2, 128], replicated, may hold values from -4 to 4
- out_weights: bfloat16 [2, 128, 128], replicated, may hold values from -1.0546875 to 1.0546875
- bias_weights: bfloat16 [2, 128, 4], replicated, may hold values from -1.06066017 to 1.06066017
Outputs:
- pair_grad: float32 [512, 512, 128], P(('row', 'head'))
- proj_grad: float32 [2, 4, 128, 128], replicated
- gate_bias_grad: float32 [2, 128], replicated
- out_grad: float32 [2, 128, 128], replicated
- bias_weight_grad: float32 [2, 128, 4], replicated
- gain_grad: float32 [2, 128], replicated
- shift_grad: float32 [2, 128], replicated
Inputs may be any that keep to these rules, and one draw needn't show every extreme that they name: `residue_mask`: 1 for the first residues of the crop and 0 for the padding after them; at least half of the 512 residues are 1.
All inputs are finite; a program needn't handle non-finite values.
Results may differ from a plain program's by a relative error of at most 0.02.
The roundings to bfloat16 on the way count: a program that leaves them out, or rounds other values in their place, can miss the bound.
Values may be sent and summed in bfloat16 or wider, within the bound.
No kernel may reach another device: no remote copies, remote signals or barrier semaphores. Data moves between devices by JAX's collectives and lax.ppermute only.
A program may use at most 64 MiB of HBM per device.

v0:
```python
import math

import jax
import jax.numpy as jnp
from jax import lax
from jax.sharding import Mesh
from jax.sharding import PartitionSpec as P

HEAD = ("head_0", "head_1")
ROW_HEAD = ("row", "head_0", "head_1")


EPS = 1e-05
MASKED = 1000000000.0


def whole_of(x, axes, dim):
    for axis in reversed(axes):
        x = lax.all_gather(x, axis, axis=dim, tiled=True)
    return x


def joined_along(parts, dim):
    parts = jnp.moveaxis(parts, 0, dim)
    dims = parts.shape
    return parts.reshape(*dims[:dim], dims[dim] * dims[dim + 1], *dims[dim + 2 :])


def from_everyone(x, axis):
    length = lax.axis_size(axis)
    return lax.all_to_all(jnp.broadcast_to(x[None], (length, *x.shape)), axis, 0, 0, tiled=True)


def gather_directly(x, axis, dim):
    return joined_along(from_everyone(x, axis), dim)


def split_up(x, dim, length):
    dims = x.shape
    parts = x.reshape(*dims[:dim], length, dims[dim] // length, *dims[dim + 1 :])
    return jnp.moveaxis(parts, dim, 0)


def sent_and_summed(x, axis, dim):
    length = lax.axis_size(axis)
    parts = lax.all_to_all(split_up(x, dim, length), axis, 0, 0, tiled=True)
    return jnp.sum(parts.astype(jnp.float32), axis=0)


def summed_on_arrival(x, axis, dim):
    parts = split_up(x, dim, lax.axis_size(axis))
    arrived = lax.all_to_all(parts, axis, split_axis=0, concat_axis=0, tiled=True)
    return arrived.sum(axis=0)


def joined_exchange(x, axis, axes, splits, concats):
    sizes = [lax.axis_size(a) for a in axes]
    parts = split_up(x, splits[0], sizes[0])
    parts = jnp.moveaxis(split_up(parts, splits[1] + 1, sizes[1]), 0, 1)
    inside = parts.shape[2:]
    parts = parts.reshape(-1, *inside)
    parts = lax.all_to_all(parts, axis, split_axis=0, concat_axis=0, tiled=True)
    parts = joined_along(parts.reshape(*sizes, *inside), concats[0] + 1)
    return joined_along(parts, concats[1])


def layer_norm(values, norm_scale, norm_offset):
    floats = values.astype(jnp.float32)
    centred = floats - jnp.mean(floats, axis=-1, keepdims=True)
    inverse = lax.rsqrt(jnp.mean(centred * centred, axis=-1, keepdims=True) + EPS)
    normed = centred * inverse
    return (normed, inverse, (normed * norm_scale + norm_offset).astype(jnp.bfloat16))


def norm_backward(grad_normal, normed, inverse, norm_scale):
    grad_hat = grad_normal * norm_scale
    first_mean = jnp.mean(grad_hat, axis=-1, keepdims=True)
    second_mean = jnp.mean(grad_hat * normed, axis=-1, keepdims=True)
    return inverse * (grad_hat - first_mean - normed * second_mean)


def class_columns(values, head_index, row_count, head_count, slab_rows):
    leading = values.shape[0]
    shaped = values.reshape(leading, row_count, head_count, slab_rows, values.shape[-1])
    picked = lax.dynamic_index_in_dim(shaped, head_index, axis=2, keepdims=False)
    return picked.reshape(leading, row_count * slab_rows, values.shape[-1])


def forward_block(pair_rows, key_bias, params, layout):
    norm_scale, norm_offset, projection, gate_offset, out_proj, bias_proj = params
    slab_rows, row_count, head_count, head_index = layout
    head_total = bias_proj.shape[1]
    inner_width = projection.shape[2]
    head_size = inner_width // head_total
    query_scale = 1.0 / math.sqrt(head_size)
    normed, inverse, normal_own = layer_norm(pair_rows, norm_scale, norm_offset)
    normal_rows = whole_of(normal_own, HEAD, 0)
    bias_own = jnp.einsum(
        "snc,ch->hsn", normal_own, bias_proj, preferred_element_type=jnp.float32
    ).astype(jnp.bfloat16)
    bias_query = gather_directly(bias_own, "row", 1)
    normal_query = class_columns(normal_rows, head_index, row_count, head_count, slab_rows)
    block_rows = normal_query.shape[0]
    query_count = normal_query.shape[1]
    key_count = normal_rows.shape[1]
    queries = (
        jnp.dot(normal_query, projection[0], preferred_element_type=jnp.float32) * query_scale
    ).astype(jnp.bfloat16)
    joined_weights = jnp.concatenate([projection[1], projection[2]], axis=1)
    key_value = jnp.dot(normal_rows, joined_weights, preferred_element_type=jnp.float32).astype(
        jnp.bfloat16
    )
    gate_values = jax.nn.sigmoid(
        jnp.dot(normal_query, projection[3], preferred_element_type=jnp.float32) + gate_offset
    )
    head_queries = queries.reshape(block_rows, query_count, head_total, head_size).transpose(
        2, 0, 1, 3
    )
    head_pairs = key_value.reshape(block_rows, key_count, 2, head_total, head_size).transpose(
        2, 3, 0, 1, 4
    )

    def attend(inputs):
        query_head, key_head, value_head, bias_head = inputs
        logits = jnp.einsum(
            "rqd,rnd->rqn", query_head, key_head, preferred_element_type=jnp.float32
        )
        logits = logits + bias_head.astype(jnp.float32)[None] + key_bias
        largest = jnp.max(logits, axis=-1, keepdims=True)
        weights = jnp.exp(logits - largest)
        total = jnp.sum(weights, axis=-1, keepdims=True)
        soft_weights = weights / total
        attended = jnp.einsum(
            "rqn,rnd->rqd",
            soft_weights.astype(jnp.bfloat16),
            value_head,
            preferred_element_type=jnp.float32,
        )
        return ((largest + jnp.log(total))[..., 0], attended)

    log_totals, attended = lax.map(attend, (head_queries, head_pairs[0], head_pairs[1], bias_query))
    attended = attended.transpose(1, 2, 0, 3).reshape(block_rows, query_count, inner_width)
    gated_out = (gate_values * attended).astype(jnp.bfloat16)
    update = jnp.dot(gated_out, out_proj, preferred_element_type=jnp.float32).astype(jnp.bfloat16)
    saved_state = (
        normed,
        inverse,
        normal_own,
        normal_rows,
        normal_query,
        head_queries,
        head_pairs,
        bias_query,
        gate_values,
        attended,
        gated_out,
        log_totals,
    )
    return (saved_state, update)


def backward_block(saved_state, grad_query, key_bias, params, layout):
    norm_scale, norm_offset, projection, gate_offset, out_proj, bias_proj = params
    slab_rows, row_count, head_count, head_index = layout
    (
        normed,
        inverse,
        normal_own,
        normal_rows,
        normal_query,
        head_queries,
        head_pairs,
        bias_query,
        gate_values,
        attended,
        gated_out,
        log_totals,
    ) = saved_state
    channels = normal_own.shape[2]
    head_total, block_rows, query_count, head_size = head_queries.shape
    key_count = normal_rows.shape[1]
    inner_width = head_total * head_size
    query_scale = 1.0 / math.sqrt(head_size)
    grad_gated = jnp.dot(grad_query, out_proj.T, preferred_element_type=jnp.float32)
    grad_att = (grad_gated * gate_values).astype(jnp.bfloat16)
    grad_pre = (grad_gated * attended * gate_values * (1.0 - gate_values)).astype(jnp.bfloat16)
    head_grads = grad_att.reshape(block_rows, query_count, head_total, head_size).transpose(
        2, 0, 1, 3
    )

    def differentiate(inputs):
        total_head, query_head, key_head, value_head, bias_head, grad_head = inputs
        logits = jnp.einsum(
            "rqd,rnd->rqn", query_head, key_head, preferred_element_type=jnp.float32
        )
        logits = logits + bias_head.astype(jnp.float32)[None] + key_bias
        soft_weights = jnp.exp(logits - total_head[..., None])
        grad_weights = jnp.einsum(
            "rqd,rnd->rqn", grad_head, value_head, preferred_element_type=jnp.float32
        )
        grad_logits = soft_weights * (
            grad_weights - jnp.sum(soft_weights * grad_weights, axis=-1, keepdims=True)
        )
        logits_half = grad_logits.astype(jnp.bfloat16)
        grad_queries = (
            jnp.einsum("rqn,rnd->rqd", logits_half, key_head, preferred_element_type=jnp.float32)
            * query_scale
        ).astype(jnp.bfloat16)
        grad_keys = jnp.einsum(
            "rqn,rqd->rnd", logits_half, query_head, preferred_element_type=jnp.float32
        ).astype(jnp.bfloat16)
        grad_values = jnp.einsum(
            "rqn,rqd->rnd",
            soft_weights.astype(jnp.bfloat16),
            grad_head,
            preferred_element_type=jnp.float32,
        ).astype(jnp.bfloat16)
        return (grad_queries, grad_keys, grad_values, jnp.sum(grad_logits, axis=0))

    grad_queries, grad_keys, grad_values, grad_bias = lax.map(
        differentiate,
        (log_totals, head_queries, head_pairs[0], head_pairs[1], bias_query, head_grads),
    )
    grad_queries = grad_queries.transpose(1, 2, 0, 3).reshape(block_rows, query_count, inner_width)
    key_weights = projection[1].reshape(channels, head_total, head_size).transpose(1, 2, 0)
    value_weights = projection[2].reshape(channels, head_total, head_size).transpose(1, 2, 0)
    query_side = jnp.dot(grad_queries, projection[0].T, preferred_element_type=jnp.float32)
    query_side = query_side + jnp.dot(grad_pre, projection[3].T, preferred_element_type=jnp.float32)
    count = slab_rows * lax.axis_size(HEAD)
    term = jnp.einsum("hrnd,hdc->rnc", grad_keys, key_weights, preferred_element_type=jnp.float32)
    term = term + jnp.einsum(
        "hrnd,hdc->rnc", grad_values, value_weights, preferred_element_type=jnp.float32
    )
    shaped = term.reshape(count, row_count, head_count, slab_rows, channels)
    current = lax.dynamic_slice_in_dim(shaped, head_index, 1, 2)
    query_slice = query_side.reshape(count, row_count, 1, slab_rows, channels)
    shaped = lax.dynamic_update_slice_in_dim(shaped, current + query_slice, head_index, 2)
    grad_normal = sent_and_summed(
        shaped.reshape(count, key_count, channels).astype(jnp.bfloat16), HEAD, 0
    )
    bias_total = summed_on_arrival(grad_bias, "row", 1)
    bias_half = bias_total.astype(jnp.bfloat16)
    grad_normal = grad_normal + jnp.einsum(
        "hsn,ch->snc", bias_half, bias_proj, preferred_element_type=jnp.float32
    )
    grad_pair = norm_backward(grad_normal, normed, inverse, norm_scale)
    projection_grads = jnp.stack(
        [
            jnp.einsum(
                "rqc,rqe->ce", normal_query, grad_queries, preferred_element_type=jnp.float32
            ),
            jnp.einsum(
                "rnc,hrnd->chd", normal_rows, grad_keys, preferred_element_type=jnp.float32
            ).reshape(channels, inner_width),
            jnp.einsum(
                "rnc,hrnd->chd", normal_rows, grad_values, preferred_element_type=jnp.float32
            ).reshape(channels, inner_width),
            jnp.einsum("rqc,rqe->ce", normal_query, grad_pre, preferred_element_type=jnp.float32),
        ]
    )
    weight_grads = (
        projection_grads,
        jnp.sum(grad_pre.astype(jnp.float32), axis=(0, 1)),
        jnp.einsum("rqe,rqc->ec", gated_out, grad_query, preferred_element_type=jnp.float32),
        jnp.einsum("snc,hsn->ch", normal_own, bias_half, preferred_element_type=jnp.float32),
        jnp.sum(grad_normal * normed, axis=(0, 1)),
        jnp.sum(grad_normal, axis=(0, 1)),
    )
    return (grad_pair, weight_grads)


def to_queries(grad_rows, layout):
    slab_rows, row_count, head_count, head_index = layout
    channels = grad_rows.shape[2]
    shaped = grad_rows.reshape(slab_rows, row_count, head_count, slab_rows, channels)
    moved = lax.all_to_all(shaped, HEAD, split_axis=2, concat_axis=0, tiled=True)
    return moved.reshape(slab_rows * head_count, row_count * slab_rows, channels)


def local(
    pair_input,
    cotangent,
    residue_mask,
    norm_gain,
    norm_shift,
    proj_weights,
    gate_bias,
    out_weights,
    bias_weights,
):
    slab_rows = pair_input.shape[0]
    channels = pair_input.shape[2]
    row_count = lax.axis_size("row")
    head_count = lax.axis_size(HEAD)
    layout = (slab_rows, row_count, head_count, lax.axis_index(HEAD))
    key_bias = (residue_mask.astype(jnp.float32) - 1.0) * MASKED
    params = [
        (
            norm_gain[which],
            norm_shift[which],
            proj_weights[which],
            gate_bias[which],
            out_weights[which],
            bias_weights[which],
        )
        for which in range(2)
    ]
    first_state, first_update = forward_block(pair_input, key_bias, params[0], layout)
    returned = lax.all_to_all(
        first_update.reshape(slab_rows * head_count, row_count, 1, slab_rows, channels),
        HEAD,
        split_axis=0,
        concat_axis=2,
        tiled=True,
    )
    after_first = (
        pair_input.astype(jnp.float32)
        + returned.reshape(slab_rows, -1, channels).astype(jnp.float32)
    ).astype(jnp.bfloat16)
    joined = jnp.concatenate([after_first, cotangent], axis=2)
    moved = joined_exchange(
        joined.reshape(1, 1, slab_rows, row_count, head_count, slab_rows, 2 * channels),
        ROW_HEAD,
        ("row", HEAD),
        (3, 4),
        (0, 1),
    )
    flipped = moved.reshape(-1, slab_rows, 2 * channels).transpose(1, 0, 2)
    second_state, second_update = forward_block(
        flipped[:, :, :channels], key_bias, params[1], layout
    )
    second_grad, second_weights = backward_block(
        second_state, to_queries(flipped[:, :, channels:], layout), key_bias, params[1], layout
    )
    sent_back = joined_exchange(
        second_grad.astype(jnp.bfloat16).reshape(
            1, 1, slab_rows, row_count, head_count, slab_rows, channels
        ),
        ROW_HEAD,
        ("row", HEAD),
        (3, 4),
        (0, 1),
    )
    end_grad = sent_back.reshape(-1, slab_rows, channels).transpose(1, 0, 2)
    grad_after = cotangent.astype(jnp.float32) + end_grad.astype(jnp.float32)
    start_grad, first_weights = backward_block(
        first_state,
        to_queries(grad_after.astype(jnp.bfloat16), layout),
        key_bias,
        params[0],
        layout,
    )
    pair_grad = grad_after + start_grad
    combined = [
        jnp.stack([start_part, end_part])
        for start_part, end_part in zip(first_weights, second_weights)
    ]
    stacked = lax.psum(
        (combined[0], combined[1], combined[2], combined[3], combined[4], combined[5]), ROW_HEAD
    )
    return (pair_grad, stacked[0], stacked[1], stacked[2], stacked[3], stacked[4], stacked[5])


def solution(mesh):
    finer = Mesh(mesh.devices.reshape(mesh.shape["row"], 4, 2), ("row", "head_0", "head_1"))
    in_specs = (P(ROW_HEAD, None, None), P(ROW_HEAD, None, None), P(), P(), P(), P(), P(), P(), P())
    out_specs = (P(ROW_HEAD, None, None), P(), P(), P(), P(), P(), P())
    return jax.shard_map(local, mesh=finer, in_specs=in_specs, out_specs=out_specs, check_vma=False)
```

profile of v0, /device:TPU:1, one launch (start us, length us, event | category | flops | bytes accessed | tf_op | source)
XLA Modules:
  0.0 951.6 jit_solution(1266465462356417426)
XLA Ops:
  11.9 5.2 all_gather.12
  18.7 20.5 %all-to-all-start = ((bf16[64,4,1,512]{3,1,2,0:T(4,128)(2,1)}), bf16[64,4,1,512]{3,1,2,0:T(4,128)(2,1)S(1)}, u32[]{:S(2)}, u32[]{:S(2)}) async-start(bf16[64,4,1,512]{3,1,2,0:T(4,128)(2,1)} %broadcast_in_dim.57), calls=%async_computation | async-start | bytes 524288 | tf_op jit(solution)/shard_map/all_to_all | solution.py:31
  40.8 22.2 %all-to-all-done = bf16[64,4,1,512]{3,1,2,0:T(4,128)(2,1)S(1)} async-done(((bf16[64,4,1,512]{3,1,2,0:T(4,128)(2,1)}), bf16[64,4,1,512]{3,1,2,0:T(4,128)(2,1)S(1)}, u32[]{:S(2)}, u32[]{:S(2)}) %all-to-all-start) | async-done | bytes 262176 | tf_op jit(solution)/shard_map/all_to_all | solution.py:31
  68.0 11.2 %while.56 = (s32[]{:T(128)}, f32[4,8,64]{2,1,0:T(8,128)}, f32[4,8,64,32]{2,3,1,0:T(8,128)S(1)}, bf16[4,8,64,32]{2,3,1,0:T(8,128)(2,1)S(1)}, bf16[4,8,512,32]{2,3...) while((s32[]{:T(128)}, f32[4,8,64]{2,1,0:T(8,128)}, ...), condition=%wide.region_5.6_spmd, body=%wide.region_2.5_spmd.sunk | while | flops 35683840 | bytes 4221537 | solution.py:141
  81.3 9.2 all_to_all.79
  92.2 36.4 %all_to_all.80 = bf16[512,2,128]{2,1,0:T(2,128)(2,1)S(1)} all-to-all(bf16[512,2,128]{2,1,0:T(2,128)(2,1)S(1)} %reshape.464), channel_id=1, replica_groups=mesh['row'=64,'head_0'=4,'head_1'=2] {'row','head_0','head_1'}, dimensions={0} | all-to-all | bytes 524288 | tf_op jit(solution)/shard_map/all_to_all | solution.py:62
  129.4 6.0 all_gather.14
  136.1 3.4 all-to-all-start.4
  139.6 5.0 all-to-all-done.4
  145.4 6.2 all-to-all-start.3
  152.1 23.3 %all-to-all-done.3 = bf16[64,4,1,512]{3,1,2,0:T(4,128)(2,1)S(1)} async-done(((bf16[64,4,1,512]{3,1,2,0:T(4,128)(2,1)}), bf16[64,4,1,512]{3,1,2,0:T(4,128)(2,1)S(1)}, u32[]{:S(2)}, u32[]{:S(2)}) %all-to-all-start.3) | async-done | bytes 262176 | tf_op jit(solution)/shard_map/all_to_all | solution.py:31
  176.1 1.9 convolution_convert_fusion.4
  182.5 18.3 %while.57 = (s32[]{:T(128)}, f32[4,8,64]{2,1,0:T(8,128)}, f32[4,8,64,32]{2,3,1,0:T(8,128)S(1)}, bf16[4,8,64,32]{2,3,1,0:T(8,128)(2,1)S(1)}, bf16[4,8,512,32]{2,3...) while((s32[]{:T(128)}, f32[4,8,64]{2,1,0:T(8,128)}, ...), condition=%wide.region_11.12_spmd, body=%wide.region_8.11_spmd.sunk | while | flops 35683840 | bytes 4221537 | solution.py:141
  207.3 51.8 %while.58 = (s32[]{:T(128)}, bf16[4,8,64,32]{2,3,1,0:T(8,128)(2,1)}, bf16[4,8,512,32]{2,3,1,0:T(8,128)(2,1)}, bf16[4,8,512,32]{2,3,1,0:T(8,128)(2,1)}, f32[4,64,...) while((s32[]{:T(128)}, ...), condition=%wide.region_15.16_spmd, body=%wide.region_12.15_spmd.sunk | while | flops 86801920 | bytes 10505361 | solution.py:220
  213.0 3.6 dynamic_update_slice.78
  218.4 1.8 fusion.298
  225.9 3.6 dynamic_update_slice.78
  231.4 1.8 fusion.298
  238.9 3.6 dynamic_update_slice.78
  244.3 1.8 fusion.298
  251.8 3.6 dynamic_update_slice.78
  257.2 1.8 fusion.298
  264.6 6.1 dynamic_update_slice.47
  270.9 18.0 %all_to_all.81 = bf16[8,1,512,128]{3,2,1,0:T(8,128)(2,1)S(1)} all-to-all(bf16[8,1,512,128]{3,2,1,0:T(8,128)(2,1)S(1)} %convert_bitcast_fusion.1), channel_id=1, replica_groups=mesh['row'=64,'head_0'=4,'head_1'=2] {'head_0','head_1'}, dimensions={0} | all-to-all | bytes 2097152 | tf_op jit(solution)/shard_map/all_to_all | solution.py:46
  288.8 4.7 all-to-all-start.6
  294.4 32.6 %all-to-all-done.6 = f32[64,4,1,512]{3,1,2,0:T(4,128)S(1)} async-done(((f32[64,4,1,512]{3,1,2,0:T(4,128)}), f32[64,4,1,512]{3,1,2,0:T(4,128)S(1)}, u32[]{:S(2)}, u32[]{:S(2)}) %all-to-all-start.6) | async-done | bytes 524320 | tf_op jit(solution)/shard_map/all_to_all | solution.py:52
  327.1 1.9 fusion.141
  331.6 9.3 all-to-all-start.7
  340.9 24.7 %all-to-all-done.7 = bf16[512,1,1,1,1,1,1,128]{7,6,5,4,3,2,1,0:T(2,128)(2,1)S(1)} async-done(((bf16[512,1,1,1,1,1,1,128]{7,6,5,4,3,2,1,0:T(2,128)(2,1)}), bf16[512,1,1,1,1,1,1,128]{7,6,5,4,3,2,1,0:T(2,128)(2,1)S(1)}, u32[]{:S(2)}, u32[]{:S(2)}) %all-to-all-start.7) | async-done | bytes 131104 | tf_op jit(solution)/shard_map/all_to_all | solution.py:62
  367.2 3.4 all-to-all-start.8
  373.0 2.8 all-to-all-done.8
  381.1 40.7 %while.59 = (s32[]{:T(128)}, bf16[4,8,64,32]{2,3,1,0:T(8,128)(2,1)}, bf16[4,8,512,32]{2,3,1,0:T(8,128)(2,1)}, bf16[4,8,512,32]{2,3,1,0:T(8,128)(2,1)}, f32[4,64,...) while((s32[]{:T(128)}, ...), condition=%wide.region_23.24_spmd, body=%wide.region_20.23_spmd.sunk | while | flops 86801920 | bytes 10505361 | solution.py:220
  385.8 3.6 dynamic_update_slice.82
  396.0 3.6 dynamic_update_slice.82
  406.1 3.6 dynamic_update_slice.82
  416.3 3.6 dynamic_update_slice.82
  427.3 6.1 dynamic_update_slice.48
  434.5 3.7 all-to-all-start.9
  438.2 2.3 fusion.107
  442.1 1.8 convolution_bitcast_fusion.4
  445.8 2.0 convolution_bitcast_fusion.2
  447.7 5.1 all-to-all-done.9
  452.8 6.7 all-to-all-start.10
  461.4 2.3 fusion.113
  470.6 22.2 %all-to-all-done.10 = f32[64,4,1,512]{3,1,2,0:T(4,128)} async-done(((f32[64,4,1,512]{3,1,2,0:T(4,128)}), f32[64,4,1,512]{3,1,2,0:T(4,128)}, u32[]{:S(2)}, u32[]{:S(2)}) %all-to-all-start.10) | async-done | bytes 524320 | tf_op jit(solution)/shard_map/all_to_all | solution.py:52
  494.8 100.0 %all-reduce = (f32[2,128]{1,0:T(2,128)}, f32[2,128,4]{1,2,0:T(4,128)}, f32[2,128]{1,0:T(2,128)}, f32[2,128]{1,0:T(2,128)}) all-reduce(f32[2,128]{1,0:T(2,128)S(1)} %pad_maximum_fusion.3, f32[2,128,4]{1,2,0:T(4,128)S(1)} %pad_maximum_fusion.2, ...), channel_id=1, replica_groups=mesh['row'=64,'head_0'=4,'head_1'=2] {'row','head_0','head_1'}, use_global_device_ids=true, to_apply=%region_31.32 | all-reduce | flops 1792 | bytes 14336 | tf_op jit(solution)/shard_map/psum | solution.py:358
  595.8 345.8 %all-reduce.4.cloned.1.call-done = (f32[2,4,128,128]{3,2,1,0:T(8,128)}, f32[2,128,128]{2,1,0:T(8,128)}) async-done(((f32[2,4,128,128]{3,2,1,0:T(8,128)}, f32[2,128,128]{2,1,0:T(8,128)}), (f32[2,4,128,128]{3,2,1,0:T(8,128)}, f32[2,128,128]{2,1,0:T(8,128)})) %all-reduce.4.cloned.1.call-update) | async-done | bytes 655376 | tf_op jit(solution)/shard_map/psum | solution.py:358
  941.6 1.9 copy.317
  (382 shorter events, 157.2 us)
Async XLA Ops:
  7.2 32.2 %copy-start.40 = (bf16[2,4,128,128]{3,2,1,0:T(8,128)(2,1)S(1)}, bf16[2,4,128,128]{3,2,1,0:T(8,128)(2,1)}, u32[]{:S(2)}) copy-start(bf16[2,4,128,128]{3,2,1,0:T(8,128)(2,1)} %param.22) | copy-start | bytes 786436
  7.2 33.1 %copy-start.68 = (f32[2,128]{1,0:T(2,128)S(1)}, f32[2,128]{1,0:T(2,128)}, u32[]{:S(2)}) copy-start(f32[2,128]{1,0:T(2,128)} %param.23) | copy-start | bytes 3076
  7.2 33.6 %copy-start.66 = (s32[512]{0:T(512)S(1)}, s32[512]{0:T(512)}, u32[]{:S(2)}) copy-start(s32[512]{0:T(512)} %param.19) | copy-start | bytes 6148
  7.2 55.9 %all-gather.3.cloned.1.call-start = ((), (), s32[]{:S(2)}) async-start(), calls=%async_computation.11 | async-start | bytes 1310720 | tf_op jit(solution)/shard_map/all_gather | solution.py:19
  9.5 30.8 %copy-start.53 = (f32[512]{0:T(512)}, f32[512]{0:T(512)S(1)}, u32[]{:S(2)}) copy-start(f32[512]{0:T(512)S(1)} %add_rsqrt_fusion.1) | copy-start | bytes 6148
  10.7 118.4 %copy-start.59 = (f32[128]{0:T(128)}, f32[128]{0:T(128)S(1)}, u32[]{:S(2)}) copy-start(f32[128]{0:T(128)S(1)} %get-tuple-element.487) | copy-start | bytes 1540
  11.9 53.3 %copy-start.18 = (bf16[1,512,128]{2,1,0:T(8,128)(2,1)}, bf16[1,512,128]{2,1,0:T(8,128)(2,1)S(1)}, u32[]{:S(2)}) copy-start(bf16[1,512,128]{2,1,0:T(8,128)(2,1)S(1)} %fusion.128) | copy-start | bytes 393220
  18.7 44.3 %all-to-all-start = ((bf16[64,4,1,512]{3,1,2,0:T(4,128)(2,1)}), bf16[64,4,1,512]{3,1,2,0:T(4,128)(2,1)S(1)}, u32[]{:S(2)}, u32[]{:S(2)}) async-start(bf16[64,4,1,512]{3,1,2,0:T(4,128)(2,1)} %broadcast_in_dim.57), calls=%async_computation | async-start | bytes 524288 | tf_op jit(solution)/shard_map/all_to_all | solution.py:31
  39.3 136.8 %all-gather.5.cloned.1.call-start = ((), (), s32[]{:S(2)}) async-start(), calls=%async_computation.12 | async-start | bytes 1310720 | tf_op jit(solution)/shard_map/all_gather | solution.py:19
  40.1 25.8 %copy-start.41 = (bf16[1,1,128,128]{2,3,1,0:T(8,128)(2,1)}, bf16[1,1,128,128]{2,3,1,0:T(8,128)(2,1)S(1)}, u32[]{:S(2)}) copy-start(bf16[1,1,128,128]{2,3,1,0:T(8,128)(2,1)S(1)} %copy.210) | copy-start | bytes 98308
  40.2 25.7 %copy-start.42 = (bf16[1,1,128,128]{2,3,1,0:T(8,128)(2,1)}, bf16[1,1,128,128]{2,3,1,0:T(8,128)(2,1)S(1)}, u32[]{:S(2)}) copy-start(bf16[1,1,128,128]{2,3,1,0:T(8,128)(2,1)S(1)} %copy.211) | copy-start | bytes 98308
  80.3 48.3 %copy-start.37 = (bf16[8,64,128]{2,1,0:T(8,128)(2,1)}, bf16[8,64,128]{2,1,0:T(8,128)(2,1)S(1)}, u32[]{:S(2)}) copy-start(bf16[8,64,128]{2,1,0:T(8,128)(2,1)S(1)} %get-tuple-element.481) | copy-start | bytes 393220
  90.7 38.4 %copy-start.65 = (f32[128]{0:T(128)S(1)}, f32[128]{0:T(128)}, u32[]{:S(2)}) copy-start(f32[128]{0:T(128)} %get-tuple-element.479) | copy-start | bytes 1540
  92.2 47.3 %copy-start.61 = (bf16[2,128,4]{1,2,0:T(4,128)(2,1)S(1)}, bf16[2,128,4]{1,2,0:T(4,128)(2,1)}, u32[]{:S(2)}) copy-start(bf16[2,128,4]{1,2,0:T(4,128)(2,1)} %param.25) | copy-start | bytes 6148
  128.5 23.1 %copy-start.52 = (bf16[1,1,128,128]{3,2,1,0:T(8,128)(2,1)S(1)}, bf16[1,1,128,128]{3,2,1,0:T(8,128)(2,1)}, u32[]{:S(2)}) copy-start(bf16[1,1,128,128]{3,2,1,0:T(8,128)(2,1)} %get-tuple-element.471) | copy-start | bytes 98308
  128.5 23.2 %copy-start.51 = (bf16[1,1,128,128]{3,2,1,0:T(8,128)(2,1)S(1)}, bf16[1,1,128,128]{3,2,1,0:T(8,128)(2,1)}, u32[]{:S(2)}) copy-start(bf16[1,1,128,128]{3,2,1,0:T(8,128)(2,1)} %get-tuple-element.474) | copy-start | bytes 98308
  128.7 23.2 %copy-start.49 = (bf16[2,128,128]{2,1,0:T(8,128)(2,1)S(1)}, bf16[2,128,128]{2,1,0:T(8,128)(2,1)}, u32[]{:S(2)}) copy-start(bf16[2,128,128]{2,1,0:T(8,128)(2,1)} %param.24) | copy-start | bytes 196612
  128.7 49.3 %copy-start.6 = (bf16[512,1,1,1,1,1,1,256]{7,0,5,4,3,2,1,6:T(8,128)(2,1)}, bf16[512,1,1,1,1,1,1,256]{7,0,5,4,3,2,1,6:T(8,128)(2,1)S(1)}, u32[]{:S(2)}) copy-start(bf16[512,1,1,1,1,1,1,256]{7,0,5,4,3,2,1,6:T(8,128)(2,1)S(1)} %copy.243) | copy-start | bytes 786436
  129.4 48.7 %copy-start.20 = (bf16[1,512,128]{2,1,0:T(8,128)(2,1)}, bf16[1,512,128]{2,1,0:T(8,128)(2,1)S(1)}, u32[]{:S(2)}) copy-start(bf16[1,512,128]{2,1,0:T(8,128)(2,1)S(1)} %fusion.136) | copy-start | bytes 393220
  136.1 8.6 all-to-all-start.4
  144.7 33.4 %copy-start.25 = (bf16[1,64,8,1,128]{4,1,3,0,2:T(8,128)(2,1)}, bf16[1,64,8,1,128]{4,1,3,0,2:T(8,128)(2,1)S(1)}, u32[]{:S(2)}) copy-start(bf16[1,64,8,1,128]{4,1,3,0,2:T(8,128)(2,1)S(1)} %all-to-all-done.4) | copy-start | bytes 393220
  145.4 29.9 %all-to-all-start.3 = ((bf16[64,4,1,512]{3,1,2,0:T(4,128)(2,1)}), bf16[64,4,1,512]{3,1,2,0:T(4,128)(2,1)S(1)}, u32[]{:S(2)}, u32[]{:S(2)}) async-start(bf16[64,4,1,512]{3,1,2,0:T(4,128)(2,1)} %broadcast_in_dim.74), calls=%async_computation.3 | async-start | bytes 524288 | tf_op jit(solution)/shard_map/all_to_all | solution.py:31
  151.7 26.3 %copy-start.44 = (bf16[1,1,128,128]{2,3,1,0:T(8,128)(2,1)}, bf16[1,1,128,128]{2,3,1,0:T(8,128)(2,1)S(1)}, u32[]{:S(2)}) copy-start(bf16[1,1,128,128]{2,3,1,0:T(8,128)(2,1)S(1)} %copy.213) | copy-start | bytes 98308
  151.9 26.4 %copy-start.46 = (bf16[1,1,128,128]{2,3,1,0:T(8,128)(2,1)}, bf16[1,1,128,128]{2,3,1,0:T(8,128)(2,1)S(1)}, u32[]{:S(2)}) copy-start(bf16[1,1,128,128]{2,3,1,0:T(8,128)(2,1)S(1)} %copy.214) | copy-start | bytes 98308
  207.3 51.8 %copy-start.45 = (bf16[1,1,128,128]{2,3,1,0:T(8,128)(2,1)S(1)}, bf16[1,1,128,128]{2,3,1,0:T(8,128)(2,1)}, u32[]{:S(2)}) copy-start(bf16[1,1,128,128]{2,3,1,0:T(8,128)(2,1)} %copy-done.44) | copy-start | bytes 98308
  270.8 56.3 %copy-start.7 = (bf16[512,1,1,1,1,1,1,256]{7,0,5,4,3,2,1,6:T(8,128)(2,1)S(1)}, bf16[512,1,1,1,1,1,1,256]{7,0,5,4,3,2,1,6:T(8,128)(2,1)}, u32[]{:S(2)}) copy-start(bf16[512,1,1,1,1,1,1,256]{7,0,5,4,3,2,1,6:T(8,128)(2,1)} %copy-done.6) | copy-start | bytes 786436
  270.8 56.3 %copy-start.56 = (f32[512]{0:T(512)S(1)}, f32[512]{0:T(512)}, u32[]{:S(2)}) copy-start(f32[512]{0:T(512)} %copy-done.55) | copy-start | bytes 6148
  270.8 56.3 %copy-start.60 = (f32[128]{0:T(128)S(1)}, f32[128]{0:T(128)}, u32[]{:S(2)}) copy-start(f32[128]{0:T(128)} %copy-done.59) | copy-start | bytes 1540
  270.9 56.3 %copy-start.62 = (bf16[2,128,4]{1,2,0:T(4,128)(2,1)S(1)}, bf16[2,128,4]{1,2,0:T(4,128)(2,1)}, u32[]{:S(2)}) copy-start(bf16[2,128,4]{1,2,0:T(4,128)(2,1)} %param.25) | copy-start | bytes 6148
  288.8 38.1 %all-to-all-start.6 = ((f32[64,4,1,512]{3,1,2,0:T(4,128)}), f32[64,4,1,512]{3,1,2,0:T(4,128)S(1)}, u32[]{:S(2)}, u32[]{:S(2)}) async-start(f32[64,4,1,512]{3,1,2,0:T(4,128)} %bitcast.128), calls=%async_computation.6 | async-start | bytes 1048576 | tf_op jit(solution)/shard_map/all_to_all | solution.py:52
  293.5 73.0 %copy-start.29 = (bf16[1,512,128]{2,1,0:T(8,128)(2,1)S(1)}, bf16[1,512,128]{2,1,0:T(8,128)(2,1)}, u32[]{:S(2)}) copy-start(bf16[1,512,128]{2,1,0:T(8,128)(2,1)} %param.18) | copy-start | bytes 393220
  327.1 43.5 %copy-start.3 = (bf16[4,8,512,32]{2,3,1,0:T(8,128)(2,1)S(1)}, bf16[4,8,512,32]{2,3,1,0:T(8,128)(2,1)}, u32[]{:S(2)}) copy-start(bf16[4,8,512,32]{2,3,1,0:T(8,128)(2,1)} %get-tuple-element.225) | copy-start | bytes 3145732
  331.6 33.9 %all-to-all-start.7 = ((bf16[512,1,1,1,1,1,1,128]{7,6,5,4,3,2,1,0:T(2,128)(2,1)}), bf16[512,1,1,1,1,1,1,128]{7,6,5,4,3,2,1,0:T(2,128)(2,1)S(1)}, u32[]{:S(2)}, u32[]{:S(2)}) async-start(bf16[512,1,1,1,1,1,1,128]{7,6,5,4,3,2,1,0:T(2,128)(2,1)} %copy.171), calls=%async_computation.7 | async-start | bytes 524288 | tf_op jit(solution)/shard_map/all_to_all | solution.py:62
  340.8 35.0 %copy-start.32 = (f32[8,64,128]{2,1,0:T(8,128)S(1)}, f32[8,64,128]{2,1,0:T(8,128)}, u32[]{:S(2)}) copy-start(f32[8,64,128]{2,1,0:T(8,128)} %copy-done.31) | copy-start | bytes 786436
  340.8 35.0 %copy-start.50 = (bf16[2,128,128]{2,1,0:T(8,128)(2,1)S(1)}, bf16[2,128,128]{2,1,0:T(8,128)(2,1)}, u32[]{:S(2)}) copy-start(bf16[2,128,128]{2,1,0:T(8,128)(2,1)} %param.24) | copy-start | bytes 196612
  367.2 8.6 all-to-all-start.8
  377.0 48.6 %copy-start.26 = (bf16[8,64,128]{2,1,0:T(8,128)(2,1)}, bf16[8,64,128]{2,1,0:T(8,128)(2,1)S(1)}, u32[]{:S(2)}) copy-start(bf16[8,64,128]{2,1,0:T(8,128)(2,1)S(1)} %get-tuple-element.450) | copy-start | bytes 393220
  434.5 18.3 %all-to-all-start.9 = ((bf16[8,1,512,128]{3,2,1,0:T(8,128)(2,1)}), bf16[8,1,512,128]{3,2,1,0:T(8,128)(2,1)S(1)}, u32[]{:S(2)}, u32[]{:S(2)}) async-start(bf16[8,1,512,128]{3,2,1,0:T(8,128)(2,1)} %convert_bitcast_fusion), calls=%async_computation.9 | async-start | bytes 2097152 | tf_op jit(solution)/shard_map/all_to_all | solution.py:46
  452.8 40.0 %all-to-all-start.10 = ((f32[64,4,1,512]{3,1,2,0:T(4,128)}), f32[64,4,1,512]{3,1,2,0:T(4,128)}, u32[]{:S(2)}, u32[]{:S(2)}) async-start(f32[64,4,1,512]{3,1,2,0:T(4,128)} %bitcast.624), calls=%async_computation.10 | async-start | bytes 1048576 | tf_op jit(solution)/shard_map/all_to_all | solution.py:52
  459.5 482.1 %all-reduce.4.cloned.1.call-start = ((), (), s32[]{:S(2)}) async-start(), calls=%async_computation.13 | async-start | bytes 1310720 | tf_op jit(solution)/shard_map/psum | solution.py:358
  468.6 25.4 %copy-start.19 = (bf16[1,512,128]{2,1,0:T(8,128)(2,1)S(1)}, bf16[1,512,128]{2,1,0:T(8,128)(2,1)}, u32[]{:S(2)}) copy-start(bf16[1,512,128]{2,1,0:T(8,128)(2,1)} %copy-done.18) | copy-start | bytes 393220
  468.6 25.6 %copy-start.54 = (f32[512]{0:T(512)S(1)}, f32[512]{0:T(512)}, u32[]{:S(2)}) copy-start(f32[512]{0:T(512)} %copy-done.53) | copy-start | bytes 6148
  468.6 25.6 %copy-start.58 = (f32[128]{0:T(128)S(1)}, f32[128]{0:T(128)}, u32[]{:S(2)}) copy-start(f32[128]{0:T(128)} %copy-done.57) | copy-start | bytes 1540
  468.6 25.5 %copy-start.63 = (bf16[2,128,4]{1,2,0:T(4,128)(2,1)S(1)}, bf16[2,128,4]{1,2,0:T(4,128)(2,1)}, u32[]{:S(2)}) copy-start(bf16[2,128,4]{1,2,0:T(4,128)(2,1)} %param.25) | copy-start | bytes 6148
  469.5 25.2 %copy-start.64 = (f32[128]{0:T(128)S(1)}, f32[128]{0:T(128)}, u32[]{:S(2)}) copy-start(f32[128]{0:T(128)} %get-tuple-element.361) | copy-start | bytes 1540
  469.6 25.2 %copy-start.67 = (f32[128]{0:T(128)S(1)}, f32[128]{0:T(128)}, u32[]{:S(2)}) copy-start(f32[128]{0:T(128)} %get-tuple-element.355) | copy-start | bytes 1540
  469.6 125.2 %copy-start.14 = (f32[512,1,1,1,1,1,1,128]{7,6,5,4,3,2,1,0:T(1,128)S(1)}, f32[512,1,1,1,1,1,1,128]{7,6,5,4,3,2,1,0:T(1,128)}, u32[]{:S(2)}) copy-start(f32[512,1,1,1,1,1,1,128]{7,6,5,4,3,2,1,0:T(1,128)} %copy-done.13) | copy-start | bytes 786436
  469.6 125.2 %copy-start.30 = (bf16[1,512,128]{2,1,0:T(8,128)(2,1)S(1)}, bf16[1,512,128]{2,1,0:T(8,128)(2,1)}, u32[]{:S(2)}) copy-start(bf16[1,512,128]{2,1,0:T(8,128)(2,1)} %param.18) | copy-start | bytes 393220
  (34 other events, 228.3 us)
Sparse Core Ops, SparseCore 0:
  17.2 35.9 all-gather.2
  135.5 18.4 all-gather.4
  470.6 471.0 all-reduce.3
where the time goes:
time: 957 us; the launch traced here: 952 us
  waiting for transfers between devices  484 us (51%)
  blocking collectives  175 us (18%)
  matrix products  101 us (11%)
  local copies, waits for them, and re-layouts  82.8 us (9%)
  starting transfers between devices  57.9 us (6%)
  other arithmetic  35.6 us (4%)
  between operations  15 us (2%)
    psum x1, waiting for transfers between devices, local(): lax.psum((combined[0], combined[1], combined[2], combined[3], combined[4]...  346 us
    psum x1, blocking collectives, local(): lax.psum((combined[0], combined[1], combined[2], combined[3], combined[4]...  100 us
    all_to_all x2, waiting for transfers between devices, summed_on_arrival(): lax.all_to_all(parts, axis, split_axis=0, concat_axis=0, tiled=True)  54.8 us
    all_to_all x2, waiting for transfers between devices, from_everyone(): lax.all_to_all(jnp.broadcast_to(x[None], (length, *x.shape)), axis, 0, 0,...  45.5 us
    all_to_all x1, blocking collectives, joined_exchange(): parts = lax.all_to_all(parts, axis, split_axis=0, concat_axis=0, tiled=True)  36.4 us
    dynamic_update_slice x16, local copies, waits for them, and re-layouts, backward_block(): lax.map(differentiate, (log_totals, head_queries, head_pairs[0], head_pai...  30.2 us
    all_to_all x2, starting transfers between devices, from_everyone(): lax.all_to_all(jnp.broadcast_to(x[None], (length, *x.shape)), axis, 0, 0,...  26.7 us
    all_to_all x1, waiting for transfers between devices, joined_exchange(): parts = lax.all_to_all(parts, axis, split_axis=0, concat_axis=0, tiled=True)  24.7 us
  transfers between devices with their start and end apart: 11, of which 9 were waited for; matrix products, arithmetic and copies ran while one was open for 3% of the time, Pallas kernels for 0%

commit v1 on v0

v1 whole, which is shorter than its diff:
```python
import math

import jax
import jax.numpy as jnp
from jax import lax
from jax.sharding import Mesh
from jax.sharding import PartitionSpec as P

HEAD = ("head_0", "head_1")
ROW_HEAD = ("row", "head_0", "head_1")


EPS = 1e-05
MASKED = 1000000000.0
LANES = 128


def exchanged(parts, axis):
    return lax.all_to_all(parts, axis, split_axis=0, concat_axis=0, tiled=True)


def to_all(x, axis):
    return jnp.broadcast_to(x[None], (lax.axis_size(axis), *x.shape))


def layer_norm(values, norm_scale, norm_offset):
    floats = values.astype(jnp.float32)
    centred = floats - jnp.mean(floats, axis=-1, keepdims=True)
    inverse = lax.rsqrt(jnp.mean(centred * centred, axis=-1, keepdims=True) + EPS)
    normed = centred * inverse
    return (normed, inverse, (normed * norm_scale + norm_offset).astype(jnp.bfloat16))


def norm_backward(grad_normal, normed, inverse, norm_scale):
    grad_hat = grad_normal * norm_scale
    first_mean = jnp.mean(grad_hat, axis=-1, keepdims=True)
    second_mean = jnp.mean(grad_hat * normed, axis=-1, keepdims=True)
    return inverse * (grad_hat - first_mean - normed * second_mean)


def forward_block(normal_rows, normal_query, bias_query, key_bias, params):
    _, _, projection, gate_offset, out_proj, bias_proj = params
    head_total = bias_proj.shape[1]
    inner_width = projection.shape[2]
    head_size = inner_width // head_total
    query_scale = 1.0 / math.sqrt(head_size)
    block_rows, query_count, _ = normal_query.shape
    key_count = normal_rows.shape[1]
    queries = (
        jnp.dot(normal_query, projection[0], preferred_element_type=jnp.float32) * query_scale
    ).astype(jnp.bfloat16)
    joined_weights = jnp.concatenate([projection[1], projection[2]], axis=1)
    key_value = jnp.dot(normal_rows, joined_weights, preferred_element_type=jnp.float32).astype(
        jnp.bfloat16
    )
    gate_values = jax.nn.sigmoid(
        jnp.dot(normal_query, projection[3], preferred_element_type=jnp.float32) + gate_offset
    )
    head_queries = queries.reshape(block_rows, query_count, head_total, head_size).transpose(
        2, 0, 1, 3
    )
    head_pairs = key_value.reshape(block_rows, key_count, 2, head_total, head_size).transpose(
        2, 3, 0, 1, 4
    )

    def attend(inputs):
        query_head, key_head, value_head, bias_head = inputs
        logits = jnp.einsum(
            "rqd,rnd->rqn", query_head, key_head, preferred_element_type=jnp.float32
        )
        logits = logits + bias_head.astype(jnp.float32)[None] + key_bias
        largest = jnp.max(logits, axis=-1, keepdims=True)
        weights = jnp.exp(logits - largest)
        total = jnp.sum(weights, axis=-1, keepdims=True)
        soft_weights = weights / total
        attended = jnp.einsum(
            "rqn,rnd->rqd",
            soft_weights.astype(jnp.bfloat16),
            value_head,
            preferred_element_type=jnp.float32,
        )
        return ((largest + jnp.log(total))[..., 0], attended)

    log_totals, attended = lax.map(attend, (head_queries, head_pairs[0], head_pairs[1], bias_query))
    attended = attended.transpose(1, 2, 0, 3).reshape(block_rows, query_count, inner_width)
    gated_out = (gate_values * attended).astype(jnp.bfloat16)
    update = jnp.dot(gated_out, out_proj, preferred_element_type=jnp.float32).astype(jnp.bfloat16)
    saved = (head_queries, head_pairs, gate_values, attended, gated_out, log_totals)
    return (saved, update)


def backward_block(saved, normal_rows, normal_query, bias_query, grad_query, key_bias, params):
    _, _, projection, gate_offset, out_proj, bias_proj = params
    head_queries, head_pairs, gate_values, attended, gated_out, log_totals = saved
    channels = normal_rows.shape[2]
    head_total, block_rows, query_count, head_size = head_queries.shape
    key_count = normal_rows.shape[1]
    inner_width = head_total * head_size
    query_scale = 1.0 / math.sqrt(head_size)
    grad_gated = jnp.dot(grad_query, out_proj.T, preferred_element_type=jnp.float32)
    grad_att = (grad_gated * gate_values).astype(jnp.bfloat16)
    grad_pre = (grad_gated * attended * gate_values * (1.0 - gate_values)).astype(jnp.bfloat16)
    head_grads = grad_att.reshape(block_rows, query_count, head_total, head_size).transpose(
        2, 0, 1, 3
    )

    def differentiate(inputs):
        total_head, query_head, key_head, value_head, bias_head, grad_head = inputs
        logits = jnp.einsum(
            "rqd,rnd->rqn", query_head, key_head, preferred_element_type=jnp.float32
        )
        logits = logits + bias_head.astype(jnp.float32)[None] + key_bias
        soft_weights = jnp.exp(logits - total_head[..., None])
        grad_weights = jnp.einsum(
            "rqd,rnd->rqn", grad_head, value_head, preferred_element_type=jnp.float32
        )
        grad_logits = soft_weights * (
            grad_weights - jnp.sum(soft_weights * grad_weights, axis=-1, keepdims=True)
        )
        logits_half = grad_logits.astype(jnp.bfloat16)
        grad_queries = (
            jnp.einsum("rqn,rnd->rqd", logits_half, key_head, preferred_element_type=jnp.float32)
            * query_scale
        ).astype(jnp.bfloat16)
        grad_keys = jnp.einsum(
            "rqn,rqd->rnd", logits_half, query_head, preferred_element_type=jnp.float32
        ).astype(jnp.bfloat16)
        grad_values = jnp.einsum(
            "rqn,rqd->rnd",
            soft_weights.astype(jnp.bfloat16),
            grad_head,
            preferred_element_type=jnp.float32,
        ).astype(jnp.bfloat16)
        return (grad_queries, grad_keys, grad_values, jnp.sum(grad_logits, axis=0))

    grad_queries, grad_keys, grad_values, grad_bias = lax.map(
        differentiate,
        (log_totals, head_queries, head_pairs[0], head_pairs[1], bias_query, head_grads),
    )
    grad_queries = grad_queries.transpose(1, 2, 0, 3).reshape(block_rows, query_count, inner_width)
    key_weights = projection[1].reshape(channels, head_total, head_size).transpose(1, 2, 0)
    value_weights = projection[2].reshape(channels, head_total, head_size).transpose(1, 2, 0)
    query_side = jnp.dot(grad_queries, projection[0].T, preferred_element_type=jnp.float32)
    query_side = query_side + jnp.dot(grad_pre, projection[3].T, preferred_element_type=jnp.float32)
    term = jnp.einsum("hrnd,hdc->rnc", grad_keys, key_weights, preferred_element_type=jnp.float32)
    term = term + jnp.einsum(
        "hrnd,hdc->rnc", grad_values, value_weights, preferred_element_type=jnp.float32
    )
    shaped = term.reshape(block_rows, -1, query_count, channels)
    classes = lax.broadcasted_iota(jnp.int32, (1, shaped.shape[1], 1, 1), 1)
    own_class = classes == lax.axis_index(HEAD)
    partial = (shaped + jnp.where(own_class, query_side[:, None], 0.0)).astype(jnp.bfloat16)
    weight_sums = (
        jnp.einsum("rqc,rqe->ce", normal_query, grad_queries, preferred_element_type=jnp.float32),
        jnp.einsum(
            "rnc,hrnd->chd", normal_rows, grad_keys, preferred_element_type=jnp.float32
        ).reshape(channels, inner_width),
        jnp.einsum(
            "rnc,hrnd->chd", normal_rows, grad_values, preferred_element_type=jnp.float32
        ).reshape(channels, inner_width),
        jnp.einsum("rqc,rqe->ce", normal_query, grad_pre, preferred_element_type=jnp.float32),
        jnp.einsum("rqe,rqc->ec", gated_out, grad_query, preferred_element_type=jnp.float32),
        jnp.sum(grad_pre.astype(jnp.float32), axis=(0, 1))[None],
    )
    return (partial, grad_bias, jnp.concatenate(weight_sums, axis=0))


def padded_rows(x, rows):
    return jnp.pad(x, ((0, 0),) * (x.ndim - 2) + ((0, rows - x.shape[-2]), (0, 0)))


def rounded_up(value, step):
    return -(-value // step) * step


def local(
    pair_input,
    cotangent,
    residue_mask,
    norm_gain,
    norm_shift,
    proj_weights,
    gate_bias,
    out_weights,
    bias_weights,
):
    channels = pair_input.shape[2]
    groups = lax.axis_size("row")
    classes = lax.axis_size(HEAD)
    positions = groups * classes
    head_total = bias_weights.shape[2]
    bias_rows = head_total * positions // LANES
    half = jnp.bfloat16
    key_bias = (residue_mask.astype(jnp.float32) - 1.0) * MASKED
    key_bias = key_bias.reshape(groups, classes).T.reshape(positions)
    params = [
        (
            norm_gain[which],
            norm_shift[which],
            proj_weights[which],
            gate_bias[which],
            out_weights[which],
            bias_weights[which],
        )
        for which in range(2)
    ]

    own_pair = pair_input.reshape(groups, classes, channels).transpose(1, 0, 2)
    normed_own, inverse_own, normal_own = layer_norm(own_pair, norm_gain[0], norm_shift[0])
    normal_flat = normal_own.reshape(positions, channels)
    bias_own = jnp.einsum(
        "nc,ch->hn", normal_flat, bias_weights[0], preferred_element_type=jnp.float32
    ).astype(half)
    own_cotangent = cotangent.reshape(groups, classes, channels)
    arrived = exchanged(
        jnp.concatenate(
            [to_all(normal_flat, HEAD), own_pair, own_cotangent.transpose(1, 0, 2)], axis=1
        ),
        HEAD,
    )
    first_rows = arrived[:, :positions]
    pair_query = arrived[:, positions : positions + groups]
    cotangent_query = arrived[:, positions + groups :]
    first_query = lax.dynamic_index_in_dim(
        first_rows.reshape(classes, classes, groups, channels),
        lax.axis_index(HEAD),
        axis=1,
        keepdims=False,
    )
    arrived = exchanged(
        jnp.concatenate(
            [
                to_all(bias_own.reshape(bias_rows, LANES), "row"),
                own_cotangent,
            ],
            axis=1,
        ),
        "row",
    )
    first_bias = (
        arrived[:, :bias_rows].reshape(groups, head_total, positions).transpose(1, 0, 2)
    )
    second_grad_query = arrived[:, bias_rows:].transpose(1, 0, 2)
    first_saved, update = forward_block(first_rows, first_query, first_bias, key_bias, params[0])

    after_query = (pair_query.astype(jnp.float32) + update.astype(jnp.float32)).astype(half)
    after_normed, after_inverse, after_normal = layer_norm(
        after_query, norm_gain[1], norm_shift[1]
    )
    second_bias_own = jnp.einsum(
        "abc,ch->ahb", after_normal, bias_weights[1], preferred_element_type=jnp.float32
    ).astype(half)
    after_own = exchanged(after_query, HEAD)
    arrived = exchanged(
        jnp.concatenate(
            [
                to_all(second_bias_own.reshape(bias_rows, LANES), "row"),
                after_own.transpose(1, 0, 2),
            ],
            axis=1,
        ),
        "row",
    )
    second_bias = (
        arrived[:, :bias_rows]
        .reshape(groups, classes, head_total * groups)
        .transpose(2, 1, 0)
        .reshape(head_total, groups, positions)
    )
    flipped_query = arrived[:, bias_rows:].transpose(1, 0, 2)
    _, _, second_query = layer_norm(flipped_query, norm_gain[1], norm_shift[1])
    second_rows = (
        exchanged(to_all(second_query, HEAD), HEAD)
        .transpose(1, 0, 2, 3)
        .reshape(classes, positions, channels)
    )
    second_saved, _ = forward_block(second_rows, second_query, second_bias, key_bias, params[1])
    partial, grad_bias, second_sums = backward_block(
        second_saved, second_rows, second_query, second_bias, second_grad_query, key_bias, params[1]
    )

    share_rows = rounded_up(-(-second_sums.shape[0] // classes), 8)
    group_rows = rounded_up(share_rows, groups) // groups

    def shares_of(sums):
        return padded_rows(sums, classes * share_rows).astype(half).reshape(
            classes, share_rows, LANES
        )

    def group_shares_of(arrived_shares):
        summed = jnp.sum(arrived_shares.astype(jnp.float32), axis=0)
        summed = padded_rows(summed, groups * group_rows).astype(half)
        return padded_rows(summed.reshape(groups, group_rows, LANES), rounded_up(group_rows, 8))

    arrived = exchanged(
        jnp.concatenate(
            [
                partial.transpose(1, 0, 2, 3).reshape(classes, positions, channels),
                shares_of(second_sums),
            ],
            axis=1,
        ),
        HEAD,
    )
    grad_flipped = jnp.sum(arrived[:, :positions].astype(jnp.float32), axis=0).astype(half)
    bias_parts = (
        grad_bias.astype(half)
        .reshape(head_total * groups * classes, groups)
        .T.reshape(groups, bias_rows, LANES)
    )
    arrived = exchanged(
        jnp.concatenate(
            [
                bias_parts,
                grad_flipped.reshape(classes, groups, channels).transpose(1, 0, 2),
                group_shares_of(arrived[:, positions:]),
            ],
            axis=1,
        ),
        "row",
    )
    summed = jnp.sum(arrived[:, :bias_rows].astype(jnp.float32), axis=0)
    second_bias_half = summed.reshape(head_total, groups, classes).astype(half)
    second_own = jnp.sum(
        arrived[:, bias_rows + classes : bias_rows + classes + group_rows].astype(jnp.float32),
        axis=0,
    )
    grad_query = exchanged(arrived[:, bias_rows : bias_rows + classes].transpose(1, 0, 2), HEAD)
    grad_normal = grad_query.astype(jnp.float32) + jnp.einsum(
        "hba,ch->abc", second_bias_half, bias_weights[1], preferred_element_type=jnp.float32
    )
    end_query = norm_backward(grad_normal, after_normed, after_inverse, norm_gain[1]).astype(half)
    second_small = jnp.concatenate(
        [
            jnp.einsum(
                "abc,hba->hc", after_normal, second_bias_half, preferred_element_type=jnp.float32
            ),
            jnp.sum(grad_normal * after_normed, axis=(0, 1))[None],
            jnp.sum(grad_normal, axis=(0, 1))[None],
        ],
        axis=0,
    )

    after_grad_query = (
        cotangent_query.astype(jnp.float32) + end_query.astype(jnp.float32)
    ).astype(half)
    partial, grad_bias, first_sums = backward_block(
        first_saved, first_rows, first_query, first_bias, after_grad_query, key_bias, params[0]
    )
    arrived = exchanged(
        jnp.concatenate(
            [
                partial.reshape(classes, positions, channels),
                end_query,
                shares_of(jnp.concatenate([first_sums, second_small], axis=0)),
            ],
            axis=1,
        ),
        HEAD,
    )
    grad_normal = jnp.sum(arrived[:, :positions].astype(jnp.float32), axis=0)
    end_own = arrived[:, positions : positions + groups]
    shares = arrived[:, positions + groups :]
    arrived = exchanged(
        jnp.concatenate(
            [
                grad_bias.astype(half)
                .transpose(1, 0, 2)
                .reshape(groups, bias_rows, LANES),
                group_shares_of(shares),
            ],
            axis=1,
        ),
        "row",
    )
    summed = jnp.sum(arrived[:, :bias_rows].astype(jnp.float32), axis=0)
    bias_half = summed.reshape(head_total, positions).astype(half)
    first_own = jnp.sum(
        arrived[:, bias_rows : bias_rows + group_rows].astype(jnp.float32), axis=0
    )
    grad_normal = grad_normal + jnp.einsum(
        "hn,ch->nc", bias_half, bias_weights[0], preferred_element_type=jnp.float32
    )
    normed_flat = normed_own.reshape(positions, channels)
    start_grad = norm_backward(
        grad_normal, normed_flat, inverse_own.reshape(positions, 1), norm_gain[0]
    )
    moved_grad = (end_own.astype(jnp.float32) + start_grad.reshape(end_own.shape)).transpose(1, 0, 2)
    pair_grad = cotangent.astype(jnp.float32) + moved_grad.reshape(1, positions, channels)
    first_small = jnp.concatenate(
        [
            jnp.einsum("nc,hn->hc", normal_flat, bias_half, preferred_element_type=jnp.float32),
            jnp.sum(grad_normal * normed_flat, axis=0)[None],
            jnp.sum(grad_normal, axis=0)[None],
        ],
        axis=0,
    )

    small_rows = first_small.shape[0]
    tail = jnp.concatenate([first_own, second_own, first_small], axis=0).astype(half)
    tail = padded_rows(tail, rounded_up(tail.shape[0], 8))
    arrived = exchanged(to_all(tail, "row"), "row").astype(jnp.float32)
    whole_rows = groups * group_rows
    shared = jnp.concatenate(
        [
            arrived[:, :group_rows].reshape(whole_rows, LANES)[:share_rows],
            arrived[:, group_rows : 2 * group_rows].reshape(whole_rows, LANES)[:share_rows],
            padded_rows(
                jnp.sum(arrived[:, 2 * group_rows : 2 * group_rows + small_rows], axis=0),
                rounded_up(small_rows, 8),
            ),
        ],
        axis=0,
    )
    arrived = exchanged(to_all(shared, HEAD), HEAD)
    first_whole = arrived[:, :share_rows].reshape(-1, LANES)
    second_whole = arrived[:, share_rows : 2 * share_rows].reshape(-1, LANES)
    first_small = jnp.sum(arrived[:, 2 * share_rows : 2 * share_rows + small_rows], axis=0)
    main_rows = first_sums.shape[0]
    second_small = first_whole[main_rows : main_rows + small_rows]
    proj_rows = 4 * channels

    def both(first, second):
        return jnp.stack([first, second])

    return (
        pair_grad,
        both(first_whole[:proj_rows], second_whole[:proj_rows]).reshape(
            2, 4, channels, -1
        ),
        both(first_whole[main_rows - 1], second_whole[main_rows - 1]),
        both(first_whole[proj_rows : main_rows - 1], second_whole[proj_rows : main_rows - 1]),
        both(first_small[:head_total].T, second_small[:head_total].T),
        both(first_small[head_total], second_small[head_total]),
        both(first_small[head_total + 1], second_small[head_total + 1]),
    )


def solution(mesh):
    finer = Mesh(mesh.devices.reshape(mesh.shape["row"], 4, 2), ("row", "head_0", "head_1"))
    in_specs = (P(ROW_HEAD, None, None), P(ROW_HEAD, None, None), P(), P(), P(), P(), P(), P(), P())
    out_specs = (P(ROW_HEAD, None, None), P(), P(), P(), P(), P(), P())
    return jax.shard_map(local, mesh=finer, in_specs=in_specs, out_specs=out_specs, check_vma=False)
```

time: 957 us -> 505 us (0.53)
  waiting for transfers between devices: 484 us -> 180 us
  blocking collectives: 175 us -> 34.2 us
  between operations: 15 us -> 1.79 us
  local copies, waits for them, and re-layouts: 82.8 us -> 71 us
  starting transfers between devices: 57.9 us -> 67.7 us
    psum x1 -> x0, waiting for transfers between devices: 346 us -> none  [local(): lax.psum((combined[0], combined[1], combined[2], combined[3], combined[4]...]
    psum x1 -> x0, blocking collectives: 100 us -> none  [local(): lax.psum((combined[0], combined[1], combined[2], combined[3], combined[4]...]
    all_to_all x8 -> x11, waiting for transfers between devices: 138 us -> 180 us  [exchanged(): return lax.all_to_all(parts, axis, split_axis=0, concat_axis=0, tiled=True)]
    all_to_all x3 -> x1, blocking collectives: 63.5 us -> 34.2 us  [exchanged(): return lax.all_to_all(parts, axis, split_axis=0, concat_axis=0, tiled=True)]
    dynamic_update_slice x16 -> x8, local copies, waits for them, and re-layouts: 30.2 us -> 5.05 us  [backward_block(): lax.map(differentiate, (log_totals, head_queries, head_pairs[0], head_pai...]
    dynamic_update_slice x2 -> x0, local copies, waits for them, and re-layouts: 12.2 us -> none  [backward_block(): lax.dynamic_update_slice_in_dim(shaped, current + query_slice, head_index...]
    all_gather x2 -> x0, blocking collectives: 11.2 us -> none  [whole_of(): x = lax.all_gather(x, axis, axis=dim, tiled=True)]
    all_to_all x8 -> x11, starting transfers between devices: 57.8 us -> 67.7 us  [exchanged(): return lax.all_to_all(parts, axis, split_axis=0, concat_axis=0, tiled=True)]
  transfers between devices with their start and end apart: 11 -> 11, of which waited for: 9 -> 10; matrix products, arithmetic and copies ran while one was open for 3% -> 7% of each run, Pallas kernels for 0% -> 0%
where the time goes in v1:
time: 505 us; the launch traced here: 501 us
  waiting for transfers between devices  180 us (36%)
  matrix products  105 us (21%)
  local copies, waits for them, and re-layouts  71 us (14%)
  starting transfers between devices  67.7 us (13%)
  other arithmetic  41.2 us (8%)
  blocking collectives  34.2 us (7%)
    all_to_all x11, waiting for transfers between devices, exchanged(): return lax.all_to_all(parts, axis, split_axis=0, concat_axis=0, tiled=True)  180 us
    all_to_all x11, starting transfers between devices, exchanged(): return lax.all_to_all(parts, axis, split_axis=0, concat_axis=0, tiled=True)  67.7 us
    all_to_all x1, blocking collectives, exchanged(): return lax.all_to_all(parts, axis, split_axis=0, concat_axis=0, tiled=True)  34.2 us
    dot_general x8, matrix products, attend(): jnp.einsum('rqn,rnd->rqd', soft_weights.astype(jnp.bfloat16), value_head,...  13.5 us
    dot_general x8, matrix products, differentiate(): jnp.einsum('rqn,rqd->rnd', soft_weights.astype(jnp.bfloat16), grad_head,...  10.8 us
    dot_general x8, matrix products, differentiate(): jnp.einsum('rqn,rqd->rnd', logits_half, query_head, preferred_element_typ...  10.8 us
    dot_general x8, matrix products, differentiate(): jnp.einsum('rqd,rnd->rqn', grad_head, value_head, preferred_element_type=...  10.5 us
  transfers between devices with their start and end apart: 11, of which 10 were waited for; matrix products, arithmetic and copies ran while one was open for 7% of the time, Pallas kernels for 0%

profile of v1, /device:TPU:1, one launch (start us, length us, event | category | flops | bytes accessed | tf_op | source)
XLA Modules:
  0.0 500.7 jit_solution(13994483433468659424)
XLA Ops:
  6.0 1.8 add_convert_fusion.1
  9.2 6.0 %all-to-all-start = ((bf16[8,640,128]{2,1,0:T(8,128)(2,1)}), bf16[8,640,128]{2,1,0:T(8,128)(2,1)S(1)}, u32[]{:S(2)}, u32[]{:S(2)}) async-start(bf16[8,640,128]{2,1,0:T(8,128)(2,1)} %pad_maximum_fusion.1), calls=%async_computation | async-start | bytes 2621440 | tf_op jit(solution)/shard_map/all_to_all | solution.py:19
  16.2 13.9 %all-to-all-done = bf16[8,640,128]{2,1,0:T(8,128)(2,1)S(1)} async-done(((bf16[8,640,128]{2,1,0:T(8,128)(2,1)}), bf16[8,640,128]{2,1,0:T(8,128)(2,1)S(1)}, u32[]{:S(2)}, u32[]{:S(2)}) %all-to-all-start) | async-done | bytes 1310752 | tf_op jit(solution)/shard_map/all_to_all | solution.py:19
  30.1 24.0 %all-to-all-start.1 = ((bf16[64,24,128]{2,1,0:T(8,128)(2,1)}), bf16[64,24,128]{2,1,0:T(8,128)(2,1)S(1)}, u32[]{:S(2)}, u32[]{:S(2)}) async-start(bf16[64,24,128]{2,1,0:T(8,128)(2,1)} %pad_maximum_fusion.4), calls=%async_computation.1 | async-start | bytes 786432 | tf_op jit(solution)/shard_map/all_to_all | solution.py:19
  59.5 23.4 %all-to-all-done.1 = bf16[64,24,128]{2,1,0:T(8,128)(2,1)S(1)} async-done(((bf16[64,24,128]{2,1,0:T(8,128)(2,1)}), bf16[64,24,128]{2,1,0:T(8,128)(2,1)S(1)}, u32[]{:S(2)}, u32[]{:S(2)}) %all-to-all-start.1) | async-done | bytes 393248 | tf_op jit(solution)/shard_map/all_to_all | solution.py:19
  84.4 11.2 %while.60 = (s32[]{:T(128)}, f32[4,8,64]{2,1,0:T(8,128)}, f32[4,8,64,32]{2,3,1,0:T(8,128)S(1)}, bf16[4,8,64,32]{2,3,1,0:T(8,128)(2,1)S(1)}, bf16[4,8,512,32]{2,3...) while((s32[]{:T(128)}, f32[4,8,64]{2,1,0:T(8,128)}, ...), condition=%wide.wide.region_5.6_spmd, body=%wide.wide.region_2.5_spmd.sunk | while | flops 35683840 | bytes 4221545 | solution.py:84
  97.6 1.9 multiply_convert_fusion.5
  100.4 3.4 all-to-all-start.2
  106.9 2.2 all-to-all-done.2
  109.3 34.2 %all_to_all.60 = bf16[64,24,128]{2,1,0:T(8,128)(2,1)S(1)} all-to-all(bf16[64,24,128]{2,1,0:T(8,128)(2,1)S(1)} %pad_maximum_fusion.5), channel_id=1, replica_groups=mesh['row'=64,'head_0'=4,'head_1'=2] {'row'}, dimensions={0} | all-to-all | bytes 786432 | tf_op jit(solution)/shard_map/all_to_all | solution.py:19
  145.7 3.7 all-to-all-start.4
  159.3 2.2 copy.177
  161.5 2.1 reshape.323
  170.3 1.8 multiply_convert_fusion.4
  177.7 18.1 %while.61 = (s32[]{:T(128)}, f32[4,8,64]{2,1,0:T(8,128)S(1)}, f32[4,8,64,32]{2,3,1,0:T(8,128)}, bf16[4,8,64,32]{2,3,1,0:T(8,128)(2,1)}, bf16[4,8,512,32]{2,3,1,0...) while((s32[]{:T(128)}, f32[4,8,64]{2,1,0:T(8,128)S(1)}, ...), condition=%wide.wide.region_13.14_spmd, body=%wide.wide.region_10.13_spmd.sunk | while | flops 35683840 | bytes 4221037 | solution.py:84
  180.2 2.0 fusion.338
  184.8 2.0 fusion.338
  189.3 2.0 fusion.338
  193.8 2.0 fusion.338
  199.6 35.7 %while.62 = (s32[]{:T(128)}, bf16[4,8,64,32]{2,3,1,0:T(8,128)(2,1)}, bf16[4,8,512,32]{2,3,1,0:T(8,128)(2,1)}, bf16[4,8,512,32]{2,3,1,0:T(8,128)(2,1)}, bf16[4,64...) while((s32[]{:T(128)}, ...), condition=%wide.wide.region_17.18_spmd, body=%wide.wide.region_14.17_spmd.sunk | while | flops 86801920 | bytes 10047117 | solution.py:136
  205.2 1.8 fusion.351
  214.2 1.8 fusion.351
  221.3 1.8 fusion.350
  223.1 1.8 fusion.351
  230.3 1.8 fusion.350
  239.0 1.9 copy.188
  240.9 1.9 copy.189
  250.9 4.9 all-to-all-start.5
  256.4 19.4 %all-to-all-done.5 = bf16[8,600,128]{2,1,0:T(8,128)(2,1)} async-done(((bf16[8,600,128]{2,1,0:T(8,128)(2,1)}), bf16[8,600,128]{2,1,0:T(8,128)(2,1)}, u32[]{:S(2)}, u32[]{:S(2)}) %all-to-all-start.5) | async-done | bytes 1228832 | tf_op jit(solution)/shard_map/all_to_all | solution.py:19
  279.1 4.6 all-to-all-start.6
  284.4 32.7 %all-to-all-done.6 = bf16[64,32,128]{2,1,0:T(8,128)(2,1)S(1)} async-done(((bf16[64,32,128]{2,1,0:T(8,128)(2,1)}), bf16[64,32,128]{2,1,0:T(8,128)(2,1)S(1)}, u32[]{:S(2)}, u32[]{:S(2)}) %all-to-all-start.6) | async-done | bytes 524320 | tf_op jit(solution)/shard_map/all_to_all | solution.py:19
  317.8 3.6 all-to-all-start.7
  321.7 1.8 fusion.122
  323.6 3.1 all-to-all-done.7
  326.7 1.9 fusion.145
  335.5 28.0 %while.63 = (s32[]{:T(128)}, bf16[4,8,64,32]{2,3,1,0:T(8,128)(2,1)}, bf16[4,8,512,32]{2,3,1,0:T(8,128)(2,1)}, bf16[4,8,512,32]{2,3,1,0:T(8,128)(2,1)}, bf16[4,64...) while((s32[]{:T(128)}, ...), condition=%wide.wide.region_27.28_spmd, body=%wide.wide.region_24.27_spmd.sunk | while | flops 86801920 | bytes 10047117 | solution.py:136
  365.5 1.8 fusion.106
  374.7 2.3 fusion.115
  380.2 4.5 concatenate.51
  384.7 2.0 fusion.89
  387.9 3.6 all-to-all-start.8
  391.9 21.4 %all-to-all-done.8 = bf16[8,664,128]{2,1,0:T(8,128)(2,1)S(1)} async-done(((bf16[8,664,128]{2,1,0:T(8,128)(2,1)}), bf16[8,664,128]{2,1,0:T(8,128)(2,1)S(1)}, u32[]{:S(2)}, u32[]{:S(2)}) %all-to-all-start.8) | async-done | bytes 1359904 | tf_op jit(solution)/shard_map/all_to_all | solution.py:19
  414.1 5.8 %all-to-all-start.9 = ((bf16[64,24,128]{2,1,0:T(8,128)(2,1)}), bf16[64,24,128]{2,1,0:T(8,128)(2,1)S(1)}, u32[]{:S(2)}, u32[]{:S(2)}) async-start(bf16[64,24,128]{2,1,0:T(8,128)(2,1)} %fusion.130), calls=%async_computation.9 | async-start | bytes 786432 | tf_op jit(solution)/shard_map/all_to_all | solution.py:19
  421.1 27.7 %all-to-all-done.9 = bf16[64,24,128]{2,1,0:T(8,128)(2,1)S(1)} async-done(((bf16[64,24,128]{2,1,0:T(8,128)(2,1)}), bf16[64,24,128]{2,1,0:T(8,128)(2,1)S(1)}, u32[]{:S(2)}, u32[]{:S(2)}) %all-to-all-start.9) | async-done | bytes 393248 | tf_op jit(solution)/shard_map/all_to_all | solution.py:19
  450.3 4.6 all-to-all-start.10
  455.0 23.7 %all-to-all-done.10 = bf16[64,16,128]{2,1,0:T(8,128)(2,1)S(1)} async-done(((bf16[64,16,128]{2,1,0:T(8,128)(2,1)}), bf16[64,16,128]{2,1,0:T(8,128)(2,1)S(1)}, u32[]{:S(2)}, u32[]{:S(2)}) %all-to-all-start.10) | async-done | bytes 262176 | tf_op jit(solution)/shard_map/all_to_all | solution.py:19
  479.8 3.5 all-to-all-start.11
  484.5 12.2 %all-to-all-done.11 = f32[8,184,128]{2,1,0:T(8,128)S(1)} async-done(((f32[8,184,128]{2,1,0:T(8,128)}), f32[8,184,128]{2,1,0:T(8,128)S(1)}, u32[]{:S(2)}, u32[]{:S(2)}) %all-to-all-start.11) | async-done | bytes 753696 | tf_op jit(solution)/shard_map/all_to_all | solution.py:19
  (398 shorter events, 172.1 us)
Async XLA Ops:
  3.8 4.0 copy-start.43
  6.0 138.3 %copy-start.50 = (f32[128]{0:T(128)}, f32[128]{0:T(128)S(1)}, u32[]{:S(2)}) copy-start(f32[128]{0:T(128)S(1)} %get-tuple-element.495) | copy-start | bytes 1540
  7.8 7.3 %copy-start.12 = (bf16[8,64,128]{2,1,0:T(8,128)(2,1)}, bf16[8,64,128]{2,1,0:T(8,128)(2,1)S(1)}, u32[]{:S(2)}) copy-start(bf16[8,64,128]{2,1,0:T(8,128)(2,1)S(1)} %get-tuple-element.474) | copy-start | bytes 393220
  8.0 7.2 %copy-start.51 = (bf16[2,128,4]{1,2,0:T(4,128)(2,1)S(1)}, bf16[2,128,4]{1,2,0:T(4,128)(2,1)}, u32[]{:S(2)}) copy-start(bf16[2,128,4]{1,2,0:T(4,128)(2,1)} %param.25) | copy-start | bytes 6148
  9.2 6.2 %copy-start.18 = (bf16[1,512,128]{2,1,0:T(8,128)(2,1)S(1)}, bf16[1,512,128]{2,1,0:T(8,128)(2,1)}, u32[]{:S(2)}) copy-start(bf16[1,512,128]{2,1,0:T(8,128)(2,1)} %param.18) | copy-start | bytes 393220
  9.2 44.9 %copy-start.28 = (bf16[2,4,128,128]{3,2,1,0:T(8,128)(2,1)S(1)}, bf16[2,4,128,128]{3,2,1,0:T(8,128)(2,1)}, u32[]{:S(2)}) copy-start(bf16[2,4,128,128]{3,2,1,0:T(8,128)(2,1)} %param.22) | copy-start | bytes 786436
  9.2 45.8 %copy-start.54 = (s32[512]{0:T(512)S(1)}, s32[512]{0:T(512)}, u32[]{:S(2)}) copy-start(s32[512]{0:T(512)} %param.19) | copy-start | bytes 6148
  9.2 46.1 %copy-start.56 = (f32[2,128]{1,0:T(2,128)S(1)}, f32[2,128]{1,0:T(2,128)}, u32[]{:S(2)}) copy-start(f32[2,128]{1,0:T(2,128)} %param.23) | copy-start | bytes 3076
  9.2 20.9 %all-to-all-start = ((bf16[8,640,128]{2,1,0:T(8,128)(2,1)}), bf16[8,640,128]{2,1,0:T(8,128)(2,1)S(1)}, u32[]{:S(2)}, u32[]{:S(2)}) async-start(bf16[8,640,128]{2,1,0:T(8,128)(2,1)} %pad_maximum_fusion.1), calls=%async_computation | async-start | bytes 2621440 | tf_op jit(solution)/shard_map/all_to_all | solution.py:19
  30.1 52.8 %all-to-all-start.1 = ((bf16[64,24,128]{2,1,0:T(8,128)(2,1)}), bf16[64,24,128]{2,1,0:T(8,128)(2,1)S(1)}, u32[]{:S(2)}, u32[]{:S(2)}) async-start(bf16[64,24,128]{2,1,0:T(8,128)(2,1)} %pad_maximum_fusion.4), calls=%async_computation.1 | async-start | bytes 786432 | tf_op jit(solution)/shard_map/all_to_all | solution.py:19
  84.4 13.2 %copy-start.61 = (f32[128]{0:T(128)S(1)}, f32[128]{0:T(128)}, u32[]{:S(2)}) copy-start(f32[128]{0:T(128)} %get-tuple-element.479) | copy-start | bytes 1540
  95.6 11.3 %copy-start.2 = (bf16[4,8,64,32]{2,3,1,0:T(8,128)(2,1)}, bf16[4,8,64,32]{2,3,1,0:T(8,128)(2,1)S(1)}, u32[]{:S(2)}) copy-start(bf16[4,8,64,32]{2,3,1,0:T(8,128)(2,1)S(1)} %get-tuple-element.1107) | copy-start | bytes 393220
  95.6 11.3 %copy-start.7 = (bf16[4,64,512]{2,1,0:T(8,128)(2,1)}, bf16[4,64,512]{2,1,0:T(8,128)(2,1)S(1)}, u32[]{:S(2)}) copy-start(bf16[4,64,512]{2,1,0:T(8,128)(2,1)S(1)} %get-tuple-element.1118) | copy-start | bytes 786436
  95.6 4.0 copy-start.36
  95.6 10.0 %copy-start.53 = (f32[128]{0:T(128)S(1)}, f32[128]{0:T(128)}, u32[]{:S(2)}) copy-start(f32[128]{0:T(128)} %get-tuple-element.482) | copy-start | bytes 1540
  97.6 45.9 %copy-start.21 = (f32[8,64,128]{2,1,0:T(8,128)}, f32[8,64,128]{2,1,0:T(8,128)S(1)}, u32[]{:S(2)}) copy-start(f32[8,64,128]{2,1,0:T(8,128)S(1)} %copy.169) | copy-start | bytes 786436
  100.4 45.3 %copy-start.41 = (f32[8,64]{1,0:T(8,128)}, f32[8,64]{1,0:T(8,128)S(1)}, u32[]{:S(2)}) copy-start(f32[8,64]{1,0:T(8,128)S(1)} %broadcast_multiply_fusion.3) | copy-start | bytes 6148
  100.4 8.8 %all-to-all-start.2 = ((bf16[8,64,128]{2,1,0:T(8,128)(2,1)}), bf16[8,64,128]{2,1,0:T(8,128)(2,1)S(1)}, u32[]{:S(2)}, u32[]{:S(2)}) async-start(bf16[8,64,128]{2,1,0:T(8,128)(2,1)} %get-tuple-element.487), calls=%async_computation.2 | async-start | bytes 262144 | tf_op jit(solution)/shard_map/all_to_all | solution.py:19
  143.5 5.9 %copy-start.39 = (f32[8,64]{1,0:T(8,128)S(1)}, f32[8,64]{1,0:T(8,128)}, u32[]{:S(2)}) copy-start(f32[8,64]{1,0:T(8,128)} %get-tuple-element.1126) | copy-start | bytes 6148
  145.7 28.2 %all-to-all-start.4 = ((bf16[8,8,64,128]{3,2,1,0:T(8,128)(2,1)}), bf16[8,8,64,128]{3,2,1,0:T(8,128)(2,1)S(1)}, u32[]{:S(2)}, u32[]{:S(2)}) async-start(bf16[8,8,64,128]{3,2,1,0:T(8,128)(2,1)} %broadcast_in_dim.169), calls=%async_computation.4 | async-start | bytes 2097152 | tf_op jit(solution)/shard_map/all_to_all | solution.py:19
  152.3 16.4 %copy-start.60 = (f32[128]{0:T(128)S(1)}, f32[128]{0:T(128)}, u32[]{:S(2)}) copy-start(f32[128]{0:T(128)} %get-tuple-element.478) | copy-start | bytes 1540
  235.3 7.5 %copy-start = (bf16[4,8,512,32]{2,3,1,0:T(8,128)(2,1)S(1)}, bf16[4,8,512,32]{2,3,1,0:T(8,128)(2,1)}, u32[]{:S(2)}) copy-start(bf16[4,8,512,32]{2,3,1,0:T(8,128)(2,1)} %get-tuple-element.227) | copy-start | bytes 3145732
  249.8 6.0 %copy-start.24 = (bf16[4,64,512]{2,1,0:T(8,128)(2,1)S(1)}, bf16[4,64,512]{2,1,0:T(8,128)(2,1)}, u32[]{:S(2)}) copy-start(bf16[4,64,512]{2,1,0:T(8,128)(2,1)} %get-tuple-element.226) | copy-start | bytes 786436
  250.9 24.8 %all-to-all-start.5 = ((bf16[8,600,128]{2,1,0:T(8,128)(2,1)}), bf16[8,600,128]{2,1,0:T(8,128)(2,1)}, u32[]{:S(2)}, u32[]{:S(2)}) async-start(bf16[8,600,128]{2,1,0:T(8,128)(2,1)} %pad_maximum_fusion.2), calls=%async_computation.5 | async-start | bytes 2457600 | tf_op jit(solution)/shard_map/all_to_all | solution.py:19
  256.1 27.6 %copy-start.40 = (f32[8,64]{1,0:T(8,128)S(1)}, f32[8,64]{1,0:T(8,128)}, u32[]{:S(2)}) copy-start(f32[8,64]{1,0:T(8,128)} %get-tuple-element.1128) | copy-start | bytes 6148
  277.1 44.6 %copy-start.42 = (f32[8,64]{1,0:T(8,128)S(1)}, f32[8,64]{1,0:T(8,128)}, u32[]{:S(2)}) copy-start(f32[8,64]{1,0:T(8,128)} %copy-done.41) | copy-start | bytes 6148
  277.1 44.6 %copy-start.46 = (f32[8,64]{1,0:T(8,128)S(1)}, f32[8,64]{1,0:T(8,128)}, u32[]{:S(2)}) copy-start(f32[8,64]{1,0:T(8,128)} %copy-done.45) | copy-start | bytes 6148
  279.1 50.8 %copy-start.25 = (f32[8,64,128]{2,1,0:T(8,128)S(1)}, f32[8,64,128]{2,1,0:T(8,128)}, u32[]{:S(2)}) copy-start(f32[8,64,128]{2,1,0:T(8,128)} %get-tuple-element.485) | copy-start | bytes 786436
  279.1 38.0 %all-to-all-start.6 = ((bf16[64,32,128]{2,1,0:T(8,128)(2,1)}), bf16[64,32,128]{2,1,0:T(8,128)(2,1)S(1)}, u32[]{:S(2)}, u32[]{:S(2)}) async-start(bf16[64,32,128]{2,1,0:T(8,128)(2,1)} %fusion.129), calls=%async_computation.6 | async-start | bytes 1048576 | tf_op jit(solution)/shard_map/all_to_all | solution.py:19
  317.1 11.5 %copy-start.15 = (bf16[64,32,128]{2,1,0:T(8,128)(2,1)}, bf16[64,32,128]{2,1,0:T(8,128)(2,1)S(1)}, u32[]{:S(2)}) copy-start(bf16[64,32,128]{2,1,0:T(8,128)(2,1)S(1)} %all-to-all-done.6) | copy-start | bytes 1572868
  317.8 8.8 %all-to-all-start.7 = ((bf16[8,64,128]{2,1,0:T(8,128)(2,1)}), bf16[8,64,128]{2,1,0:T(8,128)(2,1)S(1)}, u32[]{:S(2)}, u32[]{:S(2)}) async-start(bf16[8,64,128]{2,1,0:T(8,128)(2,1)} %bitcast.534), calls=%async_computation.7 | async-start | bytes 262144 | tf_op jit(solution)/shard_map/all_to_all | solution.py:19
  329.8 5.6 %copy-start.3 = (bf16[4,8,64,32]{2,3,1,0:T(8,128)(2,1)S(1)}, bf16[4,8,64,32]{2,3,1,0:T(8,128)(2,1)}, u32[]{:S(2)}) copy-start(bf16[4,8,64,32]{2,3,1,0:T(8,128)(2,1)} %copy-done.2) | copy-start | bytes 393220
  335.5 31.9 %copy-start.22 = (f32[8,64,128]{2,1,0:T(8,128)S(1)}, f32[8,64,128]{2,1,0:T(8,128)}, u32[]{:S(2)}) copy-start(f32[8,64,128]{2,1,0:T(8,128)} %copy-done.21) | copy-start | bytes 786436
  363.5 8.3 %copy-start.6 = (bf16[4,8,512,32]{2,3,1,0:T(8,128)(2,1)S(1)}, bf16[4,8,512,32]{2,3,1,0:T(8,128)(2,1)}, u32[]{:S(2)}) copy-start(bf16[4,8,512,32]{2,3,1,0:T(8,128)(2,1)} %get-tuple-element.232) | copy-start | bytes 3145732
  374.6 5.5 %copy-start.55 = (bf16[4,128]{1,0:T(4,128)(2,1)S(1)}, bf16[4,128]{1,0:T(4,128)(2,1)}, u32[]{:S(2)}) copy-start(bf16[4,128]{1,0:T(4,128)(2,1)} %fusion.122) | copy-start | bytes 3076
  374.7 5.5 %copy-start.59 = (bf16[128]{0:T(256)(128)(2,1)S(1)}, bf16[128]{0:T(256)(128)(2,1)}, u32[]{:S(2)}) copy-start(bf16[128]{0:T(256)(128)(2,1)} %get-tuple-element.357) | copy-start | bytes 772
  374.7 10.0 %copy-start.58 = (pred[512]{0:T(512)(128)(4,1)S(1)}, pred[512]{0:T(512)(128)(4,1)}, u32[]{:S(2)}) copy-start(pred[512]{0:T(512)(128)(4,1)} %broadcast_in_dim.175) | copy-start | bytes 1540
  386.7 4.8 copy-start.27
  387.9 25.3 %all-to-all-start.8 = ((bf16[8,664,128]{2,1,0:T(8,128)(2,1)}), bf16[8,664,128]{2,1,0:T(8,128)(2,1)S(1)}, u32[]{:S(2)}, u32[]{:S(2)}) async-start(bf16[8,664,128]{2,1,0:T(8,128)(2,1)} %pad_maximum_fusion), calls=%async_computation.8 | async-start | bytes 2719744 | tf_op jit(solution)/shard_map/all_to_all | solution.py:19
  391.5 57.3 %copy-start.13 = (bf16[8,64,128]{2,1,0:T(8,128)(2,1)S(1)}, bf16[8,64,128]{2,1,0:T(8,128)(2,1)}, u32[]{:S(2)}) copy-start(bf16[8,64,128]{2,1,0:T(8,128)(2,1)} %copy-done.12) | copy-start | bytes 393220
  391.7 57.3 %copy-start.11 = (f32[8,64,128]{2,1,0:T(8,128)S(1)}, f32[8,64,128]{2,1,0:T(8,128)}, u32[]{:S(2)}) copy-start(f32[8,64,128]{2,1,0:T(8,128)} %get-tuple-element.475) | copy-start | bytes 786436
  391.7 57.3 %copy-start.49 = (f32[128]{0:T(128)S(1)}, f32[128]{0:T(128)}, u32[]{:S(2)}) copy-start(f32[128]{0:T(128)} %copy-done.48) | copy-start | bytes 1540
  391.7 57.2 %copy-start.52 = (bf16[2,128,4]{1,2,0:T(4,128)(2,1)S(1)}, bf16[2,128,4]{1,2,0:T(4,128)(2,1)}, u32[]{:S(2)}) copy-start(bf16[2,128,4]{1,2,0:T(4,128)(2,1)} %param.25) | copy-start | bytes 6148
  414.1 40.8 %copy-start.44 = (f32[8,64]{1,0:T(8,128)S(1)}, f32[8,64]{1,0:T(8,128)}, u32[]{:S(2)}) copy-start(f32[8,64]{1,0:T(8,128)} %copy-done.43) | copy-start | bytes 6148
  414.1 34.7 %all-to-all-start.9 = ((bf16[64,24,128]{2,1,0:T(8,128)(2,1)}), bf16[64,24,128]{2,1,0:T(8,128)(2,1)S(1)}, u32[]{:S(2)}, u32[]{:S(2)}) async-start(bf16[64,24,128]{2,1,0:T(8,128)(2,1)} %fusion.130), calls=%async_computation.9 | async-start | bytes 786432 | tf_op jit(solution)/shard_map/all_to_all | solution.py:19
  450.3 28.3 %all-to-all-start.10 = ((bf16[64,16,128]{2,1,0:T(8,128)(2,1)}), bf16[64,16,128]{2,1,0:T(8,128)(2,1)S(1)}, u32[]{:S(2)}, u32[]{:S(2)}) async-start(bf16[64,16,128]{2,1,0:T(8,128)(2,1)} %broadcast_in_dim.185), calls=%async_computation.10 | async-start | bytes 524288 | tf_op jit(solution)/shard_map/all_to_all | solution.py:19
  478.8 4.9 copy-start.19
  479.8 16.9 %all-to-all-start.11 = ((f32[8,184,128]{2,1,0:T(8,128)}), f32[8,184,128]{2,1,0:T(8,128)S(1)}, u32[]{:S(2)}, u32[]{:S(2)}) async-start(f32[8,184,128]{2,1,0:T(8,128)} %broadcast_in_dim.186), calls=%async_computation.11 | async-start | bytes 1507328 | tf_op jit(solution)/shard_map/all_to_all | solution.py:19
  (25 other events, 37.3 us)

commit v2 on v1

v2 whole, which is shorter than its diff:
```python
import functools
import math

import jax
import jax.numpy as jnp
from jax import lax
from jax.experimental import pallas as pl
from jax.experimental.pallas import tpu as pltpu
from jax.sharding import Mesh
from jax.sharding import PartitionSpec as P

HEAD = ("head_0", "head_1")
ROW_HEAD = ("row", "head_0", "head_1")


EPS = 1e-05
MASKED = 1000000000.0
LANES = 128
INTERPRET = False


def exchanged(parts, axis):
    return lax.all_to_all(parts, axis, split_axis=0, concat_axis=0, tiled=True)


def to_all(x, axis):
    return jnp.broadcast_to(x[None], (lax.axis_size(axis), *x.shape))


def layer_norm(values, norm_scale, norm_offset):
    floats = values.astype(jnp.float32)
    centred = floats - jnp.mean(floats, axis=-1, keepdims=True)
    inverse = lax.rsqrt(jnp.mean(centred * centred, axis=-1, keepdims=True) + EPS)
    normed = centred * inverse
    return (normed, inverse, (normed * norm_scale + norm_offset).astype(jnp.bfloat16))


def norm_backward(grad_normal, normed, inverse, norm_scale):
    grad_hat = grad_normal * norm_scale
    first_mean = jnp.mean(grad_hat, axis=-1, keepdims=True)
    second_mean = jnp.mean(grad_hat * normed, axis=-1, keepdims=True)
    return inverse * (grad_hat - first_mean - normed * second_mean)


def matmul(a, b, a_dim, b_dim):
    return lax.dot_general(
        a, b, (((a_dim,), (b_dim,)), ((), ())), preferred_element_type=jnp.float32
    )


def lanes_of_head(shape, head, head_size):
    lanes = lax.broadcasted_iota(jnp.int32, shape, 1)
    return (lanes >= head * head_size) & (lanes < (head + 1) * head_size)


def spread_heads(values, heads):
    size = values.shape[1] // heads
    kept = [
        jnp.where(lanes_of_head(values.shape, head, size), values, 0.0) for head in range(heads)
    ]
    return jnp.concatenate(kept, axis=0).astype(jnp.bfloat16)


def picked_heads(stacked, heads):
    rows = stacked.shape[0] // heads
    size = stacked.shape[1] // heads
    total = jnp.zeros((rows, stacked.shape[1]), jnp.float32)
    for head in range(heads):
        part = stacked[head * rows : (head + 1) * rows]
        total = jnp.where(lanes_of_head(part.shape, head, size), part, total)
    return total


def attention(x, xq, bias, wq, wkv, wg, gate_offset, heads):
    channels = wq.shape[1]
    scale = 1.0 / math.sqrt(channels // heads)
    queries = spread_heads(
        (matmul(xq, wq, 1, 0) * scale).astype(jnp.bfloat16).astype(jnp.float32), heads
    )
    key_value = matmul(x, wkv, 1, 0).astype(jnp.bfloat16)
    keys = key_value[:, :channels]
    values = key_value[:, channels:]
    gate = jax.nn.sigmoid(matmul(xq, wg, 1, 0) + gate_offset)
    logits = matmul(queries, keys, 1, 1) + bias
    weights = jnp.exp(logits - jnp.max(logits, axis=1, keepdims=True))
    probs = weights / jnp.sum(weights, axis=1, keepdims=True)
    probs_half = probs.astype(jnp.bfloat16)
    attended = picked_heads(matmul(probs_half, values, 1, 0), heads)
    return (queries, keys, values, gate, probs, probs_half, attended)


def split_bias(bias, key_bias, heads):
    count = bias.shape[1] // heads
    parts = [bias[:, head * count : (head + 1) * count] for head in range(heads)]
    return jnp.concatenate(parts, axis=0).astype(jnp.float32) + key_bias


def forward_kernel(heads, positions, class_ref, rows_ref, bias_ref, mask_ref, wq_ref, wkv_ref,
                   wg_ref, wo_ref, gate_ref, after_ref, full_bias):
    groups = after_ref.shape[1]

    @pl.when(pl.program_id(0) == 0)
    def _():
        full_bias[...] = split_bias(bias_ref[...], mask_ref[...], heads)

    x = rows_ref[0, :positions]
    start = pl.multiple_of(class_ref[0] * groups, groups)
    xq = rows_ref[0, pl.ds(start, groups)]
    result = attention(
        x, xq, full_bias[...], wq_ref[...], wkv_ref[...], wg_ref[...], gate_ref[...], heads
    )
    gated = (result[3] * result[6]).astype(jnp.bfloat16)
    update = matmul(gated, wo_ref[...], 1, 0).astype(jnp.bfloat16)
    pair = rows_ref[0, positions : positions + groups]
    after_ref[0] = (pair.astype(jnp.float32) + update.astype(jnp.float32)).astype(jnp.bfloat16)


def backward_kernel(heads, positions, second, share_rows, class_ref, rows_ref, bias_ref, mask_ref,
                    grad_ref, extra_ref, ride_ref, wq_ref, wkv_ref, wg_ref, wo_ref, gate_ref,
                    sent_ref, bias_out_ref, full_bias, bias_sum, weight_sum, share):
    step = pl.program_id(0)
    classes = sent_ref.shape[0]
    groups = positions // classes
    channels = wq_ref.shape[0]
    inner = wq_ref.shape[1]
    own_class = class_ref[0]
    share_start = positions if second else positions + groups

    @pl.when(step == 0)
    def _():
        if second:
            full_bias[...] = bias_ref[...].astype(jnp.float32).T + mask_ref[...]
        else:
            full_bias[...] = split_bias(bias_ref[...], mask_ref[...], heads)
            sent_ref[:, positions : positions + groups] = ride_ref[...]
        bias_sum[...] = jnp.zeros(bias_sum.shape, jnp.float32)
        weight_sum[...] = jnp.zeros(weight_sum.shape, jnp.float32)
        weight_sum[5 * channels : 5 * channels + 8] = extra_ref[...]

    if second:
        x = rows_ref[:, 0].reshape(positions, channels)
        xq = rows_ref[pl.ds(own_class, 1), 0].reshape(groups, channels)
    else:
        x = rows_ref[0, :positions]
        xq = rows_ref[0, pl.ds(pl.multiple_of(own_class * groups, groups), groups)]
    queries, keys, values, gate, probs, probs_half, attended = attention(
        x, xq, full_bias[...], wq_ref[...], wkv_ref[...], wg_ref[...], gate_ref[...], heads
    )
    scale = 1.0 / math.sqrt(inner // heads)
    grad = grad_ref[0]
    gated = (gate * attended).astype(jnp.bfloat16)
    grad_gated = matmul(grad, wo_ref[...], 1, 1)
    grad_att = (grad_gated * gate).astype(jnp.bfloat16).astype(jnp.float32)
    grad_pre = (grad_gated * attended * gate * (1.0 - gate)).astype(jnp.bfloat16)
    grad_heads = spread_heads(grad_att, heads)
    grad_probs = matmul(grad_heads, values, 1, 1)
    grad_logits = probs * (grad_probs - jnp.sum(probs * grad_probs, axis=1, keepdims=True))
    bias_sum[...] += grad_logits
    logits_half = grad_logits.astype(jnp.bfloat16)
    grad_queries = (picked_heads(matmul(logits_half, keys, 1, 0), heads) * scale).astype(
        jnp.bfloat16
    )
    grad_keys = matmul(logits_half, queries, 0, 0).astype(jnp.bfloat16)
    grad_values = matmul(probs_half, grad_heads, 0, 0).astype(jnp.bfloat16)
    grad_pairs = jnp.concatenate([grad_keys, grad_values], axis=1)
    share[...] = matmul(grad_pairs, wkv_ref[...], 1, 1)
    query_side = matmul(grad_queries, wq_ref[...], 1, 1) + matmul(grad_pre, wg_ref[...], 1, 1)
    own_rows = pl.ds(pl.multiple_of(own_class * groups, groups), groups)
    share[own_rows] = share[own_rows] + query_side
    partial = share[...].astype(jnp.bfloat16)
    if second:
        place = pl.ds(pl.multiple_of(step * groups, groups), groups)
        sent_ref[:, place] = partial.reshape(classes, groups, channels)
    else:
        sent_ref[pl.ds(step, 1), :positions] = partial[None]
    pair_sums = matmul(x, grad_pairs, 0, 0)
    weight_sum[:channels] += matmul(xq, grad_queries, 0, 0)
    weight_sum[channels : 2 * channels] += pair_sums[:, :inner]
    weight_sum[2 * channels : 3 * channels] += pair_sums[:, inner:]
    weight_sum[3 * channels : 4 * channels] += matmul(xq, grad_pre, 0, 0)
    weight_sum[4 * channels : 5 * channels] += matmul(gated, grad, 0, 0)
    weight_sum[5 * channels : 5 * channels + 1] += jnp.sum(
        grad_pre.astype(jnp.float32), axis=0, keepdims=True
    )

    @pl.when(step == pl.num_programs(0) - 1)
    def _():
        for peer in range(classes):
            sent_ref[peer, share_start : share_start + share_rows] = weight_sum[
                peer * share_rows : (peer + 1) * share_rows
            ].astype(jnp.bfloat16)
        if second:
            bias_out_ref[...] = bias_sum[...].T.astype(jnp.bfloat16)
        else:
            for head in range(heads):
                bias_out_ref[:, head * positions : (head + 1) * positions] = bias_sum[
                    head * groups : (head + 1) * groups
                ].astype(jnp.bfloat16)


def whole_spec(x):
    return pl.BlockSpec(x.shape, lambda step, n=x.ndim: (0,) * n)


def kernel_weights(params):
    _, _, projection, gate_offset, out_proj, _ = params
    joined = jnp.concatenate([projection[1], projection[2]], axis=1)
    return (projection[0], joined, projection[3], out_proj, gate_offset[None])


def forward_call(own_class, rows, bias, key_bias, params, heads, positions):
    classes, _, channels = rows.shape
    groups = positions // classes
    rest = (bias, key_bias, *kernel_weights(params))
    return pl.pallas_call(
        functools.partial(forward_kernel, heads, positions),
        grid=(classes,),
        in_specs=[
            pl.BlockSpec(memory_space=pltpu.SMEM),
            pl.BlockSpec((1, *rows.shape[1:]), lambda step: (step, 0, 0)),
            *[whole_spec(x) for x in rest],
        ],
        out_specs=pl.BlockSpec((1, groups, channels), lambda step: (step, 0, 0)),
        out_shape=jax.ShapeDtypeStruct((classes, groups, channels), jnp.bfloat16),
        scratch_shapes=[pltpu.VMEM((heads * groups, positions), jnp.float32)],
        compiler_params=pltpu.CompilerParams(dimension_semantics=("arbitrary",)),
        interpret=INTERPRET,
        name="forward_rows",
    )(own_class, rows, *rest)


def backward_call(own_class, rows, bias, key_bias, grad, extra, ride, params, heads, positions,
                  share_rows):
    second = ride is None
    classes, groups, channels = grad.shape
    inner = params[2].shape[2]
    if second:
        ride = jnp.zeros((8, LANES), jnp.bfloat16)
        rows_spec = pl.BlockSpec((classes, 1, groups, channels), lambda step: (0, step, 0, 0))
        bias_shape = (positions, heads * groups)
        sent_rows = positions + share_rows
    else:
        rows_spec = pl.BlockSpec((1, *rows.shape[1:]), lambda step: (step, 0, 0))
        bias_shape = (groups, heads * positions)
        sent_rows = positions + groups + share_rows
    weights = kernel_weights(params)
    sent = jax.ShapeDtypeStruct((classes, sent_rows, channels), jnp.bfloat16)
    bias_out = jax.ShapeDtypeStruct(bias_shape, jnp.bfloat16)
    return pl.pallas_call(
        functools.partial(backward_kernel, heads, positions, second, share_rows),
        grid=(classes,),
        in_specs=[
            pl.BlockSpec(memory_space=pltpu.SMEM),
            rows_spec,
            whole_spec(bias),
            whole_spec(key_bias),
            pl.BlockSpec((1, groups, channels), lambda step: (step, 0, 0)),
            whole_spec(extra),
            whole_spec(ride),
            *[whole_spec(x) for x in weights],
        ],
        out_specs=[whole_spec(sent), whole_spec(bias_out)],
        out_shape=[sent, bias_out],
        scratch_shapes=[
            pltpu.VMEM((heads * groups, positions), jnp.float32),
            pltpu.VMEM((heads * groups, positions), jnp.float32),
            pltpu.VMEM((classes * share_rows, channels), jnp.float32),
            pltpu.VMEM((positions, channels), jnp.float32),
        ],
        compiler_params=pltpu.CompilerParams(dimension_semantics=("arbitrary",)),
        interpret=INTERPRET,
        name="backward_second" if second else "backward_first",
    )(own_class, rows, bias, key_bias, grad, extra, ride, *weights)


def padded_rows(x, rows):
    return jnp.pad(x, ((0, 0),) * (x.ndim - 2) + ((0, rows - x.shape[-2]), (0, 0)))


def rounded_up(value, step):
    return -(-value // step) * step


def local(
    pair_input,
    cotangent,
    residue_mask,
    norm_gain,
    norm_shift,
    proj_weights,
    gate_bias,
    out_weights,
    bias_weights,
):
    channels = pair_input.shape[2]
    groups = lax.axis_size("row")
    classes = lax.axis_size(HEAD)
    positions = groups * classes
    head_total = bias_weights.shape[2]
    bias_rows = head_total * positions // LANES
    half = jnp.bfloat16
    key_bias = (residue_mask.astype(jnp.float32) - 1.0) * MASKED
    key_bias = key_bias.reshape(groups, classes).T.reshape(1, positions)
    own_class = lax.axis_index(HEAD).astype(jnp.int32).reshape(1)
    main_rows = 5 * channels + 1
    share_rows = rounded_up(-(-(main_rows + head_total + 2) // classes), 16)
    group_rows = rounded_up(share_rows, groups) // groups
    params = [
        (
            norm_gain[which],
            norm_shift[which],
            proj_weights[which],
            gate_bias[which],
            out_weights[which],
            bias_weights[which],
        )
        for which in range(2)
    ]

    own_pair = pair_input.reshape(groups, classes, channels).transpose(1, 0, 2)
    normed_own, inverse_own, normal_own = layer_norm(own_pair, norm_gain[0], norm_shift[0])
    normal_flat = normal_own.reshape(positions, channels)
    bias_own = jnp.einsum(
        "nc,ch->hn", normal_flat, bias_weights[0], preferred_element_type=jnp.float32
    ).astype(half)
    own_cotangent = cotangent.reshape(groups, classes, channels)
    arrived = exchanged(
        jnp.concatenate(
            [to_all(normal_flat, HEAD), own_pair, own_cotangent.transpose(1, 0, 2)], axis=1
        ),
        HEAD,
    )
    first_rows = arrived
    cotangent_query = arrived[:, positions + groups :]
    arrived = exchanged(
        jnp.concatenate(
            [
                to_all(bias_own.reshape(bias_rows, LANES), "row"),
                own_cotangent,
            ],
            axis=1,
        ),
        "row",
    )
    first_bias = arrived[:, :bias_rows].reshape(groups, head_total * positions)
    second_grad_query = arrived[:, bias_rows:].transpose(1, 0, 2)

    after_query = forward_call(
        own_class, first_rows, first_bias, key_bias, params[0], head_total, positions
    )
    after_normed, after_inverse, after_normal = layer_norm(
        after_query, norm_gain[1], norm_shift[1]
    )
    second_bias_own = jnp.einsum(
        "abc,ch->ahb", after_normal, bias_weights[1], preferred_element_type=jnp.float32
    ).astype(half)
    after_own = exchanged(after_query, HEAD)
    arrived = exchanged(
        jnp.concatenate(
            [
                to_all(second_bias_own.reshape(bias_rows, LANES), "row"),
                after_own.transpose(1, 0, 2),
            ],
            axis=1,
        ),
        "row",
    )
    second_bias = (
        arrived[:, :bias_rows]
        .reshape(groups, classes, head_total * groups)
        .transpose(1, 0, 2)
        .reshape(positions, head_total * groups)
    )
    flipped_query = arrived[:, bias_rows:].transpose(1, 0, 2)
    _, _, second_query = layer_norm(flipped_query, norm_gain[1], norm_shift[1])
    second_rows = exchanged(to_all(second_query, HEAD), HEAD)
    sent, bias_parts = backward_call(
        own_class,
        second_rows.reshape(classes, classes, groups, channels),
        second_bias,
        key_bias,
        second_grad_query,
        jnp.zeros((8, LANES), jnp.float32),
        None,
        params[1],
        head_total,
        positions,
        share_rows,
    )

    def group_shares_of(arrived_shares):
        summed = jnp.sum(arrived_shares.astype(jnp.float32), axis=0)
        summed = padded_rows(summed, groups * group_rows).astype(half)
        return padded_rows(summed.reshape(groups, group_rows, LANES), rounded_up(group_rows, 8))

    arrived = exchanged(sent, HEAD)
    grad_flipped = jnp.sum(arrived[:, :positions].astype(jnp.float32), axis=0).astype(half)
    bias_parts = (
        bias_parts.reshape(classes, groups, head_total * groups)
        .transpose(1, 0, 2)
        .reshape(groups, bias_rows, LANES)
    )
    arrived = exchanged(
        jnp.concatenate(
            [
                bias_parts,
                grad_flipped.reshape(classes, groups, channels).transpose(1, 0, 2),
                group_shares_of(arrived[:, positions:]),
            ],
            axis=1,
        ),
        "row",
    )
    summed = jnp.sum(arrived[:, :bias_rows].astype(jnp.float32), axis=0)
    second_bias_half = summed.reshape(classes, head_total, groups).astype(half)
    second_own = jnp.sum(
        arrived[:, bias_rows + classes : bias_rows + classes + group_rows].astype(jnp.float32),
        axis=0,
    )
    grad_query = exchanged(arrived[:, bias_rows : bias_rows + classes].transpose(1, 0, 2), HEAD)
    grad_normal = grad_query.astype(jnp.float32) + jnp.einsum(
        "ahb,ch->abc", second_bias_half, bias_weights[1], preferred_element_type=jnp.float32
    )
    end_query = norm_backward(grad_normal, after_normed, after_inverse, norm_gain[1]).astype(half)
    second_small = jnp.concatenate(
        [
            jnp.einsum(
                "abc,ahb->hc", after_normal, second_bias_half, preferred_element_type=jnp.float32
            ),
            jnp.sum(grad_normal * after_normed, axis=(0, 1))[None],
            jnp.sum(grad_normal, axis=(0, 1))[None],
        ],
        axis=0,
    )

    after_grad_query = (
        cotangent_query.astype(jnp.float32) + end_query.astype(jnp.float32)
    ).astype(half)
    extra = jnp.pad(second_small, ((1, 7 - second_small.shape[0]), (0, 0)))
    sent, bias_parts = backward_call(
        own_class,
        first_rows,
        first_bias,
        key_bias,
        after_grad_query,
        extra,
        end_query,
        params[0],
        head_total,
        positions,
        share_rows,
    )
    arrived = exchanged(sent, HEAD)
    grad_normal = jnp.sum(arrived[:, :positions].astype(jnp.float32), axis=0)
    end_own = arrived[:, positions : positions + groups]
    shares = arrived[:, positions + groups :]
    arrived = exchanged(
        jnp.concatenate(
            [
                bias_parts.reshape(groups, bias_rows, LANES),
                group_shares_of(shares),
            ],
            axis=1,
        ),
        "row",
    )
    summed = jnp.sum(arrived[:, :bias_rows].astype(jnp.float32), axis=0)
    bias_half = summed.reshape(head_total, positions).astype(half)
    first_own = jnp.sum(
        arrived[:, bias_rows : bias_rows + group_rows].astype(jnp.float32), axis=0
    )
    grad_normal = grad_normal + jnp.einsum(
        "hn,ch->nc", bias_half, bias_weights[0], preferred_element_type=jnp.float32
    )
    normed_flat = normed_own.reshape(positions, channels)
    start_grad = norm_backward(
        grad_normal, normed_flat, inverse_own.reshape(positions, 1), norm_gain[0]
    )
    moved_grad = (end_own.astype(jnp.float32) + start_grad.reshape(end_own.shape)).transpose(1, 0, 2)
    pair_grad = cotangent.astype(jnp.float32) + moved_grad.reshape(1, positions, channels)
    first_small = jnp.concatenate(
        [
            jnp.einsum("nc,hn->hc", normal_flat, bias_half, preferred_element_type=jnp.float32),
            jnp.sum(grad_normal * normed_flat, axis=0)[None],
            jnp.sum(grad_normal, axis=0)[None],
        ],
        axis=0,
    )

    small_rows = first_small.shape[0]
    tail = jnp.concatenate([first_own, second_own, first_small], axis=0).astype(half)
    tail = padded_rows(tail, rounded_up(tail.shape[0], 8))
    arrived = exchanged(to_all(tail, "row"), "row").astype(jnp.float32)
    whole_rows = groups * group_rows
    shared = jnp.concatenate(
        [
            arrived[:, :group_rows].reshape(whole_rows, LANES)[:share_rows],
            arrived[:, group_rows : 2 * group_rows].reshape(whole_rows, LANES)[:share_rows],
            padded_rows(
                jnp.sum(arrived[:, 2 * group_rows : 2 * group_rows + small_rows], axis=0),
                rounded_up(small_rows, 8),
            ),
        ],
        axis=0,
    )
    arrived = exchanged(to_all(shared, HEAD), HEAD)
    first_whole = arrived[:, :share_rows].reshape(-1, LANES)
    second_whole = arrived[:, share_rows : 2 * share_rows].reshape(-1, LANES)
    first_small = jnp.sum(arrived[:, 2 * share_rows : 2 * share_rows + small_rows], axis=0)
    second_small = first_whole[main_rows : main_rows + small_rows]
    proj_rows = 4 * channels

    def both(first, second):
        return jnp.stack([first, second])

    return (
        pair_grad,
        both(first_whole[:proj_rows], second_whole[:proj_rows]).reshape(
            2, 4, channels, -1
        ),
        both(first_whole[main_rows - 1], second_whole[main_rows - 1]),
        both(first_whole[proj_rows : main_rows - 1], second_whole[proj_rows : main_rows - 1]),
        both(first_small[:head_total].T, second_small[:head_total].T),
        both(first_small[head_total], second_small[head_total]),
        both(first_small[head_total + 1], second_small[head_total + 1]),
    )


def solution(mesh):
    finer = Mesh(mesh.devices.reshape(mesh.shape["row"], 4, 2), ("row", "head_0", "head_1"))
    in_specs = (P(ROW_HEAD, None, None), P(ROW_HEAD, None, None), P(), P(), P(), P(), P(), P(), P())
    out_specs = (P(ROW_HEAD, None, None), P(), P(), P(), P(), P(), P())
    return jax.shard_map(local, mesh=finer, in_specs=in_specs, out_specs=out_specs, check_vma=False)
```

time: 505 us -> 382 us (0.76)
  matrix products: 105 us -> 3.37 us
  local copies, waits for them, and re-layouts: 71 us -> 12.9 us
  Pallas kernels: 0 us -> 41.2 us
  blocking collectives: 34.2 us -> 74.3 us
  other arithmetic: 41.2 us -> 19.6 us
  starting transfers between devices: 67.7 us -> 55.9 us
  waiting for transfers between devices: 180 us -> 172 us
    dot_general x85 -> x2, matrix products: 103 us -> 0.76 us  [the longest x1 0.44 us: local(): jnp.einsum('ahb,ch->abc', second_bias_half, bias_weights[1], preferred_el...]
    pallas_call x0 -> x3, Pallas kernels: none -> 41.2 us  [the longest x2 31.6 us: backward_call(): pl.pallas_call(functools.partial(backward_kernel, heads, positions, secon...]
    all_to_all x1 -> x2, blocking collectives: 34.2 us -> 74.3 us  [exchanged(): return lax.all_to_all(parts, axis, split_axis=0, concat_axis=0, tiled=True)]
    all_to_all x11 -> x10, starting transfers between devices: 67.7 us -> 55.9 us  [exchanged(): return lax.all_to_all(parts, axis, split_axis=0, concat_axis=0, tiled=True)]
    add x16 -> x0, other arithmetic: 10.3 us -> none  [the longest x8 6.85 us: differentiate(): logits = logits + bias_head.astype(jnp.float32)[None] + key_bias]
    another operation x12 -> x0, local copies, waits for them, and re-layouts: 8.97 us -> none
    all_to_all x11 -> x10, waiting for transfers between devices: 180 us -> 172 us  [exchanged(): return lax.all_to_all(parts, axis, split_axis=0, concat_axis=0, tiled=True)]
    reshape x11 -> x4, local copies, waits for them, and re-layouts: 6.65 us -> 0.99 us  [the longest x2 0.75 us: local(): key_bias = key_bias.reshape(groups, classes).T.reshape(1, positions)]
  transfers between devices with their start and end apart: 11 -> 10, of which waited for: 10 -> 10; matrix products, arithmetic and copies ran while one was open for 7% -> 3% of each run, Pallas kernels for 0% -> 0%
where the time goes in v2:
time: 382 us; the launch traced here: 380 us
  waiting for transfers between devices  172 us (45%)
  blocking collectives  74.3 us (19%)
  starting transfers between devices  55.9 us (15%)
  Pallas kernels  41.2 us (11%)
  other arithmetic  19.6 us (5%)
  local copies, waits for them, and re-layouts  12.9 us (3%)
    all_to_all x10, waiting for transfers between devices, exchanged(): return lax.all_to_all(parts, axis, split_axis=0, concat_axis=0, tiled=True)  172 us
    all_to_all x2, blocking collectives, exchanged(): return lax.all_to_all(parts, axis, split_axis=0, concat_axis=0, tiled=True)  74.3 us
    all_to_all x10, starting transfers between devices, exchanged(): return lax.all_to_all(parts, axis, split_axis=0, concat_axis=0, tiled=True)  55.9 us
    pallas_call x2, Pallas kernels, backward_call(): pl.pallas_call(functools.partial(backward_kernel, heads, positions, secon...  31.6 us
    pallas_call x1, Pallas kernels, forward_call(): pl.pallas_call(functools.partial(forward_kernel, heads, positions), grid=...  9.58 us
  transfers between devices with their start and end apart: 10, of which 10 were waited for; matrix products, arithmetic and copies ran while one was open for 3% of the time, Pallas kernels for 0%

profile of v2, /device:TPU:1, one launch (start us, length us, event | category | flops | bytes accessed | tf_op | source)
XLA Modules:
  0.0 380.3 jit_solution(9124904628828961575)
XLA Ops:
  0.6 1.0 convert_reduce_fusion.2
  1.7 1.2 fusion.22
  2.9 0.8 slice_bitcast_fusion.14
  3.7 1.1 add_convert_fusion.1
  4.9 0.8 fusion.1
  5.7 1.7 pad_maximum_fusion.2
  7.4 19.8 %all-to-all-start.1 = ((bf16[64,24,128]{2,1,0:T(8,128)(2,1)}), bf16[64,24,128]{2,1,0:T(8,128)(2,1)S(1)}, u32[]{:S(2)}, u32[]{:S(2)}) async-start(bf16[64,24,128]{2,1,0:T(8,128)(2,1)} %pad_maximum_fusion.2), calls=%async_computation.1 | async-start | bytes 786432 | tf_op jit(solution)/shard_map/all_to_all | solution.py:23
  27.4 1.1 pad_maximum_fusion
  28.6 27.4 %all-to-all-done.1 = bf16[64,24,128]{2,1,0:T(8,128)(2,1)S(1)} async-done(((bf16[64,24,128]{2,1,0:T(8,128)(2,1)}), bf16[64,24,128]{2,1,0:T(8,128)(2,1)S(1)}, u32[]{:S(2)}, u32[]{:S(2)}) %all-to-all-start.1) | async-done | bytes 393248 | tf_op jit(solution)/shard_map/all_to_all | solution.py:23
  56.0 4.1 %all-to-all-start = ((bf16[8,640,128]{2,1,0:T(8,128)(2,1)}), bf16[8,640,128]{2,1,0:T(8,128)(2,1)S(1)}, u32[]{:S(2)}, u32[]{:S(2)}) async-start(bf16[8,640,128]{2,1,0:T(8,128)(2,1)} %pad_maximum_fusion), calls=%async_computation | async-start | bytes 2621440 | tf_op jit(solution)/shard_map/all_to_all | solution.py:23
  60.3 0.7 reshape.189.mask_ref
  63.4 0.8 copy.73
  64.2 16.4 %all-to-all-done.rows_ref = bf16[8,640,128]{2,1,0:T(8,128)(2,1)S(1)} async-done(((bf16[8,640,128]{2,1,0:T(8,128)(2,1)}), bf16[8,640,128]{2,1,0:T(8,128)(2,1)S(1)}, u32[]{:S(2)}, u32[]{:S(2)}) %all-to-all-start) | async-done | bytes 1310752 | tf_op jit(solution)/shard_map/all_to_all | solution.py:23
  80.6 1.1 copy-done
  81.7 9.6 %forward_rows.1 = bf16[8,64,128]{2,1,0:T(8,128)(2,1)} custom-call(s32[1]{0:T(128)} %bitcast.class_ref, bf16[8,640,128]{2,1,0:T(8,128)(2,1)} %copy-done, bf16[64,2048]{1,0:T(8,128)(2,1)} %bitcast.157, f32[1,512]{1,0:T(1,128)} %reshape.189.mask_ref, bf16[128,128]{1,0:T(8,128)(2,1)} %get-tuple-element.38.wq_ref, bf16[128,256]{1,0:T(8,128)(2,1)} %pad_maximum_fusion.5.wkv_ref, ...), custom_call_target="tpu_custom_call" | custom-call | tf_op jit(solution)/shard_map/forward_rows/pallas_call | solution.py:215
  91.3 1.0 convert_reduce_fusion.1
  92.3 3.4 all-to-all-start.2
  95.7 1.2 fusion.21
  97.0 1.2 fusion
  98.3 2.6 all-to-all-done.2
  101.1 35.3 %all_to_all.60 = bf16[64,24,128]{2,1,0:T(8,128)(2,1)S(1)} all-to-all(bf16[64,24,128]{2,1,0:T(8,128)(2,1)S(1)} %pad_maximum_fusion.3), channel_id=1, replica_groups=mesh['row'=64,'head_0'=4,'head_1'=2] {'row'}, dimensions={0} | all-to-all | bytes 786432 | tf_op jit(solution)/shard_map/all_to_all | solution.py:23
  137.1 1.2 broadcast_in_dim.75
  138.3 3.6 all-to-all-start.4
  143.3 0.8 copy.43
  144.1 13.7 %all-to-all-done.4.rows_ref = bf16[8,8,64,128]{3,2,1,0:T(8,128)(2,1)S(1)} async-done(((bf16[8,8,64,128]{3,2,1,0:T(8,128)(2,1)}), bf16[8,8,64,128]{3,2,1,0:T(8,128)(2,1)S(1)}, u32[]{:S(2)}, u32[]{:S(2)}) %all-to-all-start.4) | async-done | bytes 1048608 | tf_op jit(solution)/shard_map/all_to_all | solution.py:23
  159.0 15.8 %backward_second.1 = (bf16[8,608,128]{2,1,0:T(8,128)(2,1)}, bf16[512,256]{1,0:T(8,128)(2,1)}) custom-call(s32[1]{0:T(128)} %bitcast.class_ref, bf16[8,8,64,128]{3,2,1,0:T(8,128)(2,1)} %copy-done.1, bf16[512,256]{1,0:T(8,128)(2,1)} %bitcast.179, f32[1,512]{1,0:T(1,128)} %reshape.189.mask_ref, bf16[8,64,128]{2,1,0:T(8,128)(2,1)} %bitcast.187, ...), custom_call_target="tpu_custom_call" | custom-call | tf_op jit(solution)/shard_map/backward_second/pallas_call | solution.py:249
  174.8 3.7 all-to-all-start.5
  178.8 19.6 %all-to-all-done.5 = bf16[8,608,128]{2,1,0:T(8,128)(2,1)S(1)} async-done(((bf16[8,608,128]{2,1,0:T(8,128)(2,1)}), bf16[8,608,128]{2,1,0:T(8,128)(2,1)S(1)}, u32[]{:S(2)}, u32[]{:S(2)}) %all-to-all-start.5) | async-done | bytes 1245216 | tf_op jit(solution)/shard_map/all_to_all | solution.py:23
  198.7 38.9 %all_to_all.61 = bf16[64,32,128]{2,1,0:T(8,128)(2,1)S(1)} all-to-all(bf16[64,32,128]{2,1,0:T(8,128)(2,1)S(1)} %fusion.4), channel_id=1, replica_groups=mesh['row'=64,'head_0'=4,'head_1'=2] {'row'}, dimensions={0} | all-to-all | bytes 1048576 | tf_op jit(solution)/shard_map/all_to_all | solution.py:23
  237.7 0.7 copy.75
  238.5 3.4 all-to-all-start.7
  242.2 4.9 %all-to-all-done.7 = bf16[8,64,128]{2,1,0:T(8,128)(2,1)S(1)} async-done(((bf16[8,64,128]{2,1,0:T(8,128)(2,1)}), bf16[8,64,128]{2,1,0:T(8,128)(2,1)S(1)}, u32[]{:S(2)}, u32[]{:S(2)}) %all-to-all-start.7) | async-done | bytes 131104 | tf_op jit(solution)/shard_map/all_to_all | solution.py:23
  248.2 1.9 add_convert_fusion
  250.2 15.8 %backward_first.1 = (bf16[8,672,128]{2,1,0:T(8,128)(2,1)}, bf16[64,2048]{1,0:T(8,128)(2,1)}) custom-call(s32[1]{0:T(128)} %bitcast.class_ref, bf16[8,640,128]{2,1,0:T(8,128)(2,1)} %copy-done, bf16[64,2048]{1,0:T(8,128)(2,1)} %bitcast.158, f32[1,512]{1,0:T(1,128)} %reshape.189.mask_ref, bf16[8,64,128]{2,1,0:T(8,128)(2,1)} %get-tuple-element.23.grad_ref, ...), custom_call_target="tpu_custom_call" | custom-call | tf_op jit(solution)/shard_map/backward_first/pallas_call | solution.py:249
  266.0 3.7 all-to-all-start.8
  269.7 21.9 %all-to-all-done.8 = bf16[8,672,128]{2,1,0:T(8,128)(2,1)S(1)} async-done(((bf16[8,672,128]{2,1,0:T(8,128)(2,1)}), bf16[8,672,128]{2,1,0:T(8,128)(2,1)S(1)}, u32[]{:S(2)}, u32[]{:S(2)}) %all-to-all-start.8) | async-done | bytes 1376288 | tf_op jit(solution)/shard_map/all_to_all | solution.py:23
  291.7 0.8 fusion.5
  292.5 6.1 %all-to-all-start.9 = ((bf16[64,24,128]{2,1,0:T(8,128)(2,1)}), bf16[64,24,128]{2,1,0:T(8,128)(2,1)S(1)}, u32[]{:S(2)}, u32[]{:S(2)}) async-start(bf16[64,24,128]{2,1,0:T(8,128)(2,1)} %fusion.5), calls=%async_computation.9 | async-start | bytes 786432 | tf_op jit(solution)/shard_map/all_to_all | solution.py:23
  298.8 28.6 %all-to-all-done.9 = bf16[64,24,128]{2,1,0:T(8,128)(2,1)S(1)} async-done(((bf16[64,24,128]{2,1,0:T(8,128)(2,1)}), bf16[64,24,128]{2,1,0:T(8,128)(2,1)S(1)}, u32[]{:S(2)}, u32[]{:S(2)}) %all-to-all-start.9) | async-done | bytes 393248 | tf_op jit(solution)/shard_map/all_to_all | solution.py:23
  328.2 0.7 broadcast_in_dim.82
  329.0 4.6 %all-to-all-start.10 = ((bf16[64,16,128]{2,1,0:T(8,128)(2,1)}), bf16[64,16,128]{2,1,0:T(8,128)(2,1)S(1)}, u32[]{:S(2)}, u32[]{:S(2)}) async-start(bf16[64,16,128]{2,1,0:T(8,128)(2,1)} %broadcast_in_dim.82), calls=%async_computation.10 | async-start | bytes 524288 | tf_op jit(solution)/shard_map/all_to_all | solution.py:23
  333.6 23.7 %all-to-all-done.10 = bf16[64,16,128]{2,1,0:T(8,128)(2,1)S(1)} async-done(((bf16[64,16,128]{2,1,0:T(8,128)(2,1)}), bf16[64,16,128]{2,1,0:T(8,128)(2,1)S(1)}, u32[]{:S(2)}, u32[]{:S(2)}) %all-to-all-start.10) | async-done | bytes 262176 | tf_op jit(solution)/shard_map/all_to_all | solution.py:23
  357.5 0.9 broadcast_in_dim.83
  358.4 3.5 all-to-all-start.11
  362.3 0.9 bitcast_add_fusion
  363.1 13.2 %all-to-all-done.11 = f32[8,200,128]{2,1,0:T(8,128)S(1)} async-done(((f32[8,200,128]{2,1,0:T(8,128)}), f32[8,200,128]{2,1,0:T(8,128)S(1)}, u32[]{:S(2)}, u32[]{:S(2)}) %all-to-all-start.11) | async-done | bytes 819232 | tf_op jit(solution)/shard_map/all_to_all | solution.py:23
  378.9 0.8 pad_maximum_fusion.1
  379.7 0.7 pad_maximum_fusion.4
  (108 shorter events, 12.5 us)
Async XLA Ops:
  1.7 25.5 %copy-start.3 = (bf16[1,512,128]{2,1,0:T(8,128)(2,1)S(1)}, bf16[1,512,128]{2,1,0:T(8,128)(2,1)}, u32[]{:S(2)}) copy-start(bf16[1,512,128]{2,1,0:T(8,128)(2,1)} %param.9) | copy-start | bytes 393220
  3.7 23.5 %copy-start.4 = (bf16[1,512,128]{2,1,0:T(8,128)(2,1)S(1)}, bf16[1,512,128]{2,1,0:T(8,128)(2,1)}, u32[]{:S(2)}) copy-start(bf16[1,512,128]{2,1,0:T(8,128)(2,1)} %param.10) | copy-start | bytes 393220
  7.4 48.6 %all-to-all-start.1 = ((bf16[64,24,128]{2,1,0:T(8,128)(2,1)}), bf16[64,24,128]{2,1,0:T(8,128)(2,1)S(1)}, u32[]{:S(2)}, u32[]{:S(2)}) async-start(bf16[64,24,128]{2,1,0:T(8,128)(2,1)} %pad_maximum_fusion.2), calls=%async_computation.1 | async-start | bytes 786432 | tf_op jit(solution)/shard_map/all_to_all | solution.py:23
  28.6 31.6 %copy-start.10 = (s32[512]{0:T(512)S(1)}, s32[512]{0:T(512)}, u32[]{:S(2)}) copy-start(s32[512]{0:T(512)} %param.11) | copy-start | bytes 6148
  28.6 32.4 %copy-start.5 = (bf16[2,4,128,128]{3,2,1,0:T(8,128)(2,1)S(1)}, bf16[2,4,128,128]{3,2,1,0:T(8,128)(2,1)}, u32[]{:S(2)}) copy-start(bf16[2,4,128,128]{3,2,1,0:T(8,128)(2,1)} %param.14) | copy-start | bytes 786436
  28.6 33.7 %copy-start.11 = (f32[2,128]{1,0:T(2,128)S(1)}, f32[2,128]{1,0:T(2,128)}, u32[]{:S(2)}) copy-start(f32[2,128]{1,0:T(2,128)} %param.15) | copy-start | bytes 3076
  28.6 34.2 %copy-start.8 = (bf16[2,128,128]{2,1,0:T(8,128)(2,1)S(1)}, bf16[2,128,128]{2,1,0:T(8,128)(2,1)}, u32[]{:S(2)}) copy-start(bf16[2,128,128]{2,1,0:T(8,128)(2,1)} %param.16) | copy-start | bytes 196612
  56.0 24.6 %all-to-all-start = ((bf16[8,640,128]{2,1,0:T(8,128)(2,1)}), bf16[8,640,128]{2,1,0:T(8,128)(2,1)S(1)}, u32[]{:S(2)}, u32[]{:S(2)}) async-start(bf16[8,640,128]{2,1,0:T(8,128)(2,1)} %pad_maximum_fusion), calls=%async_computation | async-start | bytes 2621440 | tf_op jit(solution)/shard_map/all_to_all | solution.py:23
  63.4 33.5 %copy-start.9 = (bf16[2,128,4]{1,2,0:T(4,128)(2,1)S(1)}, bf16[2,128,4]{1,2,0:T(4,128)(2,1)}, u32[]{:S(2)}) copy-start(bf16[2,128,4]{1,2,0:T(4,128)(2,1)} %param.17) | copy-start | bytes 6148
  80.6 1.1 copy-start
  92.3 8.6 %all-to-all-start.2 = ((bf16[8,64,128]{2,1,0:T(8,128)(2,1)}), bf16[8,64,128]{2,1,0:T(8,128)(2,1)S(1)}, u32[]{:S(2)}, u32[]{:S(2)}) async-start(bf16[8,64,128]{2,1,0:T(8,128)(2,1)} %forward_rows.1), calls=%async_computation.2 | async-start | bytes 262144 | tf_op jit(solution)/shard_map/all_to_all | solution.py:23
  138.3 19.5 %all-to-all-start.4 = ((bf16[8,8,64,128]{3,2,1,0:T(8,128)(2,1)}), bf16[8,8,64,128]{3,2,1,0:T(8,128)(2,1)S(1)}, u32[]{:S(2)}, u32[]{:S(2)}) async-start(bf16[8,8,64,128]{3,2,1,0:T(8,128)(2,1)} %broadcast_in_dim.75), calls=%async_computation.4 | async-start | bytes 2097152 | tf_op jit(solution)/shard_map/all_to_all | solution.py:23
  157.8 1.2 copy-start.1
  174.8 3.7 copy-start.7
  174.8 23.6 %all-to-all-start.5 = ((bf16[8,608,128]{2,1,0:T(8,128)(2,1)}), bf16[8,608,128]{2,1,0:T(8,128)(2,1)S(1)}, u32[]{:S(2)}, u32[]{:S(2)}) async-start(bf16[8,608,128]{2,1,0:T(8,128)(2,1)} %get-tuple-element.12), calls=%async_computation.5 | async-start | bytes 2490368 | tf_op jit(solution)/shard_map/all_to_all | solution.py:23
  198.6 43.3 %copy-start.2 = (bf16[8,64,128]{2,1,0:T(8,128)(2,1)S(1)}, bf16[8,64,128]{2,1,0:T(8,128)(2,1)}, u32[]{:S(2)}) copy-start(bf16[8,64,128]{2,1,0:T(8,128)(2,1)} %forward_rows.1) | copy-start | bytes 393220
  238.5 8.6 %all-to-all-start.7 = ((bf16[8,64,128]{2,1,0:T(8,128)(2,1)}), bf16[8,64,128]{2,1,0:T(8,128)(2,1)S(1)}, u32[]{:S(2)}, u32[]{:S(2)}) async-start(bf16[8,64,128]{2,1,0:T(8,128)(2,1)} %bitcast.152), calls=%async_computation.7 | async-start | bytes 262144 | tf_op jit(solution)/shard_map/all_to_all | solution.py:23
  266.0 3.7 copy-start.6
  266.0 25.7 %all-to-all-start.8 = ((bf16[8,672,128]{2,1,0:T(8,128)(2,1)}), bf16[8,672,128]{2,1,0:T(8,128)(2,1)S(1)}, u32[]{:S(2)}, u32[]{:S(2)}) async-start(bf16[8,672,128]{2,1,0:T(8,128)(2,1)} %get-tuple-element.13), calls=%async_computation.8 | async-start | bytes 2752512 | tf_op jit(solution)/shard_map/all_to_all | solution.py:23
  292.5 34.9 %all-to-all-start.9 = ((bf16[64,24,128]{2,1,0:T(8,128)(2,1)}), bf16[64,24,128]{2,1,0:T(8,128)(2,1)S(1)}, u32[]{:S(2)}, u32[]{:S(2)}) async-start(bf16[64,24,128]{2,1,0:T(8,128)(2,1)} %fusion.5), calls=%async_computation.9 | async-start | bytes 786432 | tf_op jit(solution)/shard_map/all_to_all | solution.py:23
  329.0 28.3 %all-to-all-start.10 = ((bf16[64,16,128]{2,1,0:T(8,128)(2,1)}), bf16[64,16,128]{2,1,0:T(8,128)(2,1)S(1)}, u32[]{:S(2)}, u32[]{:S(2)}) async-start(bf16[64,16,128]{2,1,0:T(8,128)(2,1)} %broadcast_in_dim.82), calls=%async_computation.10 | async-start | bytes 524288 | tf_op jit(solution)/shard_map/all_to_all | solution.py:23
  358.4 17.9 %all-to-all-start.11 = ((f32[8,200,128]{2,1,0:T(8,128)}), f32[8,200,128]{2,1,0:T(8,128)S(1)}, u32[]{:S(2)}, u32[]{:S(2)}) async-start(f32[8,200,128]{2,1,0:T(8,128)} %broadcast_in_dim.83), calls=%async_computation.11 | async-start | bytes 1638400 | tf_op jit(solution)/shard_map/all_to_all | solution.py:23

commit v3 on v2

--- a/solution.py
+++ b/solution.py
@@ -9,6 +9,7 @@
 from jax.sharding import Mesh
 from jax.sharding import PartitionSpec as P
 
+
 HEAD = ("head_0", "head_1")
 ROW_HEAD = ("row", "head_0", "head_1")
 
@@ -21,6 +22,47 @@
 
 def exchanged(parts, axis):
     return lax.all_to_all(parts, axis, split_axis=0, concat_axis=0, tiled=True)
+
+
+def shifted_exchange(parts):
+    count = parts.shape[0]
+    pieces = [parts[0]]
+    for shift in range(1, count):
+        pairs = [(at, (at + shift) % count) for at in range(count)]
+        pieces.append(lax.ppermute(parts[shift], HEAD, pairs))
+    return pieces
+
+
+def rolled(x, by):
+    return lax.dynamic_slice_in_dim(jnp.concatenate([x, x]), by, x.shape[0], axis=0)
+
+
+def place_kernel(own_ref, *refs):
+    count = len(refs) - 1
+    for shift in range(count):
+        place = lax.rem(own_ref[0] + (count - shift), count)
+        refs[-1][pl.ds(place, 1)] = refs[shift][...][None]
+
+
+def placed(own_class, pieces):
+    return pl.pallas_call(
+        place_kernel,
+        in_specs=[
+            pl.BlockSpec(memory_space=pltpu.SMEM),
+            *[pl.BlockSpec(memory_space=pltpu.VMEM) for _ in pieces],
+        ],
+        out_specs=pl.BlockSpec(memory_space=pltpu.VMEM),
+        out_shape=jax.ShapeDtypeStruct((len(pieces), *pieces[0].shape), pieces[0].dtype),
+        interpret=INTERPRET,
+        name="place_pieces",
+    )(own_class, *pieces)
+
+
+def summed(pieces):
+    total = pieces[0].astype(jnp.float32)
+    for piece in pieces[1:]:
+        total = total + piece.astype(jnp.float32)
+    return total
 
 
 def to_all(x, axis):
@@ -132,7 +174,9 @@
             full_bias[...] = bias_ref[...].astype(jnp.float32).T + mask_ref[...]
         else:
             full_bias[...] = split_bias(bias_ref[...], mask_ref[...], heads)
-            sent_ref[:, positions : positions + groups] = ride_ref[...]
+            for peer in range(classes):
+                slot = lax.rem(peer + classes - own_class, classes)
+                sent_ref[pl.ds(slot, 1), positions : positions + groups] = ride_ref[peer][None]
         bias_sum[...] = jnp.zeros(bias_sum.shape, jnp.float32)
         weight_sum[...] = jnp.zeros(weight_sum.shape, jnp.float32)
         weight_sum[5 * channels : 5 * channels + 8] = extra_ref[...]
@@ -170,9 +214,12 @@
     partial = share[...].astype(jnp.bfloat16)
     if second:
         place = pl.ds(pl.multiple_of(step * groups, groups), groups)
-        sent_ref[:, place] = partial.reshape(classes, groups, channels)
+        for peer in range(classes):
+            slot = lax.rem(peer + classes - own_class, classes)
+            sent_ref[pl.ds(slot, 1), place] = partial[peer * groups : (peer + 1) * groups][None]
     else:
-        sent_ref[pl.ds(step, 1), :positions] = partial[None]
+        slot = lax.rem(step + classes - own_class, classes)
+        sent_ref[pl.ds(slot, 1), :positions] = partial[None]
     pair_sums = matmul(x, grad_pairs, 0, 0)
     weight_sum[:channels] += matmul(xq, grad_queries, 0, 0)
     weight_sum[channels : 2 * channels] += pair_sums[:, :inner]
@@ -186,9 +233,10 @@
     @pl.when(step == pl.num_programs(0) - 1)
     def _():
         for peer in range(classes):
-            sent_ref[peer, share_start : share_start + share_rows] = weight_sum[
+            slot = lax.rem(peer + classes - own_class, classes)
+            sent_ref[pl.ds(slot, 1), share_start : share_start + share_rows] = weight_sum[
                 peer * share_rows : (peer + 1) * share_rows
-            ].astype(jnp.bfloat16)
+            ].astype(jnp.bfloat16)[None]
         if second:
             bias_out_ref[...] = bias_sum[...].T.astype(jnp.bfloat16)
         else:
@@ -233,7 +281,6 @@
                   share_rows):
     second = ride is None
     classes, groups, channels = grad.shape
-    inner = params[2].shape[2]
     if second:
         ride = jnp.zeros((8, LANES), jnp.bfloat16)
         rows_spec = pl.BlockSpec((classes, 1, groups, channels), lambda step: (0, step, 0, 0))
@@ -324,14 +371,11 @@
         "nc,ch->hn", normal_flat, bias_weights[0], preferred_element_type=jnp.float32
     ).astype(half)
     own_cotangent = cotangent.reshape(groups, classes, channels)
-    arrived = exchanged(
-        jnp.concatenate(
-            [to_all(normal_flat, HEAD), own_pair, own_cotangent.transpose(1, 0, 2)], axis=1
-        ),
-        HEAD,
-    )
-    first_rows = arrived
-    cotangent_query = arrived[:, positions + groups :]
+    class_parts = jnp.concatenate([own_pair, own_cotangent.transpose(1, 0, 2)], axis=1)
+    class_parts = rolled(class_parts, own_class[0])
+    pieces = shifted_exchange(jnp.concatenate([to_all(normal_flat, HEAD), class_parts], axis=1))
+    first_rows = placed(own_class, pieces)
+    cotangent_query = first_rows[:, positions + groups :]
     arrived = exchanged(
         jnp.concatenate(
             [
@@ -388,36 +432,27 @@
         share_rows,
     )
 
-    def group_shares_of(arrived_shares):
-        summed = jnp.sum(arrived_shares.astype(jnp.float32), axis=0)
-        summed = padded_rows(summed, groups * group_rows).astype(half)
-        return padded_rows(summed.reshape(groups, group_rows, LANES), rounded_up(group_rows, 8))
-
-    arrived = exchanged(sent, HEAD)
-    grad_flipped = jnp.sum(arrived[:, :positions].astype(jnp.float32), axis=0).astype(half)
+    def group_shares_of(shares):
+        padded = padded_rows(shares, groups * group_rows).astype(half)
+        return padded.reshape(groups, group_rows, LANES)
+
+    pieces = shifted_exchange(sent)
     bias_parts = (
         bias_parts.reshape(classes, groups, head_total * groups)
         .transpose(1, 0, 2)
         .reshape(groups, bias_rows, LANES)
     )
+    bias_arrived = exchanged(bias_parts, "row")
+    total = summed(pieces)
+    grad_flipped = total[:positions].astype(half)
+    second_shares = total[positions:]
     arrived = exchanged(
-        jnp.concatenate(
-            [
-                bias_parts,
-                grad_flipped.reshape(classes, groups, channels).transpose(1, 0, 2),
-                group_shares_of(arrived[:, positions:]),
-            ],
-            axis=1,
-        ),
+        grad_flipped.reshape(classes, groups, channels).transpose(1, 0, 2),
         "row",
     )
-    summed = jnp.sum(arrived[:, :bias_rows].astype(jnp.float32), axis=0)
-    second_bias_half = summed.reshape(classes, head_total, groups).astype(half)
-    second_own = jnp.sum(
-        arrived[:, bias_rows + classes : bias_rows + classes + group_rows].astype(jnp.float32),
-        axis=0,
-    )
-    grad_query = exchanged(arrived[:, bias_rows : bias_rows + classes].transpose(1, 0, 2), HEAD)
+    bias_total = jnp.sum(bias_arrived.astype(jnp.float32), axis=0)
+    second_bias_half = bias_total.reshape(classes, head_total, groups).astype(half)
+    grad_query = exchanged(arrived.transpose(1, 0, 2), HEAD)
     grad_normal = grad_query.astype(jnp.float32) + jnp.einsum(
         "ahb,ch->abc", second_bias_half, bias_weights[1], preferred_element_type=jnp.float32
     )
@@ -450,25 +485,21 @@
         positions,
         share_rows,
     )
-    arrived = exchanged(sent, HEAD)
-    grad_normal = jnp.sum(arrived[:, :positions].astype(jnp.float32), axis=0)
-    end_own = arrived[:, positions : positions + groups]
-    shares = arrived[:, positions + groups :]
-    arrived = exchanged(
-        jnp.concatenate(
-            [
-                bias_parts.reshape(groups, bias_rows, LANES),
-                group_shares_of(shares),
-            ],
-            axis=1,
-        ),
-        "row",
-    )
-    summed = jnp.sum(arrived[:, :bias_rows].astype(jnp.float32), axis=0)
-    bias_half = summed.reshape(head_total, positions).astype(half)
-    first_own = jnp.sum(
-        arrived[:, bias_rows : bias_rows + group_rows].astype(jnp.float32), axis=0
-    )
+    pieces = shifted_exchange(sent)
+    bias_arrived = exchanged(bias_parts.reshape(groups, bias_rows, LANES), "row")
+    grad_normal = summed([piece[:positions] for piece in pieces])
+    end_own = rolled(
+        jnp.stack([piece[positions : positions + groups] for piece in pieces[::-1]]),
+        classes - 1 - own_class[0],
+    )
+    first_shares = summed([piece[positions + groups :] for piece in pieces])
+    group_shares = jnp.concatenate(
+        [group_shares_of(first_shares), group_shares_of(second_shares)], axis=1
+    )
+    shares_arrived = exchanged(padded_rows(group_shares, rounded_up(2 * group_rows, 8)), "row")
+    shares_total = jnp.sum(shares_arrived[:, : 2 * group_rows].astype(jnp.float32), axis=0)
+    bias_total = jnp.sum(bias_arrived.astype(jnp.float32), axis=0)
+    bias_half = bias_total.reshape(head_total, positions).astype(half)
     grad_normal = grad_normal + jnp.einsum(
         "hn,ch->nc", bias_half, bias_weights[0], preferred_element_type=jnp.float32
     )
@@ -488,22 +519,25 @@
     )
 
     small_rows = first_small.shape[0]
-    tail = jnp.concatenate([first_own, second_own, first_small], axis=0).astype(half)
+    tail = jnp.concatenate([shares_total, first_small], axis=0).astype(half)
     tail = padded_rows(tail, rounded_up(tail.shape[0], 8))
-    arrived = exchanged(to_all(tail, "row"), "row").astype(jnp.float32)
+    arrived = exchanged(to_all(tail, "row"), "row")
     whole_rows = groups * group_rows
     shared = jnp.concatenate(
         [
             arrived[:, :group_rows].reshape(whole_rows, LANES)[:share_rows],
             arrived[:, group_rows : 2 * group_rows].reshape(whole_rows, LANES)[:share_rows],
             padded_rows(
-                jnp.sum(arrived[:, 2 * group_rows : 2 * group_rows + small_rows], axis=0),
+                jnp.sum(
+                    arrived[:, 2 * group_rows : 2 * group_rows + small_rows].astype(jnp.float32),
+                    axis=0,
+                ).astype(half),
                 rounded_up(small_rows, 8),
             ),
         ],
         axis=0,
     )
-    arrived = exchanged(to_all(shared, HEAD), HEAD)
+    arrived = exchanged(to_all(shared, HEAD), HEAD).astype(jnp.float32)
     first_whole = arrived[:, :share_rows].reshape(-1, LANES)
     second_whole = arrived[:, share_rows : 2 * share_rows].reshape(-1, LANES)
     first_small = jnp.sum(arrived[:, 2 * share_rows : 2 * share_rows + small_rows], axis=0)
@@ -530,4 +564,5 @@
     finer = Mesh(mesh.devices.reshape(mesh.shape["row"], 4, 2), ("row", "head_0", "head_1"))
     in_specs = (P(ROW_HEAD, None, None), P(ROW_HEAD, None, None), P(), P(), P(), P(), P(), P(), P())
     out_specs = (P(ROW_HEAD, None, None), P(), P(), P(), P(), P(), P())
+
     return jax.shard_map(local, mesh=finer, in_specs=in_specs, out_specs=out_specs, check_vma=False)

time: 382 us -> 417 us (1.092)
  starting transfers between devices: 55.9 us -> 128 us
  blocking collectives: 74.3 us -> 48.1 us
  waiting for transfers between devices: 172 us -> 150 us
  local copies, waits for them, and re-layouts: 12.9 us -> 18.8 us
    ppermute x0 -> x21, starting transfers between devices: none -> 65.7 us  [shifted_exchange(): pieces.append(lax.ppermute(parts[shift], HEAD, pairs))]
    all_to_all x10, waiting for transfers between devices: 172 us -> 134 us  [exchanged(): return lax.all_to_all(parts, axis, split_axis=0, concat_axis=0, tiled=True)]
    all_to_all x2 -> x1, blocking collectives: 74.3 us -> 48.1 us  [exchanged(): return lax.all_to_all(parts, axis, split_axis=0, concat_axis=0, tiled=True)]
    ppermute x0 -> x21, waiting for transfers between devices: none -> 15.7 us  [shifted_exchange(): pieces.append(lax.ppermute(parts[shift], HEAD, pairs))]
    all_to_all x10, starting transfers between devices: 55.9 us -> 62.5 us  [exchanged(): return lax.all_to_all(parts, axis, split_axis=0, concat_axis=0, tiled=True)]
  transfers between devices with their start and end apart: 10 -> 31, of which waited for: 10 -> 15; matrix products, arithmetic and copies ran while one was open for 3% -> 4% of each run, Pallas kernels for 0% -> 1%
where the time goes in v3:
time: 417 us; the launch traced here: 415 us
  waiting for transfers between devices  150 us (36%)
  starting transfers between devices  128 us (31%)
  blocking collectives  48.1 us (12%)
  Pallas kernels  43.7 us (10%)
  other arithmetic  20.5 us (5%)
  local copies, waits for them, and re-layouts  18.8 us (5%)
  matrix products  4.3 us (1%)
    all_to_all x10, waiting for transfers between devices, exchanged(): return lax.all_to_all(parts, axis, split_axis=0, concat_axis=0, tiled=True)  134 us
    ppermute x21, starting transfers between devices, shifted_exchange(): pieces.append(lax.ppermute(parts[shift], HEAD, pairs))  65.7 us
    all_to_all x10, starting transfers between devices, exchanged(): return lax.all_to_all(parts, axis, split_axis=0, concat_axis=0, tiled=True)  62.5 us
    all_to_all x1, blocking collectives, exchanged(): return lax.all_to_all(parts, axis, split_axis=0, concat_axis=0, tiled=True)  48.1 us
    pallas_call x2, Pallas kernels, backward_call(): pl.pallas_call(functools.partial(backward_kernel, heads, positions, secon...  31.6 us
    ppermute x21, waiting for transfers between devices, shifted_exchange(): pieces.append(lax.ppermute(parts[shift], HEAD, pairs))  15.7 us
    pallas_call x1, Pallas kernels, forward_call(): pl.pallas_call(functools.partial(forward_kernel, heads, positions), grid=...  9.59 us
  transfers between devices with their start and end apart: 31, of which 15 were waited for; matrix products, arithmetic and copies ran while one was open for 4% of the time, Pallas kernels for 1%

profile of v3, /device:TPU:1, one launch (start us, length us, event | category | flops | bytes accessed | tf_op | source)
XLA Modules:
  0.0 415.2 jit_solution(455302076999136642)
XLA Ops:
  6.6 19.8 %all-to-all-start = ((bf16[64,24,128]{2,1,0:T(8,128)(2,1)}), bf16[64,24,128]{2,1,0:T(8,128)(2,1)S(1)}, u32[]{:S(2)}, u32[]{:S(2)}) async-start(bf16[64,24,128]{2,1,0:T(8,128)(2,1)} %pad_maximum_fusion.1), calls=%async_computation | async-start | bytes 786432 | tf_op jit(solution)/shard_map/all_to_all | solution.py:24
  28.3 4.5 %collective-permute-start.6 = (bf16[640,128]{1,0:T(8,128)(2,1)S(1)}, bf16[640,128]{1,0:T(8,128)(2,1)S(1)}, u32[]{:S(2)}, u32[]{:S(2)}) collective-permute-start(bf16[640,128]{1,0:T(8,128)(2,1)S(1)} %get-tuple-element.32), channel_id=1, source_target_pairs={{0,7},{1,0},{2,1},{3,2},{4,3},{5,4},{6,5},{7,6},{8,15},{9,8},{10,9... | collective-permute-start | bytes 491528 | tf_op jit(solution)/shard_map/ppermute | solution.py:32
  34.7 2.0 collective-permute-start.1
  36.7 4.1 collective-permute-start.2
  40.8 4.4 %collective-permute-start.3 = (bf16[640,128]{1,0:T(8,128)(2,1)S(1)}, bf16[640,128]{1,0:T(8,128)(2,1)S(1)}, u32[]{:S(2)}, u32[]{:S(2)}) collective-permute-start(bf16[640,128]{1,0:T(8,128)(2,1)S(1)} %get-tuple-element.37), channel_id=1, source_target_pairs={{0,4},{1,5},{2,6},{3,7},{4,0},{5,1},{6,2},{7,3},{8,12},{9,13},{10,... | collective-permute-start | bytes 491528 | tf_op jit(solution)/shard_map/ppermute | solution.py:32
  46.5 3.5 collective-permute-start.4
  50.1 3.1 collective-permute-start.5
  55.2 2.6 collective-permute-done.5.refs_6_
  58.5 2.5 place_pieces.1.rows_ref
  61.8 9.6 %forward_rows.1 = bf16[8,64,128]{2,1,0:T(8,128)(2,1)} custom-call(s32[1]{0:T(128)} %bitcast.own_ref.class_ref, bf16[8,640,128]{2,1,0:T(8,128)(2,1)} %place_pieces.1.rows_ref, bf16[64,2048]{1,0:T(8,128)(2,1)} %bitcast.254, f32[1,512]{1,0:T(1,128)} %reshape.199.mask_ref, bf16[128,128]{1,0:T(8,128)(2,1)} %get-tuple-element.60.wq_ref, ...), custom_call_target="tpu_custom_call" | custom-call | tf_op jit(solution)/shard_map/forward_rows/pallas_call | solution.py:263
  72.5 3.7 all-to-all-start.1
  78.7 2.7 all-to-all-done.1
  81.6 48.1 %all_to_all.55 = bf16[64,24,128]{2,1,0:T(8,128)(2,1)S(1)} all-to-all(bf16[64,24,128]{2,1,0:T(8,128)(2,1)S(1)} %pad_maximum_fusion.2), channel_id=1, replica_groups=mesh['row'=64,'head_0'=4,'head_1'=2] {'row'}, dimensions={0} | all-to-all | bytes 786432 | tf_op jit(solution)/shard_map/all_to_all | solution.py:24
  131.6 3.6 all-to-all-start.3
  137.3 13.7 %all-to-all-done.3.rows_ref = bf16[8,8,64,128]{3,2,1,0:T(8,128)(2,1)S(1)} async-done(((bf16[8,8,64,128]{3,2,1,0:T(8,128)(2,1)}), bf16[8,8,64,128]{3,2,1,0:T(8,128)(2,1)S(1)}, u32[]{:S(2)}, u32[]{:S(2)}) %all-to-all-start.3) | async-done | bytes 1048608 | tf_op jit(solution)/shard_map/all_to_all | solution.py:24
  152.3 15.8 %backward_second.1 = (bf16[8,608,128]{2,1,0:T(8,128)(2,1)}, bf16[512,256]{1,0:T(8,128)(2,1)}) custom-call(s32[1]{0:T(128)} %bitcast.own_ref.class_ref, bf16[8,8,64,128]{3,2,1,0:T(8,128)(2,1)} %copy-done, bf16[512,256]{1,0:T(8,128)(2,1)} %bitcast.276, f32[1,512]{1,0:T(1,128)} %reshape.199.mask_ref, bf16[8,64,128]{2,1,0:T(8,128)(2,1)} %bitcast.283, ...), custom_call_target="tpu_custom_call" | custom-call | tf_op jit(solution)/shard_map/backward_second/pallas_call | solution.py:296
  169.5 3.2 collective-permute-start.7
  172.7 4.3 %collective-permute-start.13 = (bf16[608,128]{1,0:T(8,128)(2,1)S(1)}, bf16[608,128]{1,0:T(8,128)(2,1)S(1)}, u32[]{:S(2)}, u32[]{:S(2)}) collective-permute-start(bf16[608,128]{1,0:T(8,128)(2,1)S(1)} %get-tuple-element.41), channel_id=1, source_target_pairs={{0,7},{1,0},{2,1},{3,2},{4,3},{5,4},{6,5},{7,6},{8,15},{9,8},{10,9... | collective-permute-start | bytes 466952 | tf_op jit(solution)/shard_map/ppermute | solution.py:32
  179.0 2.5 collective-permute-start.11
  181.4 4.3 %collective-permute-start.10 = (bf16[608,128]{1,0:T(8,128)(2,1)S(1)}, bf16[608,128]{1,0:T(8,128)(2,1)S(1)}, u32[]{:S(2)}, u32[]{:S(2)}) collective-permute-start(bf16[608,128]{1,0:T(8,128)(2,1)S(1)} %get-tuple-element.44), channel_id=1, source_target_pairs={{0,4},{1,5},{2,6},{3,7},{4,0},{5,1},{6,2},{7,3},{8,12},{9,13},{10,... | collective-permute-start | bytes 466952 | tf_op jit(solution)/shard_map/ppermute | solution.py:32
  187.7 2.8 collective-permute-start.8
  190.9 3.7 collective-permute-done.9
  194.5 3.5 collective-permute-done.8
  199.9 7.7 %all-to-all-start.4 = ((bf16[64,8,128]{2,1,0:T(8,128)(2,1)}), bf16[64,8,128]{2,1,0:T(8,128)(2,1)S(1)}, u32[]{:S(2)}, u32[]{:S(2)}) async-start(bf16[64,8,128]{2,1,0:T(8,128)(2,1)} %bitcast.251), calls=%async_computation.4 | async-start | bytes 262144 | tf_op jit(solution)/shard_map/all_to_all | solution.py:24
  208.5 17.6 %all-to-all-done.4 = bf16[64,8,128]{2,1,0:T(8,128)(2,1)S(1)} async-done(((bf16[64,8,128]{2,1,0:T(8,128)(2,1)}), bf16[64,8,128]{2,1,0:T(8,128)(2,1)S(1)}, u32[]{:S(2)}, u32[]{:S(2)}) %all-to-all-start.4) | async-done | bytes 131104 | tf_op jit(solution)/shard_map/all_to_all | solution.py:24
  226.2 4.6 %all-to-all-start.6 = ((bf16[64,16,128]{2,1,0:T(8,128)(2,1)}), bf16[64,16,128]{2,1,0:T(8,128)(2,1)S(1)}, u32[]{:S(2)}, u32[]{:S(2)}) async-start(bf16[64,16,128]{2,1,0:T(8,128)(2,1)} %reshape.204), calls=%async_computation.6 | async-start | bytes 524288 | tf_op jit(solution)/shard_map/all_to_all | solution.py:24
  231.5 23.2 %all-to-all-done.6 = bf16[64,16,128]{2,1,0:T(8,128)(2,1)S(1)} async-done(((bf16[64,16,128]{2,1,0:T(8,128)(2,1)}), bf16[64,16,128]{2,1,0:T(8,128)(2,1)S(1)}, u32[]{:S(2)}, u32[]{:S(2)}) %all-to-all-start.6) | async-done | bytes 262176 | tf_op jit(solution)/shard_map/all_to_all | solution.py:24
  254.7 3.4 all-to-all-start.5
  258.5 5.4 %all-to-all-done.5 = bf16[8,64,128]{2,1,0:T(8,128)(2,1)S(1)} async-done(((bf16[8,64,128]{2,1,0:T(8,128)(2,1)}), bf16[8,64,128]{2,1,0:T(8,128)(2,1)S(1)}, u32[]{:S(2)}, u32[]{:S(2)}) %all-to-all-start.5) | async-done | bytes 131104 | tf_op jit(solution)/shard_map/all_to_all | solution.py:24
  265.0 1.9 add_convert_fusion
  266.9 15.8 %backward_first.1 = (bf16[8,672,128]{2,1,0:T(8,128)(2,1)}, bf16[64,2048]{1,0:T(8,128)(2,1)}) custom-call(s32[1]{0:T(128)} %bitcast.own_ref.class_ref, bf16[8,640,128]{2,1,0:T(8,128)(2,1)} %place_pieces.1.rows_ref, bf16[64,2048]{1,0:T(8,128)(2,1)} %bitcast.255, f32[1,512]{1,0:T(1,128)} %reshape.199.mask_ref, bf16[8,64,128]{2,1,0:T(8,128)(2,1)} %get-tuple-element.23.grad_ref, ...), custom_call_target="tpu_custom_call" | custom-call | tf_op jit(solution)/shard_map/backward_first/pallas_call | solution.py:296
  284.2 2.8 collective-permute-start.20
  287.0 2.2 collective-permute-start.19
  289.2 3.0 collective-permute-start.18
  292.2 4.4 %collective-permute-start.17 = (bf16[672,128]{1,0:T(8,128)(2,1)S(1)}, bf16[672,128]{1,0:T(8,128)(2,1)S(1)}, u32[]{:S(2)}, u32[]{:S(2)}) collective-permute-start(bf16[672,128]{1,0:T(8,128)(2,1)S(1)} %get-tuple-element.28), channel_id=1, source_target_pairs={{0,4},{1,5},{2,6},{3,7},{4,0},{5,1},{6,2},{7,3},{8,12},{9,13},{10,... | collective-permute-start | bytes 516104 | tf_op jit(solution)/shard_map/ppermute | solution.py:32
  296.6 3.9 collective-permute-start.16
  300.6 2.6 collective-permute-start.15
  303.2 2.4 collective-permute-start.14
  306.4 2.4 collective-permute-done.15
  308.9 3.0 collective-permute-done.14
  313.4 5.6 %all-to-all-start.8 = ((bf16[64,8,128]{2,1,0:T(8,128)(2,1)}), bf16[64,8,128]{2,1,0:T(8,128)(2,1)S(1)}, u32[]{:S(2)}, u32[]{:S(2)}) async-start(bf16[64,8,128]{2,1,0:T(8,128)(2,1)} %fusion.63), calls=%async_computation.8 | async-start | bytes 262144 | tf_op jit(solution)/shard_map/all_to_all | solution.py:24
  319.8 17.9 %all-to-all-done.8 = bf16[64,8,128]{2,1,0:T(8,128)(2,1)S(1)} async-done(((bf16[64,8,128]{2,1,0:T(8,128)(2,1)}), bf16[64,8,128]{2,1,0:T(8,128)(2,1)S(1)}, u32[]{:S(2)}, u32[]{:S(2)}) %all-to-all-start.8) | async-done | bytes 131104 | tf_op jit(solution)/shard_map/all_to_all | solution.py:24
  337.7 4.5 %all-to-all-start.7 = ((bf16[64,16,128]{2,1,0:T(8,128)(2,1)}), bf16[64,16,128]{2,1,0:T(8,128)(2,1)S(1)}, u32[]{:S(2)}, u32[]{:S(2)}) async-start(bf16[64,16,128]{2,1,0:T(8,128)(2,1)} %bitcast.99), calls=%async_computation.7 | async-start | bytes 524288 | tf_op jit(solution)/shard_map/all_to_all | solution.py:24
  342.3 23.7 %all-to-all-done.7 = bf16[64,16,128]{2,1,0:T(8,128)(2,1)S(1)} async-done(((bf16[64,16,128]{2,1,0:T(8,128)(2,1)}), bf16[64,16,128]{2,1,0:T(8,128)(2,1)S(1)}, u32[]{:S(2)}, u32[]{:S(2)}) %all-to-all-start.7) | async-done | bytes 262176 | tf_op jit(solution)/shard_map/all_to_all | solution.py:24
  368.4 4.2 %all-to-all-start.9 = ((bf16[64,16,128]{2,1,0:T(8,128)(2,1)}), bf16[64,16,128]{2,1,0:T(8,128)(2,1)S(1)}, u32[]{:S(2)}, u32[]{:S(2)}) async-start(bf16[64,16,128]{2,1,0:T(8,128)(2,1)} %broadcast_in_dim.82), calls=%async_computation.9 | async-start | bytes 524288 | tf_op jit(solution)/shard_map/all_to_all | solution.py:24
  373.6 22.5 %all-to-all-done.9 = bf16[64,16,128]{2,1,0:T(8,128)(2,1)S(1)} async-done(((bf16[64,16,128]{2,1,0:T(8,128)(2,1)}), bf16[64,16,128]{2,1,0:T(8,128)(2,1)S(1)}, u32[]{:S(2)}, u32[]{:S(2)}) %all-to-all-start.9) | async-done | bytes 262176 | tf_op jit(solution)/shard_map/all_to_all | solution.py:24
  397.1 5.6 %all-to-all-start.10 = ((bf16[8,200,128]{2,1,0:T(8,128)(2,1)}), bf16[8,200,128]{2,1,0:T(8,128)(2,1)S(1)}, u32[]{:S(2)}, u32[]{:S(2)}) async-start(bf16[8,200,128]{2,1,0:T(8,128)(2,1)} %broadcast_in_dim.83), calls=%async_computation.10 | async-start | bytes 819200 | tf_op jit(solution)/shard_map/all_to_all | solution.py:24
  403.6 7.5 %all-to-all-done.10 = bf16[8,200,128]{2,1,0:T(8,128)(2,1)S(1)} async-done(((bf16[8,200,128]{2,1,0:T(8,128)(2,1)}), bf16[8,200,128]{2,1,0:T(8,128)(2,1)S(1)}, u32[]{:S(2)}, u32[]{:S(2)}) %all-to-all-start.10) | async-done | bytes 409632 | tf_op jit(solution)/shard_map/all_to_all | solution.py:24
  (177 shorter events, 47.8 us)
Async XLA Ops:
  0.6 5.1 %copy-start.3 = (bf16[1,512,128]{2,1,0:T(8,128)(2,1)S(1)}, bf16[1,512,128]{2,1,0:T(8,128)(2,1)}, u32[]{:S(2)}) copy-start(bf16[1,512,128]{2,1,0:T(8,128)(2,1)} %param.10) | copy-start | bytes 393220
  1.7 24.6 %copy-start.2 = (bf16[1,512,128]{2,1,0:T(8,128)(2,1)S(1)}, bf16[1,512,128]{2,1,0:T(8,128)(2,1)}, u32[]{:S(2)}) copy-start(bf16[1,512,128]{2,1,0:T(8,128)(2,1)} %param.9) | copy-start | bytes 393220
  6.6 54.5 %all-to-all-start = ((bf16[64,24,128]{2,1,0:T(8,128)(2,1)}), bf16[64,24,128]{2,1,0:T(8,128)(2,1)S(1)}, u32[]{:S(2)}, u32[]{:S(2)}) async-start(bf16[64,24,128]{2,1,0:T(8,128)(2,1)} %pad_maximum_fusion.1), calls=%async_computation | async-start | bytes 786432 | tf_op jit(solution)/shard_map/all_to_all | solution.py:24
  27.5 17.7 %copy-start.14 = (bf16[2,128,128]{2,1,0:T(8,128)(2,1)S(1)}, bf16[2,128,128]{2,1,0:T(8,128)(2,1)}, u32[]{:S(2)}) copy-start(bf16[2,128,128]{2,1,0:T(8,128)(2,1)} %param.16) | copy-start | bytes 196612
  27.5 18.4 %copy-start.4 = (bf16[2,4,128,128]{3,2,1,0:T(8,128)(2,1)S(1)}, bf16[2,4,128,128]{3,2,1,0:T(8,128)(2,1)}, u32[]{:S(2)}) copy-start(bf16[2,4,128,128]{3,2,1,0:T(8,128)(2,1)} %param.14) | copy-start | bytes 786436
  27.5 19.0 %copy-start.15 = (s32[512]{0:T(512)S(1)}, s32[512]{0:T(512)}, u32[]{:S(2)}) copy-start(s32[512]{0:T(512)} %param.11) | copy-start | bytes 6148
  27.5 25.7 %copy-start.16 = (f32[2,128]{1,0:T(2,128)S(1)}, f32[2,128]{1,0:T(2,128)}, u32[]{:S(2)}) copy-start(f32[2,128]{1,0:T(2,128)} %param.15) | copy-start | bytes 3076
  28.3 18.2 %collective-permute-start.6 = (bf16[640,128]{1,0:T(8,128)(2,1)S(1)}, bf16[640,128]{1,0:T(8,128)(2,1)S(1)}, u32[]{:S(2)}, u32[]{:S(2)}) collective-permute-start(bf16[640,128]{1,0:T(8,128)(2,1)S(1)} %get-tuple-element.32), channel_id=1, source_target_pairs={{0,7},{1,0},{2,1},{3,2},{4,3},{5,4},{6,5},{7,6},{8,15},{9,8},{10,9... | collective-permute-start | bytes 491528 | tf_op jit(solution)/shard_map/ppermute | solution.py:32
  32.8 17.3 %collective-permute-start = (bf16[640,128]{1,0:T(8,128)(2,1)S(1)}, bf16[640,128]{1,0:T(8,128)(2,1)S(1)}, u32[]{:S(2)}, u32[]{:S(2)}) collective-permute-start(bf16[640,128]{1,0:T(8,128)(2,1)S(1)} %get-tuple-element.34), channel_id=1, source_target_pairs={{0,1},{1,2},{2,3},{3,4},{4,5},{5,6},{6,7},{7,0},{8,9},{9,10},{10,1... | collective-permute-start | bytes 491528 | tf_op jit(solution)/shard_map/ppermute | solution.py:32
  34.7 20.4 %collective-permute-start.1 = (bf16[640,128]{1,0:T(8,128)(2,1)S(1)}, bf16[640,128]{1,0:T(8,128)(2,1)S(1)}, u32[]{:S(2)}, u32[]{:S(2)}) collective-permute-start(bf16[640,128]{1,0:T(8,128)(2,1)S(1)} %get-tuple-element.35), channel_id=1, source_target_pairs={{0,2},{1,3},{2,4},{3,5},{4,6},{5,7},{6,0},{7,1},{8,10},{9,11},{10,... | collective-permute-start | bytes 491528 | tf_op jit(solution)/shard_map/ppermute | solution.py:32
  36.7 18.5 %collective-permute-start.2 = (bf16[640,128]{1,0:T(8,128)(2,1)S(1)}, bf16[640,128]{1,0:T(8,128)(2,1)S(1)}, u32[]{:S(2)}, u32[]{:S(2)}) collective-permute-start(bf16[640,128]{1,0:T(8,128)(2,1)S(1)} %get-tuple-element.36), channel_id=1, source_target_pairs={{0,3},{1,4},{2,5},{3,6},{4,7},{5,0},{6,1},{7,2},{8,11},{9,12},{10,... | collective-permute-start | bytes 491528 | tf_op jit(solution)/shard_map/ppermute | solution.py:32
  40.8 14.3 %collective-permute-start.3 = (bf16[640,128]{1,0:T(8,128)(2,1)S(1)}, bf16[640,128]{1,0:T(8,128)(2,1)S(1)}, u32[]{:S(2)}, u32[]{:S(2)}) collective-permute-start(bf16[640,128]{1,0:T(8,128)(2,1)S(1)} %get-tuple-element.37), channel_id=1, source_target_pairs={{0,4},{1,5},{2,6},{3,7},{4,0},{5,1},{6,2},{7,3},{8,12},{9,13},{10,... | collective-permute-start | bytes 491528 | tf_op jit(solution)/shard_map/ppermute | solution.py:32
  46.5 11.3 %copy-start.7 = (bf16[640,128]{1,0:T(8,128)(2,1)}, bf16[640,128]{1,0:T(8,128)(2,1)S(1)}, u32[]{:S(2)}) copy-start(bf16[640,128]{1,0:T(8,128)(2,1)S(1)} %collective-permute-done.6.refs_7_) | copy-start | bytes 491524
  46.5 8.7 %collective-permute-start.4 = (bf16[640,128]{1,0:T(8,128)(2,1)S(1)}, bf16[640,128]{1,0:T(8,128)(2,1)S(1)}, u32[]{:S(2)}, u32[]{:S(2)}) collective-permute-start(bf16[640,128]{1,0:T(8,128)(2,1)S(1)} %get-tuple-element.38), channel_id=1, source_target_pairs={{0,5},{1,6},{2,7},{3,0},{4,1},{5,2},{6,3},{7,4},{8,13},{9,14},{10,... | collective-permute-start | bytes 491528 | tf_op jit(solution)/shard_map/ppermute | solution.py:32
  50.1 7.8 %copy-start.8 = (bf16[640,128]{1,0:T(8,128)(2,1)}, bf16[640,128]{1,0:T(8,128)(2,1)S(1)}, u32[]{:S(2)}) copy-start(bf16[640,128]{1,0:T(8,128)(2,1)S(1)} %collective-permute-done.refs_1_) | copy-start | bytes 491524
  50.1 7.8 %collective-permute-start.5 = (bf16[640,128]{1,0:T(8,128)(2,1)S(1)}, bf16[640,128]{1,0:T(8,128)(2,1)S(1)}, u32[]{:S(2)}, u32[]{:S(2)}) collective-permute-start(bf16[640,128]{1,0:T(8,128)(2,1)S(1)} %get-tuple-element.39), channel_id=1, source_target_pairs={{0,6},{1,7},{2,0},{3,1},{4,2},{5,3},{6,4},{7,5},{8,14},{9,15},{10,... | collective-permute-start | bytes 491528 | tf_op jit(solution)/shard_map/ppermute | solution.py:32
  55.1 2.7 copy-start.9
  55.1 2.7 copy-start.10
  55.2 2.7 copy-start.11
  55.2 2.7 copy-start.12
  61.8 15.6 %copy-start.17 = (bf16[2,128,4]{1,2,0:T(4,128)(2,1)S(1)}, bf16[2,128,4]{1,2,0:T(4,128)(2,1)}, u32[]{:S(2)}) copy-start(bf16[2,128,4]{1,2,0:T(4,128)(2,1)} %param.17) | copy-start | bytes 6148
  72.5 9.0 %all-to-all-start.1 = ((bf16[8,64,128]{2,1,0:T(8,128)(2,1)}), bf16[8,64,128]{2,1,0:T(8,128)(2,1)S(1)}, u32[]{:S(2)}, u32[]{:S(2)}) async-start(bf16[8,64,128]{2,1,0:T(8,128)(2,1)} %forward_rows.1), calls=%async_computation.1 | async-start | bytes 262144 | tf_op jit(solution)/shard_map/all_to_all | solution.py:24
  131.6 19.5 %all-to-all-start.3 = ((bf16[8,8,64,128]{3,2,1,0:T(8,128)(2,1)}), bf16[8,8,64,128]{3,2,1,0:T(8,128)(2,1)S(1)}, u32[]{:S(2)}, u32[]{:S(2)}) async-start(bf16[8,8,64,128]{3,2,1,0:T(8,128)(2,1)} %broadcast_in_dim.75), calls=%async_computation.3 | async-start | bytes 2097152 | tf_op jit(solution)/shard_map/all_to_all | solution.py:24
  151.0 1.2 copy-start
  169.5 38.1 %copy-start.5 = (bf16[512,256]{1,0:T(8,128)(2,1)S(1)}, bf16[512,256]{1,0:T(8,128)(2,1)}, u32[]{:S(2)}) copy-start(bf16[512,256]{1,0:T(8,128)(2,1)} %get-tuple-element.12) | copy-start | bytes 786436
  169.5 16.3 %collective-permute-start.7 = (bf16[608,128]{1,0:T(8,128)(2,1)S(1)}, bf16[608,128]{1,0:T(8,128)(2,1)S(1)}, u32[]{:S(2)}, u32[]{:S(2)}) collective-permute-start(bf16[608,128]{1,0:T(8,128)(2,1)S(1)} %get-tuple-element.40), channel_id=1, source_target_pairs={{0,1},{1,2},{2,3},{3,4},{4,5},{5,6},{6,7},{7,0},{8,9},{9,10},{10,1... | collective-permute-start | bytes 466952 | tf_op jit(solution)/shard_map/ppermute | solution.py:32
  172.7 15.0 %collective-permute-start.13 = (bf16[608,128]{1,0:T(8,128)(2,1)S(1)}, bf16[608,128]{1,0:T(8,128)(2,1)S(1)}, u32[]{:S(2)}, u32[]{:S(2)}) collective-permute-start(bf16[608,128]{1,0:T(8,128)(2,1)S(1)} %get-tuple-element.41), channel_id=1, source_target_pairs={{0,7},{1,0},{2,1},{3,2},{4,3},{5,4},{6,5},{7,6},{8,15},{9,8},{10,9... | collective-permute-start | bytes 466952 | tf_op jit(solution)/shard_map/ppermute | solution.py:32
  177.0 13.4 %collective-permute-start.12 = (bf16[608,128]{1,0:T(8,128)(2,1)S(1)}, bf16[608,128]{1,0:T(8,128)(2,1)S(1)}, u32[]{:S(2)}, u32[]{:S(2)}) collective-permute-start(bf16[608,128]{1,0:T(8,128)(2,1)S(1)} %get-tuple-element.42), channel_id=1, source_target_pairs={{0,6},{1,7},{2,0},{3,1},{4,2},{5,3},{6,4},{7,5},{8,14},{9,15},{10,... | collective-permute-start | bytes 466952 | tf_op jit(solution)/shard_map/ppermute | solution.py:32
  179.0 11.5 %collective-permute-start.11 = (bf16[608,128]{1,0:T(8,128)(2,1)S(1)}, bf16[608,128]{1,0:T(8,128)(2,1)S(1)}, u32[]{:S(2)}, u32[]{:S(2)}) collective-permute-start(bf16[608,128]{1,0:T(8,128)(2,1)S(1)} %get-tuple-element.43), channel_id=1, source_target_pairs={{0,5},{1,6},{2,7},{3,0},{4,1},{5,2},{6,3},{7,4},{8,13},{9,14},{10,... | collective-permute-start | bytes 466952 | tf_op jit(solution)/shard_map/ppermute | solution.py:32
  181.4 9.4 %collective-permute-start.10 = (bf16[608,128]{1,0:T(8,128)(2,1)S(1)}, bf16[608,128]{1,0:T(8,128)(2,1)S(1)}, u32[]{:S(2)}, u32[]{:S(2)}) collective-permute-start(bf16[608,128]{1,0:T(8,128)(2,1)S(1)} %get-tuple-element.44), channel_id=1, source_target_pairs={{0,4},{1,5},{2,6},{3,7},{4,0},{5,1},{6,2},{7,3},{8,12},{9,13},{10,... | collective-permute-start | bytes 466952 | tf_op jit(solution)/shard_map/ppermute | solution.py:32
  185.8 8.8 %collective-permute-start.9 = (bf16[608,128]{1,0:T(8,128)(2,1)S(1)}, bf16[608,128]{1,0:T(8,128)(2,1)S(1)}, u32[]{:S(2)}, u32[]{:S(2)}) collective-permute-start(bf16[608,128]{1,0:T(8,128)(2,1)S(1)} %get-tuple-element.45), channel_id=1, source_target_pairs={{0,3},{1,4},{2,5},{3,6},{4,7},{5,0},{6,1},{7,2},{8,11},{9,12},{10,... | collective-permute-start | bytes 466952 | tf_op jit(solution)/shard_map/ppermute | solution.py:32
  187.7 10.3 %collective-permute-start.8 = (bf16[608,128]{1,0:T(8,128)(2,1)S(1)}, bf16[608,128]{1,0:T(8,128)(2,1)S(1)}, u32[]{:S(2)}, u32[]{:S(2)}) collective-permute-start(bf16[608,128]{1,0:T(8,128)(2,1)S(1)} %get-tuple-element.46), channel_id=1, source_target_pairs={{0,2},{1,3},{2,4},{3,5},{4,6},{5,7},{6,0},{7,1},{8,10},{9,11},{10,... | collective-permute-start | bytes 466952 | tf_op jit(solution)/shard_map/ppermute | solution.py:32
  199.9 58.3 %copy-start.1 = (bf16[8,64,128]{2,1,0:T(8,128)(2,1)S(1)}, bf16[8,64,128]{2,1,0:T(8,128)(2,1)}, u32[]{:S(2)}) copy-start(bf16[8,64,128]{2,1,0:T(8,128)(2,1)} %forward_rows.1) | copy-start | bytes 393220
  199.9 26.3 %all-to-all-start.4 = ((bf16[64,8,128]{2,1,0:T(8,128)(2,1)}), bf16[64,8,128]{2,1,0:T(8,128)(2,1)S(1)}, u32[]{:S(2)}, u32[]{:S(2)}) async-start(bf16[64,8,128]{2,1,0:T(8,128)(2,1)} %bitcast.251), calls=%async_computation.4 | async-start | bytes 262144 | tf_op jit(solution)/shard_map/all_to_all | solution.py:24
  226.2 28.5 %all-to-all-start.6 = ((bf16[64,16,128]{2,1,0:T(8,128)(2,1)}), bf16[64,16,128]{2,1,0:T(8,128)(2,1)S(1)}, u32[]{:S(2)}, u32[]{:S(2)}) async-start(bf16[64,16,128]{2,1,0:T(8,128)(2,1)} %reshape.204), calls=%async_computation.6 | async-start | bytes 524288 | tf_op jit(solution)/shard_map/all_to_all | solution.py:24
  254.7 9.2 %all-to-all-start.5 = ((bf16[8,64,128]{2,1,0:T(8,128)(2,1)}), bf16[8,64,128]{2,1,0:T(8,128)(2,1)S(1)}, u32[]{:S(2)}, u32[]{:S(2)}) async-start(bf16[8,64,128]{2,1,0:T(8,128)(2,1)} %bitcast.250), calls=%async_computation.5 | async-start | bytes 262144 | tf_op jit(solution)/shard_map/all_to_all | solution.py:24
  282.7 23.0 %copy-start.6 = (bf16[64,2048]{1,0:T(8,128)(2,1)S(1)}, bf16[64,2048]{1,0:T(8,128)(2,1)}, u32[]{:S(2)}) copy-start(bf16[64,2048]{1,0:T(8,128)(2,1)} %get-tuple-element.14) | copy-start | bytes 786436
  284.2 16.4 %collective-permute-start.20 = (bf16[672,128]{1,0:T(8,128)(2,1)S(1)}, bf16[672,128]{1,0:T(8,128)(2,1)S(1)}, u32[]{:S(2)}, u32[]{:S(2)}) collective-permute-start(bf16[672,128]{1,0:T(8,128)(2,1)S(1)} %get-tuple-element.25), channel_id=1, source_target_pairs={{0,1},{1,2},{2,3},{3,4},{4,5},{5,6},{6,7},{7,0},{8,9},{9,10},{10,1... | collective-permute-start | bytes 516104 | tf_op jit(solution)/shard_map/ppermute | solution.py:32
  287.0 16.2 %collective-permute-start.19 = (bf16[672,128]{1,0:T(8,128)(2,1)S(1)}, bf16[672,128]{1,0:T(8,128)(2,1)S(1)}, u32[]{:S(2)}, u32[]{:S(2)}) collective-permute-start(bf16[672,128]{1,0:T(8,128)(2,1)S(1)} %get-tuple-element.26), channel_id=1, source_target_pairs={{0,2},{1,3},{2,4},{3,5},{4,6},{5,7},{6,0},{7,1},{8,10},{9,11},{10,... | collective-permute-start | bytes 516104 | tf_op jit(solution)/shard_map/ppermute | solution.py:32
  289.2 17.2 %collective-permute-start.18 = (bf16[672,128]{1,0:T(8,128)(2,1)S(1)}, bf16[672,128]{1,0:T(8,128)(2,1)S(1)}, u32[]{:S(2)}, u32[]{:S(2)}) collective-permute-start(bf16[672,128]{1,0:T(8,128)(2,1)S(1)} %get-tuple-element.27), channel_id=1, source_target_pairs={{0,3},{1,4},{2,5},{3,6},{4,7},{5,0},{6,1},{7,2},{8,11},{9,12},{10,... | collective-permute-start | bytes 516104 | tf_op jit(solution)/shard_map/ppermute | solution.py:32
  292.2 14.2 %collective-permute-start.17 = (bf16[672,128]{1,0:T(8,128)(2,1)S(1)}, bf16[672,128]{1,0:T(8,128)(2,1)S(1)}, u32[]{:S(2)}, u32[]{:S(2)}) collective-permute-start(bf16[672,128]{1,0:T(8,128)(2,1)S(1)} %get-tuple-element.28), channel_id=1, source_target_pairs={{0,4},{1,5},{2,6},{3,7},{4,0},{5,1},{6,2},{7,3},{8,12},{9,13},{10,... | collective-permute-start | bytes 516104 | tf_op jit(solution)/shard_map/ppermute | solution.py:32
  296.6 9.8 %collective-permute-start.16 = (bf16[672,128]{1,0:T(8,128)(2,1)S(1)}, bf16[672,128]{1,0:T(8,128)(2,1)S(1)}, u32[]{:S(2)}, u32[]{:S(2)}) collective-permute-start(bf16[672,128]{1,0:T(8,128)(2,1)S(1)} %get-tuple-element.29), channel_id=1, source_target_pairs={{0,5},{1,6},{2,7},{3,0},{4,1},{5,2},{6,3},{7,4},{8,13},{9,14},{10,... | collective-permute-start | bytes 516104 | tf_op jit(solution)/shard_map/ppermute | solution.py:32
  300.6 8.3 %collective-permute-start.15 = (bf16[672,128]{1,0:T(8,128)(2,1)S(1)}, bf16[672,128]{1,0:T(8,128)(2,1)S(1)}, u32[]{:S(2)}, u32[]{:S(2)}) collective-permute-start(bf16[672,128]{1,0:T(8,128)(2,1)S(1)} %get-tuple-element.30), channel_id=1, source_target_pairs={{0,6},{1,7},{2,0},{3,1},{4,2},{5,3},{6,4},{7,5},{8,14},{9,15},{10,... | collective-permute-start | bytes 516104 | tf_op jit(solution)/shard_map/ppermute | solution.py:32
  303.2 8.7 %collective-permute-start.14 = (bf16[672,128]{1,0:T(8,128)(2,1)S(1)}, bf16[672,128]{1,0:T(8,128)(2,1)S(1)}, u32[]{:S(2)}, u32[]{:S(2)}) collective-permute-start(bf16[672,128]{1,0:T(8,128)(2,1)S(1)} %get-tuple-element.31), channel_id=1, source_target_pairs={{0,7},{1,0},{2,1},{3,2},{4,3},{5,4},{6,5},{7,6},{8,15},{9,8},{10,9... | collective-permute-start | bytes 516104 | tf_op jit(solution)/shard_map/ppermute | solution.py:32
  313.4 24.3 %all-to-all-start.8 = ((bf16[64,8,128]{2,1,0:T(8,128)(2,1)}), bf16[64,8,128]{2,1,0:T(8,128)(2,1)S(1)}, u32[]{:S(2)}, u32[]{:S(2)}) async-start(bf16[64,8,128]{2,1,0:T(8,128)(2,1)} %fusion.63), calls=%async_computation.8 | async-start | bytes 262144 | tf_op jit(solution)/shard_map/all_to_all | solution.py:24
  337.7 28.3 %all-to-all-start.7 = ((bf16[64,16,128]{2,1,0:T(8,128)(2,1)}), bf16[64,16,128]{2,1,0:T(8,128)(2,1)S(1)}, u32[]{:S(2)}, u32[]{:S(2)}) async-start(bf16[64,16,128]{2,1,0:T(8,128)(2,1)} %bitcast.99), calls=%async_computation.7 | async-start | bytes 524288 | tf_op jit(solution)/shard_map/all_to_all | solution.py:24
  368.4 27.8 %all-to-all-start.9 = ((bf16[64,16,128]{2,1,0:T(8,128)(2,1)}), bf16[64,16,128]{2,1,0:T(8,128)(2,1)S(1)}, u32[]{:S(2)}, u32[]{:S(2)}) async-start(bf16[64,16,128]{2,1,0:T(8,128)(2,1)} %broadcast_in_dim.82), calls=%async_computation.9 | async-start | bytes 524288 | tf_op jit(solution)/shard_map/all_to_all | solution.py:24
  397.1 14.0 %all-to-all-start.10 = ((bf16[8,200,128]{2,1,0:T(8,128)(2,1)}), bf16[8,200,128]{2,1,0:T(8,128)(2,1)S(1)}, u32[]{:S(2)}, u32[]{:S(2)}) async-start(bf16[8,200,128]{2,1,0:T(8,128)(2,1)} %broadcast_in_dim.83), calls=%async_computation.10 | async-start | bytes 819200 | tf_op jit(solution)/shard_map/all_to_all | solution.py:24
  (1 other events, 0.7 us)

commit v4 on v2

--- a/solution.py
+++ b/solution.py
@@ -9,6 +9,7 @@
 from jax.sharding import Mesh
 from jax.sharding import PartitionSpec as P
 
+
 HEAD = ("head_0", "head_1")
 ROW_HEAD = ("row", "head_0", "head_1")
 
@@ -21,6 +22,40 @@
 
 def exchanged(parts, axis):
     return lax.all_to_all(parts, axis, split_axis=0, concat_axis=0, tiled=True)
+
+
+def shifted_exchange(parts):
+    count = parts.shape[0]
+    pieces = [parts[0]]
+    for shift in range(1, count):
+        pairs = [(at, (at + shift) % count) for at in range(count)]
+        pieces.append(lax.ppermute(parts[shift], HEAD, pairs))
+    return pieces
+
+
+def rolled(x, by):
+    return lax.dynamic_slice_in_dim(jnp.concatenate([x, x]), by, x.shape[0], axis=0)
+
+
+def place_kernel(own_ref, *refs):
+    count = len(refs) - 1
+    for shift in range(count):
+        place = lax.rem(own_ref[0] + (count - shift), count)
+        refs[-1][pl.ds(place, 1)] = refs[shift][...][None]
+
+
+def placed(own_class, pieces):
+    return pl.pallas_call(
+        place_kernel,
+        in_specs=[
+            pl.BlockSpec(memory_space=pltpu.SMEM),
+            *[pl.BlockSpec(memory_space=pltpu.VMEM) for _ in pieces],
+        ],
+        out_specs=pl.BlockSpec(memory_space=pltpu.VMEM),
+        out_shape=jax.ShapeDtypeStruct((len(pieces), *pieces[0].shape), pieces[0].dtype),
+        interpret=INTERPRET,
+        name="place_pieces",
+    )(own_class, *pieces)
 
 
 def to_all(x, axis):
@@ -96,7 +131,7 @@
 
 
 def forward_kernel(heads, positions, class_ref, rows_ref, bias_ref, mask_ref, wq_ref, wkv_ref,
-                   wg_ref, wo_ref, gate_ref, after_ref, full_bias):
+                   wg_ref, wo_ref, gate_ref, gain_ref, shift_ref, after_ref, normal_ref, full_bias):
     groups = after_ref.shape[1]
 
     @pl.when(pl.program_id(0) == 0)
@@ -112,7 +147,10 @@
     gated = (result[3] * result[6]).astype(jnp.bfloat16)
     update = matmul(gated, wo_ref[...], 1, 0).astype(jnp.bfloat16)
     pair = rows_ref[0, positions : positions + groups]
-    after_ref[0] = (pair.astype(jnp.float32) + update.astype(jnp.float32)).astype(jnp.bfloat16)
+    after = (pair.astype(jnp.float32) + update.astype(jnp.float32)).astype(jnp.bfloat16)
+    after_ref[0] = after
+    _, _, normal = layer_norm(after, gain_ref[...], shift_ref[...])
+    normal_ref[0] = normal
 
 
 def backward_kernel(heads, positions, second, share_rows, class_ref, rows_ref, bias_ref, mask_ref,
@@ -208,10 +246,18 @@
     return (projection[0], joined, projection[3], out_proj, gate_offset[None])
 
 
-def forward_call(own_class, rows, bias, key_bias, params, heads, positions):
+def forward_call(own_class, rows, bias, key_bias, params, next_params, heads, positions):
     classes, _, channels = rows.shape
     groups = positions // classes
-    rest = (bias, key_bias, *kernel_weights(params))
+    rest = (
+        bias,
+        key_bias,
+        *kernel_weights(params),
+        next_params[0][None],
+        next_params[1][None],
+    )
+    result_spec = pl.BlockSpec((1, groups, channels), lambda step: (step, 0, 0))
+    result = jax.ShapeDtypeStruct((classes, groups, channels), jnp.bfloat16)
     return pl.pallas_call(
         functools.partial(forward_kernel, heads, positions),
         grid=(classes,),
@@ -220,8 +266,8 @@
             pl.BlockSpec((1, *rows.shape[1:]), lambda step: (step, 0, 0)),
             *[whole_spec(x) for x in rest],
         ],
-        out_specs=pl.BlockSpec((1, groups, channels), lambda step: (step, 0, 0)),
-        out_shape=jax.ShapeDtypeStruct((classes, groups, channels), jnp.bfloat16),
+        out_specs=[result_spec, result_spec],
+        out_shape=[result, result],
         scratch_shapes=[pltpu.VMEM((heads * groups, positions), jnp.float32)],
         compiler_params=pltpu.CompilerParams(dimension_semantics=("arbitrary",)),
         interpret=INTERPRET,
@@ -233,7 +279,6 @@
                   share_rows):
     second = ride is None
     classes, groups, channels = grad.shape
-    inner = params[2].shape[2]
     if second:
         ride = jnp.zeros((8, LANES), jnp.bfloat16)
         rows_spec = pl.BlockSpec((classes, 1, groups, channels), lambda step: (0, step, 0, 0))
@@ -324,14 +369,11 @@
         "nc,ch->hn", normal_flat, bias_weights[0], preferred_element_type=jnp.float32
     ).astype(half)
     own_cotangent = cotangent.reshape(groups, classes, channels)
-    arrived = exchanged(
-        jnp.concatenate(
-            [to_all(normal_flat, HEAD), own_pair, own_cotangent.transpose(1, 0, 2)], axis=1
-        ),
-        HEAD,
-    )
-    first_rows = arrived
-    cotangent_query = arrived[:, positions + groups :]
+    class_parts = jnp.concatenate([own_pair, own_cotangent.transpose(1, 0, 2)], axis=1)
+    class_parts = rolled(class_parts, own_class[0])
+    pieces = shifted_exchange(jnp.concatenate([to_all(normal_flat, HEAD), class_parts], axis=1))
+    first_rows = placed(own_class, pieces)
+    cotangent_query = first_rows[:, positions + groups :]
     arrived = exchanged(
         jnp.concatenate(
             [
@@ -345,16 +387,14 @@
     first_bias = arrived[:, :bias_rows].reshape(groups, head_total * positions)
     second_grad_query = arrived[:, bias_rows:].transpose(1, 0, 2)
 
-    after_query = forward_call(
-        own_class, first_rows, first_bias, key_bias, params[0], head_total, positions
-    )
-    after_normed, after_inverse, after_normal = layer_norm(
-        after_query, norm_gain[1], norm_shift[1]
-    )
+    after_query, after_normal = forward_call(
+        own_class, first_rows, first_bias, key_bias, params[0], params[1], head_total, positions
+    )
+    after_normed, after_inverse, _ = layer_norm(after_query, norm_gain[1], norm_shift[1])
     second_bias_own = jnp.einsum(
         "abc,ch->ahb", after_normal, bias_weights[1], preferred_element_type=jnp.float32
     ).astype(half)
-    after_own = exchanged(after_query, HEAD)
+    after_own = exchanged(after_normal, HEAD)
     arrived = exchanged(
         jnp.concatenate(
             [
@@ -371,8 +411,7 @@
         .transpose(1, 0, 2)
         .reshape(positions, head_total * groups)
     )
-    flipped_query = arrived[:, bias_rows:].transpose(1, 0, 2)
-    _, _, second_query = layer_norm(flipped_query, norm_gain[1], norm_shift[1])
+    second_query = arrived[:, bias_rows:].transpose(1, 0, 2)
     second_rows = exchanged(to_all(second_query, HEAD), HEAD)
     sent, bias_parts = backward_call(
         own_class,
@@ -391,9 +430,10 @@
     def group_shares_of(arrived_shares):
         summed = jnp.sum(arrived_shares.astype(jnp.float32), axis=0)
         summed = padded_rows(summed, groups * group_rows).astype(half)
-        return padded_rows(summed.reshape(groups, group_rows, LANES), rounded_up(group_rows, 8))
+        return summed.reshape(groups, group_rows, LANES)
 
     arrived = exchanged(sent, HEAD)
+    second_shares = group_shares_of(arrived[:, positions:])
     grad_flipped = jnp.sum(arrived[:, :positions].astype(jnp.float32), axis=0).astype(half)
     bias_parts = (
         bias_parts.reshape(classes, groups, head_total * groups)
@@ -405,7 +445,6 @@
             [
                 bias_parts,
                 grad_flipped.reshape(classes, groups, channels).transpose(1, 0, 2),
-                group_shares_of(arrived[:, positions:]),
             ],
             axis=1,
         ),
@@ -413,10 +452,6 @@
     )
     summed = jnp.sum(arrived[:, :bias_rows].astype(jnp.float32), axis=0)
     second_bias_half = summed.reshape(classes, head_total, groups).astype(half)
-    second_own = jnp.sum(
-        arrived[:, bias_rows + classes : bias_rows + classes + group_rows].astype(jnp.float32),
-        axis=0,
-    )
     grad_query = exchanged(arrived[:, bias_rows : bias_rows + classes].transpose(1, 0, 2), HEAD)
     grad_normal = grad_query.astype(jnp.float32) + jnp.einsum(
         "ahb,ch->abc", second_bias_half, bias_weights[1], preferred_element_type=jnp.float32
@@ -458,7 +493,10 @@
         jnp.concatenate(
             [
                 bias_parts.reshape(groups, bias_rows, LANES),
-                group_shares_of(shares),
+                padded_rows(
+                    jnp.concatenate([group_shares_of(shares), second_shares], axis=1),
+                    rounded_up(2 * group_rows, 8),
+                ),
             ],
             axis=1,
         ),
@@ -466,8 +504,8 @@
     )
     summed = jnp.sum(arrived[:, :bias_rows].astype(jnp.float32), axis=0)
     bias_half = summed.reshape(head_total, positions).astype(half)
-    first_own = jnp.sum(
-        arrived[:, bias_rows : bias_rows + group_rows].astype(jnp.float32), axis=0
+    shares_total = jnp.sum(
+        arrived[:, bias_rows : bias_rows + 2 * group_rows].astype(jnp.float32), axis=0
     )
     grad_normal = grad_normal + jnp.einsum(
         "hn,ch->nc", bias_half, bias_weights[0], preferred_element_type=jnp.float32
@@ -488,22 +526,25 @@
     )
 
     small_rows = first_small.shape[0]
-    tail = jnp.concatenate([first_own, second_own, first_small], axis=0).astype(half)
+    tail = jnp.concatenate([shares_total, first_small], axis=0).astype(half)
     tail = padded_rows(tail, rounded_up(tail.shape[0], 8))
-    arrived = exchanged(to_all(tail, "row"), "row").astype(jnp.float32)
+    arrived = exchanged(to_all(tail, "row"), "row")
     whole_rows = groups * group_rows
     shared = jnp.concatenate(
         [
             arrived[:, :group_rows].reshape(whole_rows, LANES)[:share_rows],
             arrived[:, group_rows : 2 * group_rows].reshape(whole_rows, LANES)[:share_rows],
             padded_rows(
-                jnp.sum(arrived[:, 2 * group_rows : 2 * group_rows + small_rows], axis=0),
+                jnp.sum(
+                    arrived[:, 2 * group_rows : 2 * group_rows + small_rows].astype(jnp.float32),
+                    axis=0,
+                ).astype(half),
                 rounded_up(small_rows, 8),
             ),
         ],
         axis=0,
     )
-    arrived = exchanged(to_all(shared, HEAD), HEAD)
+    arrived = exchanged(to_all(shared, HEAD), HEAD).astype(jnp.float32)
     first_whole = arrived[:, :share_rows].reshape(-1, LANES)
     second_whole = arrived[:, share_rows : 2 * share_rows].reshape(-1, LANES)
     first_small = jnp.sum(arrived[:, 2 * share_rows : 2 * share_rows + small_rows], axis=0)
@@ -530,4 +571,5 @@
     finer = Mesh(mesh.devices.reshape(mesh.shape["row"], 4, 2), ("row", "head_0", "head_1"))
     in_specs = (P(ROW_HEAD, None, None), P(ROW_HEAD, None, None), P(), P(), P(), P(), P(), P(), P())
     out_specs = (P(ROW_HEAD, None, None), P(), P(), P(), P(), P(), P())
+
     return jax.shard_map(local, mesh=finer, in_specs=in_specs, out_specs=out_specs, check_vma=False)

time: 382 us -> 364 us (0.953)
  blocking collectives: 74.3 us -> 47.1 us
  starting transfers between devices: 55.9 us -> 81.4 us
  waiting for transfers between devices: 172 us -> 154 us
  Pallas kernels: 41.2 us -> 45.2 us
    all_to_all x2 -> x1, blocking collectives: 74.3 us -> 47.1 us  [exchanged(): return lax.all_to_all(parts, axis, split_axis=0, concat_axis=0, tiled=True)]
    ppermute x0 -> x7, starting transfers between devices: none -> 22.9 us  [shifted_exchange(): pieces.append(lax.ppermute(parts[shift], HEAD, pairs))]
    all_to_all x10, waiting for transfers between devices: 172 us -> 152 us  [exchanged(): return lax.all_to_all(parts, axis, split_axis=0, concat_axis=0, tiled=True)]
  transfers between devices with their start and end apart: 10 -> 17, of which waited for: 10 -> 10; matrix products, arithmetic and copies ran while one was open for 3% -> 3% of each run, Pallas kernels for 0% -> 1%
where the time goes in v4:
time: 364 us; the launch traced here: 363 us
  waiting for transfers between devices  154 us (42%)
  starting transfers between devices  81.4 us (22%)
  blocking collectives  47.1 us (13%)
  Pallas kernels  45.2 us (12%)
  other arithmetic  17.5 us (5%)
  local copies, waits for them, and re-layouts  12.9 us (4%)
    all_to_all x10, waiting for transfers between devices, exchanged(): return lax.all_to_all(parts, axis, split_axis=0, concat_axis=0, tiled=True)  152 us
    all_to_all x10, starting transfers between devices, exchanged(): return lax.all_to_all(parts, axis, split_axis=0, concat_axis=0, tiled=True)  58.5 us
    all_to_all x1, blocking collectives, exchanged(): return lax.all_to_all(parts, axis, split_axis=0, concat_axis=0, tiled=True)  47.1 us
    pallas_call x2, Pallas kernels, backward_call(): pl.pallas_call(functools.partial(backward_kernel, heads, positions, secon...  31.6 us
    ppermute x7, starting transfers between devices, shifted_exchange(): pieces.append(lax.ppermute(parts[shift], HEAD, pairs))  22.9 us
    pallas_call x1, Pallas kernels, forward_call(): pl.pallas_call(functools.partial(forward_kernel, heads, positions), grid=...  11 us
  transfers between devices with their start and end apart: 17, of which 10 were waited for; matrix products, arithmetic and copies ran while one was open for 3% of the time, Pallas kernels for 1%

profile of v4, /device:TPU:1, one launch (start us, length us, event | category | flops | bytes accessed | tf_op | source)
XLA Modules:
  0.0 363.0 jit_solution(2120464119285140639)
XLA Ops:
  0.6 1.1 convert_reduce_fusion.2
  1.8 1.2 fusion.15
  3.0 1.3 slice_bitcast_fusion.17
  4.3 1.1 add_convert_fusion.1
  5.4 0.8 fusion.1
  6.3 0.8 pad_maximum_fusion.1
  7.1 19.8 %all-to-all-start = ((bf16[64,24,128]{2,1,0:T(8,128)(2,1)}), bf16[64,24,128]{2,1,0:T(8,128)(2,1)S(1)}, u32[]{:S(2)}, u32[]{:S(2)}) async-start(bf16[64,24,128]{2,1,0:T(8,128)(2,1)} %pad_maximum_fusion.1), calls=%async_computation | async-start | bytes 786432 | tf_op jit(solution)/shard_map/all_to_all | solution.py:24
  26.9 0.9 fusion.17
  28.8 2.3 collective-permute-start
  31.1 3.1 collective-permute-start.1
  34.2 4.5 %collective-permute-start.2 = (bf16[640,128]{1,0:T(8,128)(2,1)S(1)}, bf16[640,128]{1,0:T(8,128)(2,1)S(1)}, u32[]{:S(2)}, u32[]{:S(2)}) collective-permute-start(bf16[640,128]{1,0:T(8,128)(2,1)S(1)} %get-tuple-element.33), channel_id=1, source_target_pairs={{0,3},{1,4},{2,5},{3,6},{4,7},{5,0},{6,1},{7,2},{8,11},{9,12},{10,... | collective-permute-start | bytes 491528 | tf_op jit(solution)/shard_map/ppermute | solution.py:32
  38.8 3.6 %collective-permute-start.3 = (bf16[640,128]{1,0:T(8,128)(2,1)S(1)}, bf16[640,128]{1,0:T(8,128)(2,1)S(1)}, u32[]{:S(2)}, u32[]{:S(2)}) collective-permute-start(bf16[640,128]{1,0:T(8,128)(2,1)S(1)} %get-tuple-element.34), channel_id=1, source_target_pairs={{0,4},{1,5},{2,6},{3,7},{4,0},{5,1},{6,2},{7,3},{8,12},{9,13},{10,... | collective-permute-start | bytes 491528 | tf_op jit(solution)/shard_map/ppermute | solution.py:32
  42.4 3.9 %collective-permute-start.4 = (bf16[640,128]{1,0:T(8,128)(2,1)S(1)}, bf16[640,128]{1,0:T(8,128)(2,1)S(1)}, u32[]{:S(2)}, u32[]{:S(2)}) collective-permute-start(bf16[640,128]{1,0:T(8,128)(2,1)S(1)} %get-tuple-element.35), channel_id=1, source_target_pairs={{0,5},{1,6},{2,7},{3,0},{4,1},{5,2},{6,3},{7,4},{8,13},{9,14},{10,... | collective-permute-start | bytes 491528 | tf_op jit(solution)/shard_map/ppermute | solution.py:32
  47.6 3.1 collective-permute-start.5
  50.7 2.4 collective-permute-start.6
  55.1 1.9 collective-permute-done.6.refs_7_
  57.7 2.5 place_pieces.1.rows_ref
  60.3 0.8 copy.69
  61.1 11.0 %forward_rows.1 = (bf16[8,64,128]{2,1,0:T(8,128)(2,1)}, bf16[8,64,128]{2,1,0:T(8,128)(2,1)}) custom-call(s32[1]{0:T(128)} %bitcast.own_ref.class_ref, bf16[8,640,128]{2,1,0:T(8,128)(2,1)} %place_pieces.1.rows_ref, bf16[64,2048]{1,0:T(8,128)(2,1)} %bitcast.160, f32[1,512]{1,0:T(1,128)} %reshape.176.mask_ref, bf16[128,128]{1,0:T(8,128)(2,1)} %get-tuple-element.50.wq_ref, ...), custom_call_target="tpu_custom_call" | custom-call | tf_op jit(solution)/shard_map/forward_rows/pallas_call | solution.py:261
  72.1 5.6 %all-to-all-start.1 = ((bf16[8,64,128]{2,1,0:T(8,128)(2,1)}), bf16[8,64,128]{2,1,0:T(8,128)(2,1)S(1)}, u32[]{:S(2)}, u32[]{:S(2)}) async-start(bf16[8,64,128]{2,1,0:T(8,128)(2,1)} %get-tuple-element.14), calls=%async_computation.1 | async-start | bytes 262144 | tf_op jit(solution)/shard_map/all_to_all | solution.py:24
  77.7 1.1 fusion
  78.9 4.0 %all-to-all-done.1 = bf16[8,64,128]{2,1,0:T(8,128)(2,1)S(1)} async-done(((bf16[8,64,128]{2,1,0:T(8,128)(2,1)}), bf16[8,64,128]{2,1,0:T(8,128)(2,1)S(1)}, u32[]{:S(2)}, u32[]{:S(2)}) %all-to-all-start.1) | async-done | bytes 131104 | tf_op jit(solution)/shard_map/all_to_all | solution.py:24
  83.2 47.1 %all_to_all.55 = bf16[64,24,128]{2,1,0:T(8,128)(2,1)S(1)} all-to-all(bf16[64,24,128]{2,1,0:T(8,128)(2,1)S(1)} %pad_maximum_fusion.2), channel_id=1, replica_groups=mesh['row'=64,'head_0'=4,'head_1'=2] {'row'}, dimensions={0} | all-to-all | bytes 786432 | tf_op jit(solution)/shard_map/all_to_all | solution.py:24
  130.4 1.2 broadcast_in_dim.73
  131.6 3.6 all-to-all-start.3
  137.4 13.7 %all-to-all-done.3.rows_ref = bf16[8,8,64,128]{3,2,1,0:T(8,128)(2,1)S(1)} async-done(((bf16[8,8,64,128]{3,2,1,0:T(8,128)(2,1)}), bf16[8,8,64,128]{3,2,1,0:T(8,128)(2,1)S(1)}, u32[]{:S(2)}, u32[]{:S(2)}) %all-to-all-start.3) | async-done | bytes 1048608 | tf_op jit(solution)/shard_map/all_to_all | solution.py:24
  152.3 15.8 %backward_second.1 = (bf16[8,608,128]{2,1,0:T(8,128)(2,1)}, bf16[512,256]{1,0:T(8,128)(2,1)}) custom-call(s32[1]{0:T(128)} %bitcast.own_ref.class_ref, bf16[8,8,64,128]{3,2,1,0:T(8,128)(2,1)} %copy-done, bf16[512,256]{1,0:T(8,128)(2,1)} %bitcast.183, f32[1,512]{1,0:T(1,128)} %reshape.176.mask_ref, bf16[8,64,128]{2,1,0:T(8,128)(2,1)} %bitcast.191, ...), custom_call_target="tpu_custom_call" | custom-call | tf_op jit(solution)/shard_map/backward_second/pallas_call | solution.py:294
  168.1 3.7 %all-to-all-start.4 = ((bf16[8,608,128]{2,1,0:T(8,128)(2,1)}), bf16[8,608,128]{2,1,0:T(8,128)(2,1)S(1)}, u32[]{:S(2)}, u32[]{:S(2)}) async-start(bf16[8,608,128]{2,1,0:T(8,128)(2,1)} %get-tuple-element.16), calls=%async_computation.4 | async-start | bytes 2490368 | tf_op jit(solution)/shard_map/all_to_all | solution.py:24
  172.0 19.6 %all-to-all-done.4 = bf16[8,608,128]{2,1,0:T(8,128)(2,1)S(1)} async-done(((bf16[8,608,128]{2,1,0:T(8,128)(2,1)}), bf16[8,608,128]{2,1,0:T(8,128)(2,1)S(1)}, u32[]{:S(2)}, u32[]{:S(2)}) %all-to-all-start.4) | async-done | bytes 1245216 | tf_op jit(solution)/shard_map/all_to_all | solution.py:24
  191.8 0.8 pad_maximum_fusion.3
  192.6 5.9 %all-to-all-start.5 = ((bf16[64,24,128]{2,1,0:T(8,128)(2,1)}), bf16[64,24,128]{2,1,0:T(8,128)(2,1)S(1)}, u32[]{:S(2)}, u32[]{:S(2)}) async-start(bf16[64,24,128]{2,1,0:T(8,128)(2,1)} %pad_maximum_fusion.3), calls=%async_computation.5 | async-start | bytes 786432 | tf_op jit(solution)/shard_map/all_to_all | solution.py:24
  199.0 28.4 %all-to-all-done.5 = bf16[64,24,128]{2,1,0:T(8,128)(2,1)S(1)} async-done(((bf16[64,24,128]{2,1,0:T(8,128)(2,1)}), bf16[64,24,128]{2,1,0:T(8,128)(2,1)S(1)}, u32[]{:S(2)}, u32[]{:S(2)}) %all-to-all-start.5) | async-done | bytes 393248 | tf_op jit(solution)/shard_map/all_to_all | solution.py:24
  228.2 3.6 all-to-all-start.6
  231.9 5.0 %all-to-all-done.6 = bf16[8,64,128]{2,1,0:T(8,128)(2,1)S(1)} async-done(((bf16[8,64,128]{2,1,0:T(8,128)(2,1)}), bf16[8,64,128]{2,1,0:T(8,128)(2,1)S(1)}, u32[]{:S(2)}, u32[]{:S(2)}) %all-to-all-start.6) | async-done | bytes 131104 | tf_op jit(solution)/shard_map/all_to_all | solution.py:24
  238.0 1.9 add_convert_fusion
  239.9 15.8 %backward_first.1 = (bf16[8,672,128]{2,1,0:T(8,128)(2,1)}, bf16[64,2048]{1,0:T(8,128)(2,1)}) custom-call(s32[1]{0:T(128)} %bitcast.own_ref.class_ref, bf16[8,640,128]{2,1,0:T(8,128)(2,1)} %place_pieces.1.rows_ref, bf16[64,2048]{1,0:T(8,128)(2,1)} %bitcast.161, f32[1,512]{1,0:T(1,128)} %reshape.176.mask_ref, bf16[8,64,128]{2,1,0:T(8,128)(2,1)} %get-tuple-element.27.grad_ref, ...), custom_call_target="tpu_custom_call" | custom-call | tf_op jit(solution)/shard_map/backward_first/pallas_call | solution.py:294
  255.7 3.7 %all-to-all-start.7 = ((bf16[8,672,128]{2,1,0:T(8,128)(2,1)}), bf16[8,672,128]{2,1,0:T(8,128)(2,1)S(1)}, u32[]{:S(2)}, u32[]{:S(2)}) async-start(bf16[8,672,128]{2,1,0:T(8,128)(2,1)} %get-tuple-element.17), calls=%async_computation.7 | async-start | bytes 2752512 | tf_op jit(solution)/shard_map/all_to_all | solution.py:24
  259.5 21.9 %all-to-all-done.7 = bf16[8,672,128]{2,1,0:T(8,128)(2,1)S(1)} async-done(((bf16[8,672,128]{2,1,0:T(8,128)(2,1)}), bf16[8,672,128]{2,1,0:T(8,128)(2,1)S(1)}, u32[]{:S(2)}, u32[]{:S(2)}) %all-to-all-start.7) | async-done | bytes 1376288 | tf_op jit(solution)/shard_map/all_to_all | solution.py:24
  281.5 0.8 pad_maximum_fusion.4
  282.3 4.8 %all-to-all-start.8 = ((bf16[64,24,128]{2,1,0:T(8,128)(2,1)}), bf16[64,24,128]{2,1,0:T(8,128)(2,1)S(1)}, u32[]{:S(2)}, u32[]{:S(2)}) async-start(bf16[64,24,128]{2,1,0:T(8,128)(2,1)} %pad_maximum_fusion.4), calls=%async_computation.8 | async-start | bytes 786432 | tf_op jit(solution)/shard_map/all_to_all | solution.py:24
  287.2 28.8 %all-to-all-done.8 = bf16[64,24,128]{2,1,0:T(8,128)(2,1)S(1)} async-done(((bf16[64,24,128]{2,1,0:T(8,128)(2,1)}), bf16[64,24,128]{2,1,0:T(8,128)(2,1)S(1)}, u32[]{:S(2)}, u32[]{:S(2)}) %all-to-all-start.8) | async-done | bytes 393248 | tf_op jit(solution)/shard_map/all_to_all | solution.py:24
  317.5 4.6 %all-to-all-start.9 = ((bf16[64,16,128]{2,1,0:T(8,128)(2,1)}), bf16[64,16,128]{2,1,0:T(8,128)(2,1)S(1)}, u32[]{:S(2)}, u32[]{:S(2)}) async-start(bf16[64,16,128]{2,1,0:T(8,128)(2,1)} %broadcast_in_dim.80), calls=%async_computation.9 | async-start | bytes 524288 | tf_op jit(solution)/shard_map/all_to_all | solution.py:24
  322.5 23.4 %all-to-all-done.9 = bf16[64,16,128]{2,1,0:T(8,128)(2,1)S(1)} async-done(((bf16[64,16,128]{2,1,0:T(8,128)(2,1)}), bf16[64,16,128]{2,1,0:T(8,128)(2,1)S(1)}, u32[]{:S(2)}, u32[]{:S(2)}) %all-to-all-start.9) | async-done | bytes 262176 | tf_op jit(solution)/shard_map/all_to_all | solution.py:24
  346.0 0.8 broadcast_in_dim.81
  346.8 3.5 all-to-all-start.10
  350.3 0.9 bitcast_add_fusion
  351.1 7.8 %all-to-all-done.10 = bf16[8,200,128]{2,1,0:T(8,128)(2,1)S(1)} async-done(((bf16[8,200,128]{2,1,0:T(8,128)(2,1)}), bf16[8,200,128]{2,1,0:T(8,128)(2,1)S(1)}, u32[]{:S(2)}, u32[]{:S(2)}) %all-to-all-start.10) | async-done | bytes 409632 | tf_op jit(solution)/shard_map/all_to_all | solution.py:24
  362.2 0.8 pad_maximum_fusion
  (132 shorter events, 17.2 us)
Async XLA Ops:
  0.6 5.7 %copy-start.2 = (bf16[1,512,128]{2,1,0:T(8,128)(2,1)S(1)}, bf16[1,512,128]{2,1,0:T(8,128)(2,1)}, u32[]{:S(2)}) copy-start(bf16[1,512,128]{2,1,0:T(8,128)(2,1)} %param.10) | copy-start | bytes 393220
  1.7 25.1 %copy-start.1 = (bf16[1,512,128]{2,1,0:T(8,128)(2,1)S(1)}, bf16[1,512,128]{2,1,0:T(8,128)(2,1)}, u32[]{:S(2)}) copy-start(bf16[1,512,128]{2,1,0:T(8,128)(2,1)} %param.9) | copy-start | bytes 393220
  7.1 53.2 %all-to-all-start = ((bf16[64,24,128]{2,1,0:T(8,128)(2,1)}), bf16[64,24,128]{2,1,0:T(8,128)(2,1)S(1)}, u32[]{:S(2)}, u32[]{:S(2)}) async-start(bf16[64,24,128]{2,1,0:T(8,128)(2,1)} %pad_maximum_fusion.1), calls=%async_computation | async-start | bytes 786432 | tf_op jit(solution)/shard_map/all_to_all | solution.py:24
  28.0 18.3 %copy-start.15 = (bf16[2,128,128]{2,1,0:T(8,128)(2,1)S(1)}, bf16[2,128,128]{2,1,0:T(8,128)(2,1)}, u32[]{:S(2)}) copy-start(bf16[2,128,128]{2,1,0:T(8,128)(2,1)} %param.16) | copy-start | bytes 196612
  28.0 18.9 %copy-start.5 = (bf16[2,4,128,128]{3,2,1,0:T(8,128)(2,1)S(1)}, bf16[2,4,128,128]{3,2,1,0:T(8,128)(2,1)}, u32[]{:S(2)}) copy-start(bf16[2,4,128,128]{3,2,1,0:T(8,128)(2,1)} %param.14) | copy-start | bytes 786436
  28.0 19.6 %copy-start.17 = (s32[512]{0:T(512)S(1)}, s32[512]{0:T(512)}, u32[]{:S(2)}) copy-start(s32[512]{0:T(512)} %param.11) | copy-start | bytes 6148
  28.0 25.0 %copy-start.18 = (f32[2,128]{1,0:T(2,128)S(1)}, f32[2,128]{1,0:T(2,128)}, u32[]{:S(2)}) copy-start(f32[2,128]{1,0:T(2,128)} %param.15) | copy-start | bytes 3076
  28.8 18.8 %collective-permute-start = (bf16[640,128]{1,0:T(8,128)(2,1)S(1)}, bf16[640,128]{1,0:T(8,128)(2,1)S(1)}, u32[]{:S(2)}, u32[]{:S(2)}) collective-permute-start(bf16[640,128]{1,0:T(8,128)(2,1)S(1)} %get-tuple-element.31), channel_id=1, source_target_pairs={{0,1},{1,2},{2,3},{3,4},{4,5},{5,6},{6,7},{7,0},{8,9},{9,10},{10,1... | collective-permute-start | bytes 491528 | tf_op jit(solution)/shard_map/ppermute | solution.py:32
  31.1 19.6 %collective-permute-start.1 = (bf16[640,128]{1,0:T(8,128)(2,1)S(1)}, bf16[640,128]{1,0:T(8,128)(2,1)S(1)}, u32[]{:S(2)}, u32[]{:S(2)}) collective-permute-start(bf16[640,128]{1,0:T(8,128)(2,1)S(1)} %get-tuple-element.32), channel_id=1, source_target_pairs={{0,2},{1,3},{2,4},{3,5},{4,6},{5,7},{6,0},{7,1},{8,10},{9,11},{10,... | collective-permute-start | bytes 491528 | tf_op jit(solution)/shard_map/ppermute | solution.py:32
  34.2 20.9 %collective-permute-start.2 = (bf16[640,128]{1,0:T(8,128)(2,1)S(1)}, bf16[640,128]{1,0:T(8,128)(2,1)S(1)}, u32[]{:S(2)}, u32[]{:S(2)}) collective-permute-start(bf16[640,128]{1,0:T(8,128)(2,1)S(1)} %get-tuple-element.33), channel_id=1, source_target_pairs={{0,3},{1,4},{2,5},{3,6},{4,7},{5,0},{6,1},{7,2},{8,11},{9,12},{10,... | collective-permute-start | bytes 491528 | tf_op jit(solution)/shard_map/ppermute | solution.py:32
  38.8 16.3 %collective-permute-start.3 = (bf16[640,128]{1,0:T(8,128)(2,1)S(1)}, bf16[640,128]{1,0:T(8,128)(2,1)S(1)}, u32[]{:S(2)}, u32[]{:S(2)}) collective-permute-start(bf16[640,128]{1,0:T(8,128)(2,1)S(1)} %get-tuple-element.34), channel_id=1, source_target_pairs={{0,4},{1,5},{2,6},{3,7},{4,0},{5,1},{6,2},{7,3},{8,12},{9,13},{10,... | collective-permute-start | bytes 491528 | tf_op jit(solution)/shard_map/ppermute | solution.py:32
  42.4 12.7 %collective-permute-start.4 = (bf16[640,128]{1,0:T(8,128)(2,1)S(1)}, bf16[640,128]{1,0:T(8,128)(2,1)S(1)}, u32[]{:S(2)}, u32[]{:S(2)}) collective-permute-start(bf16[640,128]{1,0:T(8,128)(2,1)S(1)} %get-tuple-element.35), channel_id=1, source_target_pairs={{0,5},{1,6},{2,7},{3,0},{4,1},{5,2},{6,3},{7,4},{8,13},{9,14},{10,... | collective-permute-start | bytes 491528 | tf_op jit(solution)/shard_map/ppermute | solution.py:32
  47.6 9.5 %copy-start.8 = (bf16[640,128]{1,0:T(8,128)(2,1)}, bf16[640,128]{1,0:T(8,128)(2,1)S(1)}, u32[]{:S(2)}) copy-start(bf16[640,128]{1,0:T(8,128)(2,1)S(1)} %collective-permute-done.refs_1_) | copy-start | bytes 491524
  47.6 7.5 %collective-permute-start.5 = (bf16[640,128]{1,0:T(8,128)(2,1)S(1)}, bf16[640,128]{1,0:T(8,128)(2,1)S(1)}, u32[]{:S(2)}, u32[]{:S(2)}) collective-permute-start(bf16[640,128]{1,0:T(8,128)(2,1)S(1)} %get-tuple-element.36), channel_id=1, source_target_pairs={{0,6},{1,7},{2,0},{3,1},{4,2},{5,3},{6,4},{7,5},{8,14},{9,15},{10,... | collective-permute-start | bytes 491528 | tf_op jit(solution)/shard_map/ppermute | solution.py:32
  50.7 6.4 %copy-start.9 = (bf16[640,128]{1,0:T(8,128)(2,1)}, bf16[640,128]{1,0:T(8,128)(2,1)S(1)}, u32[]{:S(2)}) copy-start(bf16[640,128]{1,0:T(8,128)(2,1)S(1)} %collective-permute-done.1.refs_2_) | copy-start | bytes 491524
  50.7 6.4 %collective-permute-start.6 = (bf16[640,128]{1,0:T(8,128)(2,1)S(1)}, bf16[640,128]{1,0:T(8,128)(2,1)S(1)}, u32[]{:S(2)}, u32[]{:S(2)}) collective-permute-start(bf16[640,128]{1,0:T(8,128)(2,1)S(1)} %get-tuple-element.29), channel_id=1, source_target_pairs={{0,7},{1,0},{2,1},{3,2},{4,3},{5,4},{6,5},{7,6},{8,15},{9,8},{10,9... | collective-permute-start | bytes 491528 | tf_op jit(solution)/shard_map/ppermute | solution.py:32
  55.1 2.0 copy-start.10
  55.1 2.0 copy-start.11
  55.1 2.0 copy-start.12
  55.1 2.0 copy-start.13
  57.1 0.7 copy-start.14
  60.3 17.4 %copy-start.16 = (bf16[2,128,4]{1,2,0:T(4,128)(2,1)S(1)}, bf16[2,128,4]{1,2,0:T(4,128)(2,1)}, u32[]{:S(2)}) copy-start(bf16[2,128,4]{1,2,0:T(4,128)(2,1)} %param.17) | copy-start | bytes 6148
  72.1 10.8 %all-to-all-start.1 = ((bf16[8,64,128]{2,1,0:T(8,128)(2,1)}), bf16[8,64,128]{2,1,0:T(8,128)(2,1)S(1)}, u32[]{:S(2)}, u32[]{:S(2)}) async-start(bf16[8,64,128]{2,1,0:T(8,128)(2,1)} %get-tuple-element.14), calls=%async_computation.1 | async-start | bytes 262144 | tf_op jit(solution)/shard_map/all_to_all | solution.py:24
  131.6 19.5 %all-to-all-start.3 = ((bf16[8,8,64,128]{3,2,1,0:T(8,128)(2,1)}), bf16[8,8,64,128]{3,2,1,0:T(8,128)(2,1)S(1)}, u32[]{:S(2)}, u32[]{:S(2)}) async-start(bf16[8,8,64,128]{3,2,1,0:T(8,128)(2,1)} %broadcast_in_dim.73), calls=%async_computation.3 | async-start | bytes 2097152 | tf_op jit(solution)/shard_map/all_to_all | solution.py:24
  151.1 1.2 copy-start
  168.1 3.7 %copy-start.7 = (bf16[512,256]{1,0:T(8,128)(2,1)S(1)}, bf16[512,256]{1,0:T(8,128)(2,1)}, u32[]{:S(2)}) copy-start(bf16[512,256]{1,0:T(8,128)(2,1)} %get-tuple-element.15) | copy-start | bytes 786436
  168.1 23.5 %all-to-all-start.4 = ((bf16[8,608,128]{2,1,0:T(8,128)(2,1)}), bf16[8,608,128]{2,1,0:T(8,128)(2,1)S(1)}, u32[]{:S(2)}, u32[]{:S(2)}) async-start(bf16[8,608,128]{2,1,0:T(8,128)(2,1)} %get-tuple-element.16), calls=%async_computation.4 | async-start | bytes 2490368 | tf_op jit(solution)/shard_map/all_to_all | solution.py:24
  172.0 26.5 %copy-start.4 = (bf16[8,64,128]{2,1,0:T(8,128)(2,1)S(1)}, bf16[8,64,128]{2,1,0:T(8,128)(2,1)}, u32[]{:S(2)}) copy-start(bf16[8,64,128]{2,1,0:T(8,128)(2,1)} %get-tuple-element.13) | copy-start | bytes 393220
  191.8 39.9 %copy-start.3 = (bf16[8,64,128]{2,1,0:T(8,128)(2,1)S(1)}, bf16[8,64,128]{2,1,0:T(8,128)(2,1)}, u32[]{:S(2)}) copy-start(bf16[8,64,128]{2,1,0:T(8,128)(2,1)} %get-tuple-element.14) | copy-start | bytes 393220
  192.6 34.7 %all-to-all-start.5 = ((bf16[64,24,128]{2,1,0:T(8,128)(2,1)}), bf16[64,24,128]{2,1,0:T(8,128)(2,1)S(1)}, u32[]{:S(2)}, u32[]{:S(2)}) async-start(bf16[64,24,128]{2,1,0:T(8,128)(2,1)} %pad_maximum_fusion.3), calls=%async_computation.5 | async-start | bytes 786432 | tf_op jit(solution)/shard_map/all_to_all | solution.py:24
  228.2 8.8 %all-to-all-start.6 = ((bf16[8,64,128]{2,1,0:T(8,128)(2,1)}), bf16[8,64,128]{2,1,0:T(8,128)(2,1)S(1)}, u32[]{:S(2)}, u32[]{:S(2)}) async-start(bf16[8,64,128]{2,1,0:T(8,128)(2,1)} %bitcast.155), calls=%async_computation.6 | async-start | bytes 262144 | tf_op jit(solution)/shard_map/all_to_all | solution.py:24
  255.7 3.8 %copy-start.6 = (bf16[64,2048]{1,0:T(8,128)(2,1)S(1)}, bf16[64,2048]{1,0:T(8,128)(2,1)}, u32[]{:S(2)}) copy-start(bf16[64,2048]{1,0:T(8,128)(2,1)} %get-tuple-element.18) | copy-start | bytes 786436
  255.7 25.7 %all-to-all-start.7 = ((bf16[8,672,128]{2,1,0:T(8,128)(2,1)}), bf16[8,672,128]{2,1,0:T(8,128)(2,1)S(1)}, u32[]{:S(2)}, u32[]{:S(2)}) async-start(bf16[8,672,128]{2,1,0:T(8,128)(2,1)} %get-tuple-element.17), calls=%async_computation.7 | async-start | bytes 2752512 | tf_op jit(solution)/shard_map/all_to_all | solution.py:24
  282.3 33.7 %all-to-all-start.8 = ((bf16[64,24,128]{2,1,0:T(8,128)(2,1)}), bf16[64,24,128]{2,1,0:T(8,128)(2,1)S(1)}, u32[]{:S(2)}, u32[]{:S(2)}) async-start(bf16[64,24,128]{2,1,0:T(8,128)(2,1)} %pad_maximum_fusion.4), calls=%async_computation.8 | async-start | bytes 786432 | tf_op jit(solution)/shard_map/all_to_all | solution.py:24
  317.5 28.3 %all-to-all-start.9 = ((bf16[64,16,128]{2,1,0:T(8,128)(2,1)}), bf16[64,16,128]{2,1,0:T(8,128)(2,1)S(1)}, u32[]{:S(2)}, u32[]{:S(2)}) async-start(bf16[64,16,128]{2,1,0:T(8,128)(2,1)} %broadcast_in_dim.80), calls=%async_computation.9 | async-start | bytes 524288 | tf_op jit(solution)/shard_map/all_to_all | solution.py:24
  346.8 12.1 %all-to-all-start.10 = ((bf16[8,200,128]{2,1,0:T(8,128)(2,1)}), bf16[8,200,128]{2,1,0:T(8,128)(2,1)S(1)}, u32[]{:S(2)}, u32[]{:S(2)}) async-start(bf16[8,200,128]{2,1,0:T(8,128)(2,1)} %broadcast_in_dim.81), calls=%async_computation.10 | async-start | bytes 819200 | tf_op jit(solution)/shard_map/all_to_all | solution.py:24

commit v5 on v4

--- a/solution.py
+++ b/solution.py
@@ -112,16 +112,16 @@
     queries = spread_heads(
         (matmul(xq, wq, 1, 0) * scale).astype(jnp.bfloat16).astype(jnp.float32), heads
     )
-    key_value = matmul(x, wkv, 1, 0).astype(jnp.bfloat16)
-    keys = key_value[:, :channels]
-    values = key_value[:, channels:]
+    pairs = matmul(x, wkv, 1, 0).astype(jnp.bfloat16)
+    keys = pairs[:, :channels]
+    values = pairs[:, channels:]
     gate = jax.nn.sigmoid(matmul(xq, wg, 1, 0) + gate_offset)
     logits = matmul(queries, keys, 1, 1) + bias
     weights = jnp.exp(logits - jnp.max(logits, axis=1, keepdims=True))
     probs = weights / jnp.sum(weights, axis=1, keepdims=True)
     probs_half = probs.astype(jnp.bfloat16)
     attended = picked_heads(matmul(probs_half, values, 1, 0), heads)
-    return (queries, keys, values, gate, probs, probs_half, attended)
+    return (queries, pairs, probs, gate, attended)
 
 
 def split_bias(bias, key_bias, heads):
@@ -131,7 +131,8 @@
 
 
 def forward_kernel(heads, positions, class_ref, rows_ref, bias_ref, mask_ref, wq_ref, wkv_ref,
-                   wg_ref, wo_ref, gate_ref, gain_ref, shift_ref, after_ref, normal_ref, full_bias):
+                   wg_ref, wo_ref, gate_ref, gain_ref, shift_ref, after_ref, normal_ref, queries_ref, pairs_ref, probs_ref,
+                   gates_ref, attended_ref, full_bias):
     groups = after_ref.shape[1]
 
     @pl.when(pl.program_id(0) == 0)
@@ -141,10 +142,15 @@
     x = rows_ref[0, :positions]
     start = pl.multiple_of(class_ref[0] * groups, groups)
     xq = rows_ref[0, pl.ds(start, groups)]
-    result = attention(
+    queries, pairs, probs, gate, attended = attention(
         x, xq, full_bias[...], wq_ref[...], wkv_ref[...], wg_ref[...], gate_ref[...], heads
     )
-    gated = (result[3] * result[6]).astype(jnp.bfloat16)
+    queries_ref[0] = queries
+    pairs_ref[0] = pairs
+    probs_ref[0] = probs
+    gates_ref[0] = gate
+    attended_ref[0] = attended
+    gated = (gate * attended).astype(jnp.bfloat16)
     update = matmul(gated, wo_ref[...], 1, 0).astype(jnp.bfloat16)
     pair = rows_ref[0, positions : positions + groups]
     after = (pair.astype(jnp.float32) + update.astype(jnp.float32)).astype(jnp.bfloat16)
@@ -153,9 +159,15 @@
     normal_ref[0] = normal
 
 
-def backward_kernel(heads, positions, second, share_rows, class_ref, rows_ref, bias_ref, mask_ref,
-                    grad_ref, extra_ref, ride_ref, wq_ref, wkv_ref, wg_ref, wo_ref, gate_ref,
-                    sent_ref, bias_out_ref, full_bias, bias_sum, weight_sum, share):
+def backward_kernel(heads, positions, second, share_rows, class_ref, rows_ref, grad_ref, wq_ref,
+                    wkv_ref, wg_ref, wo_ref, gate_ref, *refs):
+    if second:
+        bias_ref, mask_ref = refs[:2]
+        full_bias = refs[-1]
+        sent_ref, bias_out_ref, bias_sum, weight_sum, share = refs[2:-1]
+    else:
+        queries_ref, pairs_ref, probs_ref, gates_ref, attended_ref, extra_ref, ride_ref = refs[:7]
+        sent_ref, bias_out_ref, bias_sum, weight_sum, share = refs[7:]
     step = pl.program_id(0)
     classes = sent_ref.shape[0]
     groups = positions // classes
@@ -169,11 +181,11 @@
         if second:
             full_bias[...] = bias_ref[...].astype(jnp.float32).T + mask_ref[...]
         else:
-            full_bias[...] = split_bias(bias_ref[...], mask_ref[...], heads)
             sent_ref[:, positions : positions + groups] = ride_ref[...]
         bias_sum[...] = jnp.zeros(bias_sum.shape, jnp.float32)
         weight_sum[...] = jnp.zeros(weight_sum.shape, jnp.float32)
-        weight_sum[5 * channels : 5 * channels + 8] = extra_ref[...]
+        if not second:
+            weight_sum[5 * channels : 5 * channels + 8] = extra_ref[...]
 
     if second:
         x = rows_ref[:, 0].reshape(positions, channels)
@@ -181,9 +193,17 @@
     else:
         x = rows_ref[0, :positions]
         xq = rows_ref[0, pl.ds(pl.multiple_of(own_class * groups, groups), groups)]
-    queries, keys, values, gate, probs, probs_half, attended = attention(
-        x, xq, full_bias[...], wq_ref[...], wkv_ref[...], wg_ref[...], gate_ref[...], heads
-    )
+    if second:
+        queries, pairs, probs, gate, attended = attention(
+            x, xq, full_bias[...], wq_ref[...], wkv_ref[...], wg_ref[...], gate_ref[...], heads
+        )
+    else:
+        queries, pairs, probs, gate, attended = (
+            ref[0] for ref in (queries_ref, pairs_ref, probs_ref, gates_ref, attended_ref)
+        )
+    keys = pairs[:, :inner]
+    values = pairs[:, inner:]
+    probs_half = probs.astype(jnp.bfloat16)
     scale = 1.0 / math.sqrt(inner // heads)
     grad = grad_ref[0]
     gated = (gate * attended).astype(jnp.bfloat16)
@@ -246,9 +266,15 @@
     return (projection[0], joined, projection[3], out_proj, gate_offset[None])
 
 
+def step_spec(shape):
+    return pl.BlockSpec((1, *shape[1:]), lambda step, n=len(shape): (step,) + (0,) * (n - 1))
+
+
 def forward_call(own_class, rows, bias, key_bias, params, next_params, heads, positions):
     classes, _, channels = rows.shape
     groups = positions // classes
+    inner = params[2].shape[2]
+    half = jnp.bfloat16
     rest = (
         bias,
         key_bias,
@@ -256,18 +282,25 @@
         next_params[0][None],
         next_params[1][None],
     )
-    result_spec = pl.BlockSpec((1, groups, channels), lambda step: (step, 0, 0))
-    result = jax.ShapeDtypeStruct((classes, groups, channels), jnp.bfloat16)
+    results = [
+        jax.ShapeDtypeStruct((classes, groups, channels), half),
+        jax.ShapeDtypeStruct((classes, groups, channels), half),
+        jax.ShapeDtypeStruct((classes, heads * groups, inner), half),
+        jax.ShapeDtypeStruct((classes, positions, 2 * inner), half),
+        jax.ShapeDtypeStruct((classes, heads * groups, positions), jnp.float32),
+        jax.ShapeDtypeStruct((classes, groups, inner), jnp.float32),
+        jax.ShapeDtypeStruct((classes, groups, inner), jnp.float32),
+    ]
     return pl.pallas_call(
         functools.partial(forward_kernel, heads, positions),
         grid=(classes,),
         in_specs=[
             pl.BlockSpec(memory_space=pltpu.SMEM),
-            pl.BlockSpec((1, *rows.shape[1:]), lambda step: (step, 0, 0)),
+            step_spec(rows.shape),
             *[whole_spec(x) for x in rest],
         ],
-        out_specs=[result_spec, result_spec],
-        out_shape=[result, result],
+        out_specs=[step_spec(x.shape) for x in results],
+        out_shape=results,
         scratch_shapes=[pltpu.VMEM((heads * groups, positions), jnp.float32)],
         compiler_params=pltpu.CompilerParams(dimension_semantics=("arbitrary",)),
         interpret=INTERPRET,
@@ -275,17 +308,22 @@
     )(own_class, rows, *rest)
 
 
-def backward_call(own_class, rows, bias, key_bias, grad, extra, ride, params, heads, positions,
-                  share_rows):
-    second = ride is None
+def backward_call(own_class, rows, grad, params, heads, positions, share_rows, steps, wholes):
+    second = not steps
     classes, groups, channels = grad.shape
+    scores = pltpu.VMEM((heads * groups, positions), jnp.float32)
+    scratch = [
+        scores,
+        pltpu.VMEM((classes * share_rows, channels), jnp.float32),
+        pltpu.VMEM((positions, channels), jnp.float32),
+    ]
     if second:
-        ride = jnp.zeros((8, LANES), jnp.bfloat16)
         rows_spec = pl.BlockSpec((classes, 1, groups, channels), lambda step: (0, step, 0, 0))
         bias_shape = (positions, heads * groups)
         sent_rows = positions + share_rows
+        scratch.append(scores)
     else:
-        rows_spec = pl.BlockSpec((1, *rows.shape[1:]), lambda step: (step, 0, 0))
+        rows_spec = step_spec(rows.shape)
         bias_shape = (groups, heads * positions)
         sent_rows = positions + groups + share_rows
     weights = kernel_weights(params)
@@ -297,25 +335,53 @@
         in_specs=[
             pl.BlockSpec(memory_space=pltpu.SMEM),
             rows_spec,
-            whole_spec(bias),
-            whole_spec(key_bias),
-            pl.BlockSpec((1, groups, channels), lambda step: (step, 0, 0)),
-            whole_spec(extra),
-            whole_spec(ride),
+            step_spec(grad.shape),
             *[whole_spec(x) for x in weights],
+            *[step_spec(x.shape) for x in steps],
+            *[whole_spec(x) for x in wholes],
         ],
         out_specs=[whole_spec(sent), whole_spec(bias_out)],
         out_shape=[sent, bias_out],
-        scratch_shapes=[
-            pltpu.VMEM((heads * groups, positions), jnp.float32),
-            pltpu.VMEM((heads * groups, positions), jnp.float32),
-            pltpu.VMEM((classes * share_rows, channels), jnp.float32),
-            pltpu.VMEM((positions, channels), jnp.float32),
-        ],
+        scratch_shapes=scratch,
         compiler_params=pltpu.CompilerParams(dimension_semantics=("arbitrary",)),
         interpret=INTERPRET,
         name="backward_second" if second else "backward_first",
-    )(own_class, rows, bias, key_bias, grad, extra, ride, *weights)
+    )(own_class, rows, grad, *weights, *steps, *wholes)
+
+
+def finish_kernel(share_rows, heads, arrived_ref, proj_ref, gate_ref, out_ref, bias_ref, gain_ref,
+                  shift_ref):
+    channels = out_ref.shape[1]
+    classes = arrived_ref.shape[0]
+    small = jnp.sum(arrived_ref[:, 2 * share_rows :].astype(jnp.float32), axis=0)
+    main = 5 * channels
+    for block in range(2):
+        start = block * share_rows
+        whole = arrived_ref[:, start : start + share_rows].astype(jnp.float32)
+        whole = whole.reshape(classes * share_rows, channels)
+        proj_ref[block] = whole[: 4 * channels]
+        out_ref[block] = whole[4 * channels : main]
+        gate_ref[block : block + 1] = whole[main : main + 1]
+        if block == 0:
+            late = whole[main + 1 : main + 1 + heads + 2]
+        parts = late if block else small[: heads + 2]
+        bias_ref[block] = parts[:heads]
+        gain_ref[block : block + 1] = parts[heads : heads + 1]
+        shift_ref[block : block + 1] = parts[heads + 1 : heads + 2]
+
+
+def finish_call(arrived, share_rows, heads, channels):
+    shapes = [(2, 4 * channels, channels), (2, channels), (2, channels, channels)]
+    shapes += [(2, heads, channels), (2, channels), (2, channels)]
+    vmem = pl.BlockSpec(memory_space=pltpu.VMEM)
+    return pl.pallas_call(
+        functools.partial(finish_kernel, share_rows, heads),
+        in_specs=[vmem],
+        out_specs=[vmem] * len(shapes),
+        out_shape=[jax.ShapeDtypeStruct(shape, jnp.float32) for shape in shapes],
+        interpret=INTERPRET,
+        name="finish_weights",
+    )(arrived)
 
 
 def padded_rows(x, rows):
@@ -387,7 +453,7 @@
     first_bias = arrived[:, :bias_rows].reshape(groups, head_total * positions)
     second_grad_query = arrived[:, bias_rows:].transpose(1, 0, 2)
 
-    after_query, after_normal = forward_call(
+    after_query, after_normal, *first_saved = forward_call(
         own_class, first_rows, first_bias, key_bias, params[0], params[1], head_total, positions
     )
     after_normed, after_inverse, _ = layer_norm(after_query, norm_gain[1], norm_shift[1])
@@ -416,15 +482,13 @@
     sent, bias_parts = backward_call(
         own_class,
         second_rows.reshape(classes, classes, groups, channels),
-        second_bias,
-        key_bias,
         second_grad_query,
-        jnp.zeros((8, LANES), jnp.float32),
-        None,
         params[1],
         head_total,
         positions,
         share_rows,
+        (),
+        (second_bias, key_bias),
     )
 
     def group_shares_of(arrived_shares):
@@ -475,15 +539,13 @@
     sent, bias_parts = backward_call(
         own_class,
         first_rows,
-        first_bias,
-        key_bias,
         after_grad_query,
-        extra,
-        end_query,
         params[0],
         head_total,
         positions,
         share_rows,
+        tuple(first_saved),
+        (extra, end_query),
     )
     arrived = exchanged(sent, HEAD)
     grad_normal = jnp.sum(arrived[:, :positions].astype(jnp.float32), axis=0)
@@ -544,26 +606,18 @@
         ],
         axis=0,
     )
-    arrived = exchanged(to_all(shared, HEAD), HEAD).astype(jnp.float32)
-    first_whole = arrived[:, :share_rows].reshape(-1, LANES)
-    second_whole = arrived[:, share_rows : 2 * share_rows].reshape(-1, LANES)
-    first_small = jnp.sum(arrived[:, 2 * share_rows : 2 * share_rows + small_rows], axis=0)
-    second_small = first_whole[main_rows : main_rows + small_rows]
-    proj_rows = 4 * channels
-
-    def both(first, second):
-        return jnp.stack([first, second])
-
+    arrived = exchanged(to_all(shared, HEAD), HEAD)
+    proj_grad, gate_grad, out_grad, bias_grad, gain_grad, shift_grad = finish_call(
+        arrived, share_rows, head_total, channels
+    )
     return (
         pair_grad,
-        both(first_whole[:proj_rows], second_whole[:proj_rows]).reshape(
-            2, 4, channels, -1
-        ),
-        both(first_whole[main_rows - 1], second_whole[main_rows - 1]),
-        both(first_whole[proj_rows : main_rows - 1], second_whole[proj_rows : main_rows - 1]),
-        both(first_small[:head_total].T, second_small[:head_total].T),
-        both(first_small[head_total], second_small[head_total]),
-        both(first_small[head_total + 1], second_small[head_total + 1]),
+        proj_grad.reshape(2, 4, channels, -1),
+        gate_grad,
+        out_grad,
+        bias_grad.transpose(0, 2, 1),
+        gain_grad,
+        shift_grad,
     )
 
 

time: 364 us -> 359 us (0.986)
  other arithmetic: 17.5 us -> 13.6 us
    pallas_call x2, Pallas kernels: 31.6 us -> 27.2 us  [backward_call(): pl.pallas_call(functools.partial(backward_kernel, heads, positions, secon...]
    another operation x6 -> x0, other arithmetic: 3.8 us -> none  [both(): return jnp.stack([first, second])]
where the time goes in v5:
time: 359 us; the launch traced here: 357 us
  waiting for transfers between devices  154 us (43%)
  starting transfers between devices  81.5 us (23%)
  blocking collectives  47.1 us (13%)
  Pallas kernels  43 us (12%)
  other arithmetic  13.6 us (4%)
  local copies, waits for them, and re-layouts  13.3 us (4%)
    all_to_all x10, waiting for transfers between devices, exchanged(): return lax.all_to_all(parts, axis, split_axis=0, concat_axis=0, tiled=True)  152 us
    all_to_all x10, starting transfers between devices, exchanged(): return lax.all_to_all(parts, axis, split_axis=0, concat_axis=0, tiled=True)  58.6 us
    all_to_all x1, blocking collectives, exchanged(): return lax.all_to_all(parts, axis, split_axis=0, concat_axis=0, tiled=True)  47.1 us
    pallas_call x2, Pallas kernels, backward_call(): pl.pallas_call(functools.partial(backward_kernel, heads, positions, secon...  27.2 us
    ppermute x7, starting transfers between devices, shifted_exchange(): pieces.append(lax.ppermute(parts[shift], HEAD, pairs))  22.9 us
    pallas_call x1, Pallas kernels, forward_call(): pl.pallas_call(functools.partial(forward_kernel, heads, positions), grid=...  11.2 us
  transfers between devices with their start and end apart: 17, of which 10 were waited for; matrix products, arithmetic and copies ran while one was open for 3% of the time, Pallas kernels for 1%

profile of v5, /device:TPU:1, one launch (start us, length us, event | category | flops | bytes accessed | tf_op | source)
XLA Modules:
  0.0 357.4 jit_solution(3832306904543820005)
XLA Ops:
  0.6 1.1 convert_reduce_fusion.2
  1.8 1.2 fusion.15
  3.0 1.3 slice_bitcast_fusion.13
  4.3 1.1 add_convert_fusion.1
  5.4 0.8 fusion.1
  6.3 0.8 pad_maximum_fusion
  7.1 19.8 %all-to-all-start = ((bf16[64,24,128]{2,1,0:T(8,128)(2,1)}), bf16[64,24,128]{2,1,0:T(8,128)(2,1)S(1)}, u32[]{:S(2)}, u32[]{:S(2)}) async-start(bf16[64,24,128]{2,1,0:T(8,128)(2,1)} %pad_maximum_fusion), calls=%async_computation | async-start | bytes 786432 | tf_op jit(solution)/shard_map/all_to_all | solution.py:24
  26.9 0.9 fusion.17
  28.8 2.3 collective-permute-start
  31.1 3.1 collective-permute-start.1
  34.2 4.5 %collective-permute-start.2 = (bf16[640,128]{1,0:T(8,128)(2,1)S(1)}, bf16[640,128]{1,0:T(8,128)(2,1)S(1)}, u32[]{:S(2)}, u32[]{:S(2)}) collective-permute-start(bf16[640,128]{1,0:T(8,128)(2,1)S(1)} %get-tuple-element.55), channel_id=1, source_target_pairs={{0,3},{1,4},{2,5},{3,6},{4,7},{5,0},{6,1},{7,2},{8,11},{9,12},{10,... | collective-permute-start | bytes 491528 | tf_op jit(solution)/shard_map/ppermute | solution.py:32
  38.8 3.6 %collective-permute-start.3 = (bf16[640,128]{1,0:T(8,128)(2,1)S(1)}, bf16[640,128]{1,0:T(8,128)(2,1)S(1)}, u32[]{:S(2)}, u32[]{:S(2)}) collective-permute-start(bf16[640,128]{1,0:T(8,128)(2,1)S(1)} %get-tuple-element.56), channel_id=1, source_target_pairs={{0,4},{1,5},{2,6},{3,7},{4,0},{5,1},{6,2},{7,3},{8,12},{9,13},{10,... | collective-permute-start | bytes 491528 | tf_op jit(solution)/shard_map/ppermute | solution.py:32
  42.4 3.9 %collective-permute-start.4 = (bf16[640,128]{1,0:T(8,128)(2,1)S(1)}, bf16[640,128]{1,0:T(8,128)(2,1)S(1)}, u32[]{:S(2)}, u32[]{:S(2)}) collective-permute-start(bf16[640,128]{1,0:T(8,128)(2,1)S(1)} %get-tuple-element.57), channel_id=1, source_target_pairs={{0,5},{1,6},{2,7},{3,0},{4,1},{5,2},{6,3},{7,4},{8,13},{9,14},{10,... | collective-permute-start | bytes 491528 | tf_op jit(solution)/shard_map/ppermute | solution.py:32
  47.6 3.1 collective-permute-start.5
  50.7 2.4 collective-permute-start.6
  55.1 2.0 collective-permute-done.6.refs_7_
  57.7 2.6 place_pieces.1.rows_ref
  61.2 11.2 %forward_rows.1 = (bf16[8,64,128]{2,1,0:T(8,128)(2,1)}, bf16[8,64,128]{2,1,0:T(8,128)(2,1)}, bf16[8,256,128]{2,1,0:T(8,128)(2,1)}, bf16[8,512,256]{2,1,0:T(8,128...) custom-call(s32[1]{0:T(128)} %bitcast.own_ref.class_ref, ...), custom_call_target="tpu_custom_call" | custom-call | tf_op jit(solution)/shard_map/forward_rows/pallas_call | solution.py:294
  72.4 5.6 %all-to-all-start.1 = ((bf16[8,64,128]{2,1,0:T(8,128)(2,1)}), bf16[8,64,128]{2,1,0:T(8,128)(2,1)S(1)}, u32[]{:S(2)}, u32[]{:S(2)}) async-start(bf16[8,64,128]{2,1,0:T(8,128)(2,1)} %get-tuple-element.25), calls=%async_computation.1 | async-start | bytes 262144 | tf_op jit(solution)/shard_map/all_to_all | solution.py:24
  78.0 1.1 fusion
  79.2 4.0 %all-to-all-done.1 = bf16[8,64,128]{2,1,0:T(8,128)(2,1)S(1)} async-done(((bf16[8,64,128]{2,1,0:T(8,128)(2,1)}), bf16[8,64,128]{2,1,0:T(8,128)(2,1)S(1)}, u32[]{:S(2)}, u32[]{:S(2)}) %all-to-all-start.1) | async-done | bytes 131104 | tf_op jit(solution)/shard_map/all_to_all | solution.py:24
  83.5 47.1 %all_to_all.55 = bf16[64,24,128]{2,1,0:T(8,128)(2,1)S(1)} all-to-all(bf16[64,24,128]{2,1,0:T(8,128)(2,1)S(1)} %pad_maximum_fusion.1), channel_id=1, replica_groups=mesh['row'=64,'head_0'=4,'head_1'=2] {'row'}, dimensions={0} | all-to-all | bytes 786432 | tf_op jit(solution)/shard_map/all_to_all | solution.py:24
  130.7 1.2 broadcast_in_dim.67
  131.9 3.6 all-to-all-start.3
  137.7 13.7 %all-to-all-done.3.rows_ref = bf16[8,8,64,128]{3,2,1,0:T(8,128)(2,1)S(1)} async-done(((bf16[8,8,64,128]{3,2,1,0:T(8,128)(2,1)}), bf16[8,8,64,128]{3,2,1,0:T(8,128)(2,1)S(1)}, u32[]{:S(2)}, u32[]{:S(2)}) %all-to-all-start.3) | async-done | bytes 1048608 | tf_op jit(solution)/shard_map/all_to_all | solution.py:24
  151.4 1.0 copy-done
  152.4 15.8 %backward_second.1 = (bf16[8,608,128]{2,1,0:T(8,128)(2,1)}, bf16[512,256]{1,0:T(8,128)(2,1)}) custom-call(s32[1]{0:T(128)} %bitcast.own_ref.class_ref, bf16[8,8,64,128]{3,2,1,0:T(8,128)(2,1)} %copy-done, bf16[8,64,128]{2,1,0:T(8,128)(2,1)} %bitcast.167, bf16[128,128]{1,0:T(8,128)(2,1)} %get-tuple-element.63.wq_ref, ...), custom_call_target="tpu_custom_call" | custom-call | tf_op jit(solution)/shard_map/backward_second/pallas_call | solution.py:332
  168.1 3.7 %all-to-all-start.4 = ((bf16[8,608,128]{2,1,0:T(8,128)(2,1)}), bf16[8,608,128]{2,1,0:T(8,128)(2,1)S(1)}, u32[]{:S(2)}, u32[]{:S(2)}) async-start(bf16[8,608,128]{2,1,0:T(8,128)(2,1)} %get-tuple-element.27), calls=%async_computation.4 | async-start | bytes 2490368 | tf_op jit(solution)/shard_map/all_to_all | solution.py:24
  172.1 19.6 %all-to-all-done.4 = bf16[8,608,128]{2,1,0:T(8,128)(2,1)S(1)} async-done(((bf16[8,608,128]{2,1,0:T(8,128)(2,1)}), bf16[8,608,128]{2,1,0:T(8,128)(2,1)S(1)}, u32[]{:S(2)}, u32[]{:S(2)}) %all-to-all-start.4) | async-done | bytes 1245216 | tf_op jit(solution)/shard_map/all_to_all | solution.py:24
  191.9 0.8 pad_maximum_fusion.2
  192.8 6.0 %all-to-all-start.5 = ((bf16[64,24,128]{2,1,0:T(8,128)(2,1)}), bf16[64,24,128]{2,1,0:T(8,128)(2,1)S(1)}, u32[]{:S(2)}, u32[]{:S(2)}) async-start(bf16[64,24,128]{2,1,0:T(8,128)(2,1)} %pad_maximum_fusion.2), calls=%async_computation.5 | async-start | bytes 786432 | tf_op jit(solution)/shard_map/all_to_all | solution.py:24
  199.2 28.4 %all-to-all-done.5 = bf16[64,24,128]{2,1,0:T(8,128)(2,1)S(1)} async-done(((bf16[64,24,128]{2,1,0:T(8,128)(2,1)}), bf16[64,24,128]{2,1,0:T(8,128)(2,1)S(1)}, u32[]{:S(2)}, u32[]{:S(2)}) %all-to-all-start.5) | async-done | bytes 393248 | tf_op jit(solution)/shard_map/all_to_all | solution.py:24
  228.4 3.6 all-to-all-start.6
  232.1 5.0 %all-to-all-done.6 = bf16[8,64,128]{2,1,0:T(8,128)(2,1)S(1)} async-done(((bf16[8,64,128]{2,1,0:T(8,128)(2,1)}), bf16[8,64,128]{2,1,0:T(8,128)(2,1)S(1)}, u32[]{:S(2)}, u32[]{:S(2)}) %all-to-all-start.6) | async-done | bytes 131104 | tf_op jit(solution)/shard_map/all_to_all | solution.py:24
  238.2 1.9 add_convert_fusion
  240.1 11.5 %backward_first.1 = (bf16[8,672,128]{2,1,0:T(8,128)(2,1)}, bf16[64,2048]{1,0:T(8,128)(2,1)}) custom-call(s32[1]{0:T(128)} %bitcast.own_ref.class_ref, bf16[8,640,128]{2,1,0:T(8,128)(2,1)} %place_pieces.1.rows_ref, bf16[8,64,128]{2,1,0:T(8,128)(2,1)} %get-tuple-element.49.grad_ref, bf16[128,128]{1,0:T(8,128)(2,1)} %get-tuple-element.67.wq_ref, ...), custom_call_target="tpu_custom_call" | custom-call | tf_op jit(solution)/shard_map/backward_first/pallas_call | solution.py:332
  251.6 3.7 %all-to-all-start.7 = ((bf16[8,672,128]{2,1,0:T(8,128)(2,1)}), bf16[8,672,128]{2,1,0:T(8,128)(2,1)S(1)}, u32[]{:S(2)}, u32[]{:S(2)}) async-start(bf16[8,672,128]{2,1,0:T(8,128)(2,1)} %get-tuple-element.33), calls=%async_computation.7 | async-start | bytes 2752512 | tf_op jit(solution)/shard_map/all_to_all | solution.py:24
  255.4 21.9 %all-to-all-done.7 = bf16[8,672,128]{2,1,0:T(8,128)(2,1)S(1)} async-done(((bf16[8,672,128]{2,1,0:T(8,128)(2,1)}), bf16[8,672,128]{2,1,0:T(8,128)(2,1)S(1)}, u32[]{:S(2)}, u32[]{:S(2)}) %all-to-all-start.7) | async-done | bytes 1376288 | tf_op jit(solution)/shard_map/all_to_all | solution.py:24
  277.5 0.8 pad_maximum_fusion.3
  278.2 4.7 %all-to-all-start.8 = ((bf16[64,24,128]{2,1,0:T(8,128)(2,1)}), bf16[64,24,128]{2,1,0:T(8,128)(2,1)S(1)}, u32[]{:S(2)}, u32[]{:S(2)}) async-start(bf16[64,24,128]{2,1,0:T(8,128)(2,1)} %pad_maximum_fusion.3), calls=%async_computation.8 | async-start | bytes 786432 | tf_op jit(solution)/shard_map/all_to_all | solution.py:24
  283.1 28.8 %all-to-all-done.8 = bf16[64,24,128]{2,1,0:T(8,128)(2,1)S(1)} async-done(((bf16[64,24,128]{2,1,0:T(8,128)(2,1)}), bf16[64,24,128]{2,1,0:T(8,128)(2,1)S(1)}, u32[]{:S(2)}, u32[]{:S(2)}) %all-to-all-start.8) | async-done | bytes 393248 | tf_op jit(solution)/shard_map/all_to_all | solution.py:24
  313.4 4.6 %all-to-all-start.9 = ((bf16[64,16,128]{2,1,0:T(8,128)(2,1)}), bf16[64,16,128]{2,1,0:T(8,128)(2,1)S(1)}, u32[]{:S(2)}, u32[]{:S(2)}) async-start(bf16[64,16,128]{2,1,0:T(8,128)(2,1)} %broadcast_in_dim.72), calls=%async_computation.9 | async-start | bytes 524288 | tf_op jit(solution)/shard_map/all_to_all | solution.py:24
  318.3 23.4 %all-to-all-done.9 = bf16[64,16,128]{2,1,0:T(8,128)(2,1)S(1)} async-done(((bf16[64,16,128]{2,1,0:T(8,128)(2,1)}), bf16[64,16,128]{2,1,0:T(8,128)(2,1)S(1)}, u32[]{:S(2)}, u32[]{:S(2)}) %all-to-all-start.9) | async-done | bytes 262176 | tf_op jit(solution)/shard_map/all_to_all | solution.py:24
  341.9 0.8 broadcast_in_dim.73
  342.7 3.5 all-to-all-start.10
  346.2 0.9 bitcast_add_fusion
  347.0 7.8 %all-to-all-done.10.arrived_ref = bf16[8,200,128]{2,1,0:T(8,128)(2,1)S(1)} async-done(((bf16[8,200,128]{2,1,0:T(8,128)(2,1)}), bf16[8,200,128]{2,1,0:T(8,128)(2,1)S(1)}, u32[]{:S(2)}, u32[]{:S(2)}) %all-to-all-start.10) | async-done | bytes 409632 | tf_op jit(solution)/shard_map/all_to_all | solution.py:24
  355.6 1.9 finish_weights.1
  (115 shorter events, 14.3 us)
Async XLA Ops:
  0.6 5.7 %copy-start.3 = (bf16[1,512,128]{2,1,0:T(8,128)(2,1)S(1)}, bf16[1,512,128]{2,1,0:T(8,128)(2,1)}, u32[]{:S(2)}) copy-start(bf16[1,512,128]{2,1,0:T(8,128)(2,1)} %param.10) | copy-start | bytes 393220
  1.7 25.1 %copy-start.1 = (bf16[1,512,128]{2,1,0:T(8,128)(2,1)S(1)}, bf16[1,512,128]{2,1,0:T(8,128)(2,1)}, u32[]{:S(2)}) copy-start(bf16[1,512,128]{2,1,0:T(8,128)(2,1)} %param.9) | copy-start | bytes 393220
  7.1 53.3 %all-to-all-start = ((bf16[64,24,128]{2,1,0:T(8,128)(2,1)}), bf16[64,24,128]{2,1,0:T(8,128)(2,1)S(1)}, u32[]{:S(2)}, u32[]{:S(2)}) async-start(bf16[64,24,128]{2,1,0:T(8,128)(2,1)} %pad_maximum_fusion), calls=%async_computation | async-start | bytes 786432 | tf_op jit(solution)/shard_map/all_to_all | solution.py:24
  28.0 18.3 %copy-start.16 = (bf16[2,128,128]{2,1,0:T(8,128)(2,1)S(1)}, bf16[2,128,128]{2,1,0:T(8,128)(2,1)}, u32[]{:S(2)}) copy-start(bf16[2,128,128]{2,1,0:T(8,128)(2,1)} %param.16) | copy-start | bytes 196612
  28.0 18.9 %copy-start.6 = (bf16[2,4,128,128]{3,2,1,0:T(8,128)(2,1)S(1)}, bf16[2,4,128,128]{3,2,1,0:T(8,128)(2,1)}, u32[]{:S(2)}) copy-start(bf16[2,4,128,128]{3,2,1,0:T(8,128)(2,1)} %param.14) | copy-start | bytes 786436
  28.0 19.6 %copy-start.18 = (s32[512]{0:T(512)S(1)}, s32[512]{0:T(512)}, u32[]{:S(2)}) copy-start(s32[512]{0:T(512)} %param.11) | copy-start | bytes 6148
  28.0 25.1 %copy-start.19 = (f32[2,128]{1,0:T(2,128)S(1)}, f32[2,128]{1,0:T(2,128)}, u32[]{:S(2)}) copy-start(f32[2,128]{1,0:T(2,128)} %param.15) | copy-start | bytes 3076
  28.8 18.8 %collective-permute-start = (bf16[640,128]{1,0:T(8,128)(2,1)S(1)}, bf16[640,128]{1,0:T(8,128)(2,1)S(1)}, u32[]{:S(2)}, u32[]{:S(2)}) collective-permute-start(bf16[640,128]{1,0:T(8,128)(2,1)S(1)} %get-tuple-element.53), channel_id=1, source_target_pairs={{0,1},{1,2},{2,3},{3,4},{4,5},{5,6},{6,7},{7,0},{8,9},{9,10},{10,1... | collective-permute-start | bytes 491528 | tf_op jit(solution)/shard_map/ppermute | solution.py:32
  31.1 19.6 %collective-permute-start.1 = (bf16[640,128]{1,0:T(8,128)(2,1)S(1)}, bf16[640,128]{1,0:T(8,128)(2,1)S(1)}, u32[]{:S(2)}, u32[]{:S(2)}) collective-permute-start(bf16[640,128]{1,0:T(8,128)(2,1)S(1)} %get-tuple-element.54), channel_id=1, source_target_pairs={{0,2},{1,3},{2,4},{3,5},{4,6},{5,7},{6,0},{7,1},{8,10},{9,11},{10,... | collective-permute-start | bytes 491528 | tf_op jit(solution)/shard_map/ppermute | solution.py:32
  34.2 20.8 %collective-permute-start.2 = (bf16[640,128]{1,0:T(8,128)(2,1)S(1)}, bf16[640,128]{1,0:T(8,128)(2,1)S(1)}, u32[]{:S(2)}, u32[]{:S(2)}) collective-permute-start(bf16[640,128]{1,0:T(8,128)(2,1)S(1)} %get-tuple-element.55), channel_id=1, source_target_pairs={{0,3},{1,4},{2,5},{3,6},{4,7},{5,0},{6,1},{7,2},{8,11},{9,12},{10,... | collective-permute-start | bytes 491528 | tf_op jit(solution)/shard_map/ppermute | solution.py:32
  38.8 16.3 %collective-permute-start.3 = (bf16[640,128]{1,0:T(8,128)(2,1)S(1)}, bf16[640,128]{1,0:T(8,128)(2,1)S(1)}, u32[]{:S(2)}, u32[]{:S(2)}) collective-permute-start(bf16[640,128]{1,0:T(8,128)(2,1)S(1)} %get-tuple-element.56), channel_id=1, source_target_pairs={{0,4},{1,5},{2,6},{3,7},{4,0},{5,1},{6,2},{7,3},{8,12},{9,13},{10,... | collective-permute-start | bytes 491528 | tf_op jit(solution)/shard_map/ppermute | solution.py:32
  42.4 12.7 %collective-permute-start.4 = (bf16[640,128]{1,0:T(8,128)(2,1)S(1)}, bf16[640,128]{1,0:T(8,128)(2,1)S(1)}, u32[]{:S(2)}, u32[]{:S(2)}) collective-permute-start(bf16[640,128]{1,0:T(8,128)(2,1)S(1)} %get-tuple-element.57), channel_id=1, source_target_pairs={{0,5},{1,6},{2,7},{3,0},{4,1},{5,2},{6,3},{7,4},{8,13},{9,14},{10,... | collective-permute-start | bytes 491528 | tf_op jit(solution)/shard_map/ppermute | solution.py:32
  47.6 9.5 %copy-start.9 = (bf16[640,128]{1,0:T(8,128)(2,1)}, bf16[640,128]{1,0:T(8,128)(2,1)S(1)}, u32[]{:S(2)}) copy-start(bf16[640,128]{1,0:T(8,128)(2,1)S(1)} %collective-permute-done.refs_1_) | copy-start | bytes 491524
  47.6 7.5 %collective-permute-start.5 = (bf16[640,128]{1,0:T(8,128)(2,1)S(1)}, bf16[640,128]{1,0:T(8,128)(2,1)S(1)}, u32[]{:S(2)}, u32[]{:S(2)}) collective-permute-start(bf16[640,128]{1,0:T(8,128)(2,1)S(1)} %get-tuple-element.58), channel_id=1, source_target_pairs={{0,6},{1,7},{2,0},{3,1},{4,2},{5,3},{6,4},{7,5},{8,14},{9,15},{10,... | collective-permute-start | bytes 491528 | tf_op jit(solution)/shard_map/ppermute | solution.py:32
  50.7 6.4 %copy-start.10 = (bf16[640,128]{1,0:T(8,128)(2,1)}, bf16[640,128]{1,0:T(8,128)(2,1)S(1)}, u32[]{:S(2)}) copy-start(bf16[640,128]{1,0:T(8,128)(2,1)S(1)} %collective-permute-done.1.refs_2_) | copy-start | bytes 491524
  50.7 6.4 %collective-permute-start.6 = (bf16[640,128]{1,0:T(8,128)(2,1)S(1)}, bf16[640,128]{1,0:T(8,128)(2,1)S(1)}, u32[]{:S(2)}, u32[]{:S(2)}) collective-permute-start(bf16[640,128]{1,0:T(8,128)(2,1)S(1)} %get-tuple-element.51), channel_id=1, source_target_pairs={{0,7},{1,0},{2,1},{3,2},{4,3},{5,4},{6,5},{7,6},{8,15},{9,8},{10,9... | collective-permute-start | bytes 491528 | tf_op jit(solution)/shard_map/ppermute | solution.py:32
  55.1 2.0 copy-start.11
  55.1 2.0 copy-start.12
  55.1 2.0 copy-start.13
  55.1 2.0 copy-start.14
  57.1 0.7 copy-start.15
  60.4 17.6 %copy-start.17 = (bf16[2,128,4]{1,2,0:T(4,128)(2,1)S(1)}, bf16[2,128,4]{1,2,0:T(4,128)(2,1)}, u32[]{:S(2)}) copy-start(bf16[2,128,4]{1,2,0:T(4,128)(2,1)} %param.17) | copy-start | bytes 6148
  72.4 10.9 %all-to-all-start.1 = ((bf16[8,64,128]{2,1,0:T(8,128)(2,1)}), bf16[8,64,128]{2,1,0:T(8,128)(2,1)S(1)}, u32[]{:S(2)}, u32[]{:S(2)}) async-start(bf16[8,64,128]{2,1,0:T(8,128)(2,1)} %get-tuple-element.25), calls=%async_computation.1 | async-start | bytes 262144 | tf_op jit(solution)/shard_map/all_to_all | solution.py:24
  131.9 19.5 %all-to-all-start.3 = ((bf16[8,8,64,128]{3,2,1,0:T(8,128)(2,1)}), bf16[8,8,64,128]{3,2,1,0:T(8,128)(2,1)S(1)}, u32[]{:S(2)}, u32[]{:S(2)}) async-start(bf16[8,8,64,128]{3,2,1,0:T(8,128)(2,1)} %broadcast_in_dim.67), calls=%async_computation.3 | async-start | bytes 2097152 | tf_op jit(solution)/shard_map/all_to_all | solution.py:24
  151.4 1.0 copy-start
  168.1 3.7 %copy-start.8 = (bf16[512,256]{1,0:T(8,128)(2,1)S(1)}, bf16[512,256]{1,0:T(8,128)(2,1)}, u32[]{:S(2)}) copy-start(bf16[512,256]{1,0:T(8,128)(2,1)} %get-tuple-element.26) | copy-start | bytes 786436
  168.1 23.6 %all-to-all-start.4 = ((bf16[8,608,128]{2,1,0:T(8,128)(2,1)}), bf16[8,608,128]{2,1,0:T(8,128)(2,1)S(1)}, u32[]{:S(2)}, u32[]{:S(2)}) async-start(bf16[8,608,128]{2,1,0:T(8,128)(2,1)} %get-tuple-element.27), calls=%async_computation.4 | async-start | bytes 2490368 | tf_op jit(solution)/shard_map/all_to_all | solution.py:24
  172.1 26.6 %copy-start.5 = (bf16[8,64,128]{2,1,0:T(8,128)(2,1)S(1)}, bf16[8,64,128]{2,1,0:T(8,128)(2,1)}, u32[]{:S(2)}) copy-start(bf16[8,64,128]{2,1,0:T(8,128)(2,1)} %get-tuple-element.24) | copy-start | bytes 393220
  191.9 40.0 %copy-start.4 = (bf16[8,64,128]{2,1,0:T(8,128)(2,1)S(1)}, bf16[8,64,128]{2,1,0:T(8,128)(2,1)}, u32[]{:S(2)}) copy-start(bf16[8,64,128]{2,1,0:T(8,128)(2,1)} %get-tuple-element.25) | copy-start | bytes 393220
  192.8 34.8 %all-to-all-start.5 = ((bf16[64,24,128]{2,1,0:T(8,128)(2,1)}), bf16[64,24,128]{2,1,0:T(8,128)(2,1)S(1)}, u32[]{:S(2)}, u32[]{:S(2)}) async-start(bf16[64,24,128]{2,1,0:T(8,128)(2,1)} %pad_maximum_fusion.2), calls=%async_computation.5 | async-start | bytes 786432 | tf_op jit(solution)/shard_map/all_to_all | solution.py:24
  228.4 8.8 %all-to-all-start.6 = ((bf16[8,64,128]{2,1,0:T(8,128)(2,1)}), bf16[8,64,128]{2,1,0:T(8,128)(2,1)S(1)}, u32[]{:S(2)}, u32[]{:S(2)}) async-start(bf16[8,64,128]{2,1,0:T(8,128)(2,1)} %bitcast.141), calls=%async_computation.6 | async-start | bytes 262144 | tf_op jit(solution)/shard_map/all_to_all | solution.py:24
  251.6 3.8 %copy-start.7 = (bf16[64,2048]{1,0:T(8,128)(2,1)S(1)}, bf16[64,2048]{1,0:T(8,128)(2,1)}, u32[]{:S(2)}) copy-start(bf16[64,2048]{1,0:T(8,128)(2,1)} %get-tuple-element.34) | copy-start | bytes 786436
  251.6 25.7 %all-to-all-start.7 = ((bf16[8,672,128]{2,1,0:T(8,128)(2,1)}), bf16[8,672,128]{2,1,0:T(8,128)(2,1)S(1)}, u32[]{:S(2)}, u32[]{:S(2)}) async-start(bf16[8,672,128]{2,1,0:T(8,128)(2,1)} %get-tuple-element.33), calls=%async_computation.7 | async-start | bytes 2752512 | tf_op jit(solution)/shard_map/all_to_all | solution.py:24
  278.2 33.7 %all-to-all-start.8 = ((bf16[64,24,128]{2,1,0:T(8,128)(2,1)}), bf16[64,24,128]{2,1,0:T(8,128)(2,1)S(1)}, u32[]{:S(2)}, u32[]{:S(2)}) async-start(bf16[64,24,128]{2,1,0:T(8,128)(2,1)} %pad_maximum_fusion.3), calls=%async_computation.8 | async-start | bytes 786432 | tf_op jit(solution)/shard_map/all_to_all | solution.py:24
  313.4 28.3 %all-to-all-start.9 = ((bf16[64,16,128]{2,1,0:T(8,128)(2,1)}), bf16[64,16,128]{2,1,0:T(8,128)(2,1)S(1)}, u32[]{:S(2)}, u32[]{:S(2)}) async-start(bf16[64,16,128]{2,1,0:T(8,128)(2,1)} %broadcast_in_dim.72), calls=%async_computation.9 | async-start | bytes 524288 | tf_op jit(solution)/shard_map/all_to_all | solution.py:24
  342.7 12.1 %all-to-all-start.10 = ((bf16[8,200,128]{2,1,0:T(8,128)(2,1)}), bf16[8,200,128]{2,1,0:T(8,128)(2,1)S(1)}, u32[]{:S(2)}, u32[]{:S(2)}) async-start(bf16[8,200,128]{2,1,0:T(8,128)(2,1)} %broadcast_in_dim.73), calls=%async_computation.10 | async-start | bytes 819200 | tf_op jit(solution)/shard_map/all_to_all | solution.py:24
  354.8 0.8 copy-start.2

commit v6 on v5

--- a/solution.py
+++ b/solution.py
@@ -18,6 +18,7 @@
 MASKED = 1000000000.0
 LANES = 128
 INTERPRET = False
+ROWS = 4
 
 
 def exchanged(parts, axis):
@@ -25,16 +26,12 @@
 
 
 def shifted_exchange(parts):
-    count = parts.shape[0]
+    count = len(parts)
     pieces = [parts[0]]
     for shift in range(1, count):
         pairs = [(at, (at + shift) % count) for at in range(count)]
         pieces.append(lax.ppermute(parts[shift], HEAD, pairs))
     return pieces
-
-
-def rolled(x, by):
-    return lax.dynamic_slice_in_dim(jnp.concatenate([x, x]), by, x.shape[0], axis=0)
 
 
 def place_kernel(own_ref, *refs):
@@ -118,7 +115,7 @@
     gate = jax.nn.sigmoid(matmul(xq, wg, 1, 0) + gate_offset)
     logits = matmul(queries, keys, 1, 1) + bias
     weights = jnp.exp(logits - jnp.max(logits, axis=1, keepdims=True))
-    probs = weights / jnp.sum(weights, axis=1, keepdims=True)
+    probs = weights * (1.0 / jnp.sum(weights, axis=1, keepdims=True))
     probs_half = probs.astype(jnp.bfloat16)
     attended = picked_heads(matmul(probs_half, values, 1, 0), heads)
     return (queries, pairs, probs, gate, attended)
@@ -139,24 +136,25 @@
     def _():
         full_bias[...] = split_bias(bias_ref[...], mask_ref[...], heads)
 
-    x = rows_ref[0, :positions]
-    start = pl.multiple_of(class_ref[0] * groups, groups)
-    xq = rows_ref[0, pl.ds(start, groups)]
-    queries, pairs, probs, gate, attended = attention(
-        x, xq, full_bias[...], wq_ref[...], wkv_ref[...], wg_ref[...], gate_ref[...], heads
-    )
-    queries_ref[0] = queries
-    pairs_ref[0] = pairs
-    probs_ref[0] = probs
-    gates_ref[0] = gate
-    attended_ref[0] = attended
-    gated = (gate * attended).astype(jnp.bfloat16)
-    update = matmul(gated, wo_ref[...], 1, 0).astype(jnp.bfloat16)
-    pair = rows_ref[0, positions : positions + groups]
-    after = (pair.astype(jnp.float32) + update.astype(jnp.float32)).astype(jnp.bfloat16)
-    after_ref[0] = after
-    _, _, normal = layer_norm(after, gain_ref[...], shift_ref[...])
-    normal_ref[0] = normal
+    for row in range(after_ref.shape[0]):
+        x = rows_ref[row, :positions]
+        start = pl.multiple_of(class_ref[0] * groups, groups)
+        xq = rows_ref[row, pl.ds(start, groups)]
+        queries, pairs, probs, gate, attended = attention(
+            x, xq, full_bias[...], wq_ref[...], wkv_ref[...], wg_ref[...], gate_ref[...], heads
+        )
+        queries_ref[row] = queries
+        pairs_ref[row] = pairs
+        probs_ref[row] = probs
+        gates_ref[row] = gate
+        attended_ref[row] = attended
+        gated = (gate * attended).astype(jnp.bfloat16)
+        update = matmul(gated, wo_ref[...], 1, 0).astype(jnp.bfloat16)
+        pair = rows_ref[row, positions : positions + groups]
+        after = (pair.astype(jnp.float32) + update.astype(jnp.float32)).astype(jnp.bfloat16)
+        after_ref[row] = after
+        _, _, normal = layer_norm(after, gain_ref[...], shift_ref[...])
+        normal_ref[row] = normal
 
 
 def backward_kernel(heads, positions, second, share_rows, class_ref, rows_ref, grad_ref, wq_ref,
@@ -187,59 +185,61 @@
         if not second:
             weight_sum[5 * channels : 5 * channels + 8] = extra_ref[...]
 
-    if second:
-        x = rows_ref[:, 0].reshape(positions, channels)
-        xq = rows_ref[pl.ds(own_class, 1), 0].reshape(groups, channels)
-    else:
-        x = rows_ref[0, :positions]
-        xq = rows_ref[0, pl.ds(pl.multiple_of(own_class * groups, groups), groups)]
-    if second:
-        queries, pairs, probs, gate, attended = attention(
-            x, xq, full_bias[...], wq_ref[...], wkv_ref[...], wg_ref[...], gate_ref[...], heads
+    for row in range(grad_ref.shape[0]):
+        index = step * grad_ref.shape[0] + row
+        if second:
+            x = rows_ref[:, row].reshape(positions, channels)
+            xq = rows_ref[pl.ds(own_class, 1), row].reshape(groups, channels)
+        else:
+            x = rows_ref[row, :positions]
+            xq = rows_ref[row, pl.ds(pl.multiple_of(own_class * groups, groups), groups)]
+        if second:
+            queries, pairs, probs, gate, attended = attention(
+                x, xq, full_bias[...], wq_ref[...], wkv_ref[...], wg_ref[...], gate_ref[...], heads
+            )
+        else:
+            queries, pairs, probs, gate, attended = (
+                ref[row] for ref in (queries_ref, pairs_ref, probs_ref, gates_ref, attended_ref)
+            )
+        keys = pairs[:, :inner]
+        values = pairs[:, inner:]
+        probs_half = probs.astype(jnp.bfloat16)
+        scale = 1.0 / math.sqrt(inner // heads)
+        grad = grad_ref[row]
+        gated = (gate * attended).astype(jnp.bfloat16)
+        grad_gated = matmul(grad, wo_ref[...], 1, 1)
+        grad_att = (grad_gated * gate).astype(jnp.bfloat16).astype(jnp.float32)
+        grad_pre = (grad_gated * attended * gate * (1.0 - gate)).astype(jnp.bfloat16)
+        grad_heads = spread_heads(grad_att, heads)
+        grad_probs = matmul(grad_heads, values, 1, 1)
+        grad_logits = probs * (grad_probs - jnp.sum(probs * grad_probs, axis=1, keepdims=True))
+        bias_sum[...] += grad_logits
+        logits_half = grad_logits.astype(jnp.bfloat16)
+        grad_queries = (picked_heads(matmul(logits_half, keys, 1, 0), heads) * scale).astype(
+            jnp.bfloat16
         )
-    else:
-        queries, pairs, probs, gate, attended = (
-            ref[0] for ref in (queries_ref, pairs_ref, probs_ref, gates_ref, attended_ref)
+        grad_keys = matmul(logits_half, queries, 0, 0).astype(jnp.bfloat16)
+        grad_values = matmul(probs_half, grad_heads, 0, 0).astype(jnp.bfloat16)
+        grad_pairs = jnp.concatenate([grad_keys, grad_values], axis=1)
+        share[row] = matmul(grad_pairs, wkv_ref[...], 1, 1)
+        query_side = matmul(grad_queries, wq_ref[...], 1, 1) + matmul(grad_pre, wg_ref[...], 1, 1)
+        own_rows = pl.ds(pl.multiple_of(own_class * groups, groups), groups)
+        share[row, own_rows] = share[row, own_rows] + query_side
+        partial = share[row].astype(jnp.bfloat16)
+        if second:
+            place = pl.ds(pl.multiple_of(index * groups, groups), groups)
+            sent_ref[:, place] = partial.reshape(classes, groups, channels)
+        else:
+            sent_ref[pl.ds(index, 1), :positions] = partial[None]
+        pair_sums = matmul(x, grad_pairs, 0, 0)
+        weight_sum[:channels] += matmul(xq, grad_queries, 0, 0)
+        weight_sum[channels : 2 * channels] += pair_sums[:, :inner]
+        weight_sum[2 * channels : 3 * channels] += pair_sums[:, inner:]
+        weight_sum[3 * channels : 4 * channels] += matmul(xq, grad_pre, 0, 0)
+        weight_sum[4 * channels : 5 * channels] += matmul(gated, grad, 0, 0)
+        weight_sum[5 * channels : 5 * channels + 1] += jnp.sum(
+            grad_pre.astype(jnp.float32), axis=0, keepdims=True
         )
-    keys = pairs[:, :inner]
-    values = pairs[:, inner:]
-    probs_half = probs.astype(jnp.bfloat16)
-    scale = 1.0 / math.sqrt(inner // heads)
-    grad = grad_ref[0]
-    gated = (gate * attended).astype(jnp.bfloat16)
-    grad_gated = matmul(grad, wo_ref[...], 1, 1)
-    grad_att = (grad_gated * gate).astype(jnp.bfloat16).astype(jnp.float32)
-    grad_pre = (grad_gated * attended * gate * (1.0 - gate)).astype(jnp.bfloat16)
-    grad_heads = spread_heads(grad_att, heads)
-    grad_probs = matmul(grad_heads, values, 1, 1)
-    grad_logits = probs * (grad_probs - jnp.sum(probs * grad_probs, axis=1, keepdims=True))
-    bias_sum[...] += grad_logits
-    logits_half = grad_logits.astype(jnp.bfloat16)
-    grad_queries = (picked_heads(matmul(logits_half, keys, 1, 0), heads) * scale).astype(
-        jnp.bfloat16
-    )
-    grad_keys = matmul(logits_half, queries, 0, 0).astype(jnp.bfloat16)
-    grad_values = matmul(probs_half, grad_heads, 0, 0).astype(jnp.bfloat16)
-    grad_pairs = jnp.concatenate([grad_keys, grad_values], axis=1)
-    share[...] = matmul(grad_pairs, wkv_ref[...], 1, 1)
-    query_side = matmul(grad_queries, wq_ref[...], 1, 1) + matmul(grad_pre, wg_ref[...], 1, 1)
-    own_rows = pl.ds(pl.multiple_of(own_class * groups, groups), groups)
-    share[own_rows] = share[own_rows] + query_side
-    partial = share[...].astype(jnp.bfloat16)
-    if second:
-        place = pl.ds(pl.multiple_of(step * groups, groups), groups)
-        sent_ref[:, place] = partial.reshape(classes, groups, channels)
-    else:
-        sent_ref[pl.ds(step, 1), :positions] = partial[None]
-    pair_sums = matmul(x, grad_pairs, 0, 0)
-    weight_sum[:channels] += matmul(xq, grad_queries, 0, 0)
-    weight_sum[channels : 2 * channels] += pair_sums[:, :inner]
-    weight_sum[2 * channels : 3 * channels] += pair_sums[:, inner:]
-    weight_sum[3 * channels : 4 * channels] += matmul(xq, grad_pre, 0, 0)
-    weight_sum[4 * channels : 5 * channels] += matmul(gated, grad, 0, 0)
-    weight_sum[5 * channels : 5 * channels + 1] += jnp.sum(
-        grad_pre.astype(jnp.float32), axis=0, keepdims=True
-    )
 
     @pl.when(step == pl.num_programs(0) - 1)
     def _():
@@ -266,8 +266,59 @@
     return (projection[0], joined, projection[3], out_proj, gate_offset[None])
 
 
+def start_kernel(heads, own_ref, pair_ref, class_cot_ref, cot_ref, gain_ref, shift_ref, wb_ref,
+                 row_ref, normed_ref, inverse_ref, *piece_refs):
+    classes, groups, channels = pair_ref.shape
+    positions = classes * groups
+    pair = pair_ref[...].reshape(positions, channels)
+    normed, inverse, normal = layer_norm(pair, gain_ref[...], shift_ref[...])
+    normed_ref[...] = normed
+    inverse_ref[...] = inverse
+    bias = matmul(wb_ref[...], normal, 0, 1)
+    tiles = positions // min(positions, LANES)
+    width = positions // tiles
+    lines = [
+        bias[head : head + 1, tile * width : (tile + 1) * width]
+        for head in range(heads)
+        for tile in range(tiles)
+    ]
+    if width < LANES:
+        lines = [jnp.concatenate(lines, axis=1)]
+    packed = jnp.concatenate(lines, axis=0).astype(jnp.bfloat16)
+    rows = packed.shape[0]
+    row_ref[:, :rows] = jnp.broadcast_to(packed[None], (groups, *packed.shape))
+    row_ref[:, rows:] = cot_ref[...]
+    for shift, piece_ref in enumerate(piece_refs):
+        peer = lax.rem(own_ref[0] + shift, classes)
+        piece_ref[:positions] = normal
+        piece_ref[positions : positions + groups] = pair_ref[pl.ds(peer, 1)][0]
+        piece_ref[positions + groups :] = class_cot_ref[pl.ds(peer, 1)][0]
+
+
+def start_call(own_class, pair, class_cot, cot, params, heads):
+    classes, groups, channels = pair.shape
+    positions = classes * groups
+    rows = heads * positions // LANES + classes
+    half = jnp.bfloat16
+    vmem = pl.BlockSpec(memory_space=pltpu.VMEM)
+    results = [
+        jax.ShapeDtypeStruct((groups, rows, channels), half),
+        jax.ShapeDtypeStruct((positions, channels), jnp.float32),
+        jax.ShapeDtypeStruct((positions, 1), jnp.float32),
+    ]
+    results += [jax.ShapeDtypeStruct((positions + 2 * groups, channels), half)] * classes
+    return pl.pallas_call(
+        functools.partial(start_kernel, heads),
+        in_specs=[pl.BlockSpec(memory_space=pltpu.SMEM)] + [vmem] * 6,
+        out_specs=[vmem] * len(results),
+        out_shape=results,
+        interpret=INTERPRET,
+        name="start_row",
+    )(own_class, pair, class_cot, cot, params[0][None], params[1][None], params[5])
+
+
 def step_spec(shape):
-    return pl.BlockSpec((1, *shape[1:]), lambda step, n=len(shape): (step,) + (0,) * (n - 1))
+    return pl.BlockSpec((ROWS, *shape[1:]), lambda step, n=len(shape): (step,) + (0,) * (n - 1))
 
 
 def forward_call(own_class, rows, bias, key_bias, params, next_params, heads, positions):
@@ -293,7 +344,7 @@
     ]
     return pl.pallas_call(
         functools.partial(forward_kernel, heads, positions),
-        grid=(classes,),
+        grid=(classes // ROWS,),
         in_specs=[
             pl.BlockSpec(memory_space=pltpu.SMEM),
             step_spec(rows.shape),
@@ -315,10 +366,10 @@
     scratch = [
         scores,
         pltpu.VMEM((classes * share_rows, channels), jnp.float32),
-        pltpu.VMEM((positions, channels), jnp.float32),
+        pltpu.VMEM((ROWS, positions, channels), jnp.float32),
     ]
     if second:
-        rows_spec = pl.BlockSpec((classes, 1, groups, channels), lambda step: (0, step, 0, 0))
+        rows_spec = pl.BlockSpec((classes, ROWS, groups, channels), lambda step: (0, step, 0, 0))
         bias_shape = (positions, heads * groups)
         sent_rows = positions + share_rows
         scratch.append(scores)
@@ -331,7 +382,7 @@
     bias_out = jax.ShapeDtypeStruct(bias_shape, jnp.bfloat16)
     return pl.pallas_call(
         functools.partial(backward_kernel, heads, positions, second, share_rows),
-        grid=(classes,),
+        grid=(classes // ROWS,),
         in_specs=[
             pl.BlockSpec(memory_space=pltpu.SMEM),
             rows_spec,
@@ -429,27 +480,20 @@
     ]
 
     own_pair = pair_input.reshape(groups, classes, channels).transpose(1, 0, 2)
-    normed_own, inverse_own, normal_own = layer_norm(own_pair, norm_gain[0], norm_shift[0])
-    normal_flat = normal_own.reshape(positions, channels)
-    bias_own = jnp.einsum(
-        "nc,ch->hn", normal_flat, bias_weights[0], preferred_element_type=jnp.float32
-    ).astype(half)
     own_cotangent = cotangent.reshape(groups, classes, channels)
-    class_parts = jnp.concatenate([own_pair, own_cotangent.transpose(1, 0, 2)], axis=1)
-    class_parts = rolled(class_parts, own_class[0])
-    pieces = shifted_exchange(jnp.concatenate([to_all(normal_flat, HEAD), class_parts], axis=1))
+    row_parts, normed_flat, inverse_flat, *parts = start_call(
+        own_class,
+        own_pair,
+        own_cotangent.transpose(1, 0, 2),
+        own_cotangent,
+        params[0],
+        head_total,
+    )
+    normal_flat = parts[0][:positions]
+    pieces = shifted_exchange(parts)
     first_rows = placed(own_class, pieces)
     cotangent_query = first_rows[:, positions + groups :]
-    arrived = exchanged(
-        jnp.concatenate(
-            [
-                to_all(bias_own.reshape(bias_rows, LANES), "row"),
-                own_cotangent,
-            ],
-            axis=1,
-        ),
-        "row",
-    )
+    arrived = exchanged(row_parts, "row")
     first_bias = arrived[:, :bias_rows].reshape(groups, head_total * positions)
     second_grad_query = arrived[:, bias_rows:].transpose(1, 0, 2)
 
@@ -572,9 +616,8 @@
     grad_normal = grad_normal + jnp.einsum(
         "hn,ch->nc", bias_half, bias_weights[0], preferred_element_type=jnp.float32
     )
-    normed_flat = normed_own.reshape(positions, channels)
     start_grad = norm_backward(
-        grad_normal, normed_flat, inverse_own.reshape(positions, 1), norm_gain[0]
+        grad_normal, normed_flat, inverse_flat, norm_gain[0]
     )
     moved_grad = (end_own.astype(jnp.float32) + start_grad.reshape(end_own.shape)).transpose(1, 0, 2)
     pair_grad = cotangent.astype(jnp.float32) + moved_grad.reshape(1, positions, channels)

time: 359 us -> 356 us (level)
  other arithmetic: 13.6 us -> 7.9 us
  local copies, waits for them, and re-layouts: 13.3 us -> 17.6 us
where the time goes in v6:
time: 356 us; the launch traced here: 355 us
  waiting for transfers between devices  154 us (43%)
  starting transfers between devices  81.8 us (23%)
  blocking collectives  47.1 us (13%)
  Pallas kernels  42.5 us (12%)
  local copies, waits for them, and re-layouts  17.6 us (5%)
  other arithmetic  7.9 us (2%)
    all_to_all x10, waiting for transfers between devices, exchanged(): return lax.all_to_all(parts, axis, split_axis=0, concat_axis=0, tiled=True)  152 us
    all_to_all x10, starting transfers between devices, exchanged(): return lax.all_to_all(parts, axis, split_axis=0, concat_axis=0, tiled=True)  58.9 us
    all_to_all x1, blocking collectives, exchanged(): return lax.all_to_all(parts, axis, split_axis=0, concat_axis=0, tiled=True)  47.1 us
    pallas_call x2, Pallas kernels, backward_call(): pl.pallas_call(functools.partial(backward_kernel, heads, positions, secon...  25.2 us
    ppermute x7, starting transfers between devices, shifted_exchange(): pieces.append(lax.ppermute(parts[shift], HEAD, pairs))  22.9 us
    pallas_call x1, Pallas kernels, forward_call(): pl.pallas_call(functools.partial(forward_kernel, heads, positions), grid=...  10 us
  transfers between devices with their start and end apart: 17, of which 10 were waited for; matrix products, arithmetic and copies ran while one was open for 3% of the time, Pallas kernels for 1%

profile of v6, /device:TPU:1, one launch (start us, length us, event | category | flops | bytes accessed | tf_op | source)
XLA Modules:
  0.0 354.8 jit_solution(11545133735246644219)
XLA Ops:
  2.1 1.6 copy.71
  3.7 1.6 copy.44.class_cot_ref
  5.3 1.4 slice_bitcast_fusion.12
  6.6 2.8 start_row.1
  9.4 19.9 %all-to-all-start = ((bf16[64,24,128]{2,1,0:T(8,128)(2,1)}), bf16[64,24,128]{2,1,0:T(8,128)(2,1)S(1)}, u32[]{:S(2)}, u32[]{:S(2)}) async-start(bf16[64,24,128]{2,1,0:T(8,128)(2,1)} %get-tuple-element.43), calls=%async_computation | async-start | bytes 786432 | tf_op jit(solution)/shard_map/all_to_all | solution.py:25
  29.3 2.3 collective-permute-start
  31.6 3.1 collective-permute-start.1
  34.8 4.5 %collective-permute-start.2 = (bf16[640,128]{1,0:T(8,128)(2,1)}, bf16[640,128]{1,0:T(8,128)(2,1)S(1)}, u32[]{:S(2)}, u32[]{:S(2)}) collective-permute-start(bf16[640,128]{1,0:T(8,128)(2,1)} %get-tuple-element.38), channel_id=1, source_target_pairs={{0,3},{1,4},{2,5},{3,6},{4,7},{5,0},{6,1},{7,2},{8,11},{9,12},{10,... | collective-permute-start | bytes 491528 | tf_op jit(solution)/shard_map/ppermute | solution.py:33
  39.3 3.6 %collective-permute-start.3 = (bf16[640,128]{1,0:T(8,128)(2,1)}, bf16[640,128]{1,0:T(8,128)(2,1)S(1)}, u32[]{:S(2)}, u32[]{:S(2)}) collective-permute-start(bf16[640,128]{1,0:T(8,128)(2,1)} %get-tuple-element.39), channel_id=1, source_target_pairs={{0,4},{1,5},{2,6},{3,7},{4,0},{5,1},{6,2},{7,3},{8,12},{9,13},{10,... | collective-permute-start | bytes 491528 | tf_op jit(solution)/shard_map/ppermute | solution.py:33
  43.0 3.9 %collective-permute-start.4 = (bf16[640,128]{1,0:T(8,128)(2,1)}, bf16[640,128]{1,0:T(8,128)(2,1)S(1)}, u32[]{:S(2)}, u32[]{:S(2)}) collective-permute-start(bf16[640,128]{1,0:T(8,128)(2,1)} %get-tuple-element.40), channel_id=1, source_target_pairs={{0,5},{1,6},{2,7},{3,0},{4,1},{5,2},{6,3},{7,4},{8,13},{9,14},{10,... | collective-permute-start | bytes 491528 | tf_op jit(solution)/shard_map/ppermute | solution.py:33
  48.2 3.1 collective-permute-start.5
  51.3 2.4 collective-permute-start.6
  55.8 1.9 collective-permute-done.6.refs_7_
  58.3 2.6 place_pieces.1.rows_ref
  61.0 0.8 copy.66
  61.8 10.0 %forward_rows.1 = (bf16[8,64,128]{2,1,0:T(8,128)(2,1)}, bf16[8,64,128]{2,1,0:T(8,128)(2,1)}, bf16[8,256,128]{2,1,0:T(8,128)(2,1)}, bf16[8,512,256]{2,1,0:T(8,128...) custom-call(s32[1]{0:T(128)} %bitcast.own_ref.class_ref, ...), custom_call_target="tpu_custom_call" | custom-call | tf_op jit(solution)/shard_map/forward_rows/pallas_call | solution.py:345
  71.8 5.6 %all-to-all-start.1 = ((bf16[8,64,128]{2,1,0:T(8,128)(2,1)}), bf16[8,64,128]{2,1,0:T(8,128)(2,1)S(1)}, u32[]{:S(2)}, u32[]{:S(2)}) async-start(bf16[8,64,128]{2,1,0:T(8,128)(2,1)} %get-tuple-element.45), calls=%async_computation.1 | async-start | bytes 262144 | tf_op jit(solution)/shard_map/all_to_all | solution.py:25
  77.4 1.1 fusion
  78.6 4.0 %all-to-all-done.1 = bf16[8,64,128]{2,1,0:T(8,128)(2,1)S(1)} async-done(((bf16[8,64,128]{2,1,0:T(8,128)(2,1)}), bf16[8,64,128]{2,1,0:T(8,128)(2,1)S(1)}, u32[]{:S(2)}, u32[]{:S(2)}) %all-to-all-start.1) | async-done | bytes 131104 | tf_op jit(solution)/shard_map/all_to_all | solution.py:25
  82.8 47.1 %all_to_all.55 = bf16[64,24,128]{2,1,0:T(8,128)(2,1)S(1)} all-to-all(bf16[64,24,128]{2,1,0:T(8,128)(2,1)S(1)} %pad_maximum_fusion), channel_id=1, replica_groups=mesh['row'=64,'head_0'=4,'head_1'=2] {'row'}, dimensions={0} | all-to-all | bytes 786432 | tf_op jit(solution)/shard_map/all_to_all | solution.py:25
  130.0 1.2 broadcast_in_dim.22
  131.2 3.6 %all-to-all-start.3 = ((bf16[8,8,64,128]{3,2,1,0:T(8,128)(2,1)}), bf16[8,8,64,128]{3,2,1,0:T(8,128)(2,1)S(1)}, u32[]{:S(2)}, u32[]{:S(2)}) async-start(bf16[8,8,64,128]{3,2,1,0:T(8,128)(2,1)} %broadcast_in_dim.22), calls=%async_computation.3 | async-start | bytes 2097152 | tf_op jit(solution)/shard_map/all_to_all | solution.py:25
  136.2 0.8 copy.49
  137.0 13.7 %all-to-all-done.3.rows_ref = bf16[8,8,64,128]{3,2,1,0:T(8,128)(2,1)S(1)} async-done(((bf16[8,8,64,128]{3,2,1,0:T(8,128)(2,1)}), bf16[8,8,64,128]{3,2,1,0:T(8,128)(2,1)S(1)}, u32[]{:S(2)}, u32[]{:S(2)}) %all-to-all-start.3) | async-done | bytes 1048608 | tf_op jit(solution)/shard_map/all_to_all | solution.py:25
  150.7 1.0 copy-done
  151.7 14.7 %backward_second.1 = (bf16[8,608,128]{2,1,0:T(8,128)(2,1)}, bf16[512,256]{1,0:T(8,128)(2,1)}) custom-call(s32[1]{0:T(128)} %bitcast.own_ref.class_ref, bf16[8,8,64,128]{3,2,1,0:T(8,128)(2,1)} %copy-done, bf16[8,64,128]{2,1,0:T(8,128)(2,1)} %bitcast.114, bf16[128,128]{1,0:T(8,128)(2,1)} %get-tuple-element.77.wq_ref, ...), custom_call_target="tpu_custom_call" | custom-call | tf_op jit(solution)/shard_map/backward_second/pallas_call | solution.py:383
  166.4 3.9 %all-to-all-start.4 = ((bf16[8,608,128]{2,1,0:T(8,128)(2,1)}), bf16[8,608,128]{2,1,0:T(8,128)(2,1)S(1)}, u32[]{:S(2)}, u32[]{:S(2)}) async-start(bf16[8,608,128]{2,1,0:T(8,128)(2,1)} %get-tuple-element.47), calls=%async_computation.4 | async-start | bytes 2490368 | tf_op jit(solution)/shard_map/all_to_all | solution.py:25
  170.6 19.5 %all-to-all-done.4 = bf16[8,608,128]{2,1,0:T(8,128)(2,1)S(1)} async-done(((bf16[8,608,128]{2,1,0:T(8,128)(2,1)}), bf16[8,608,128]{2,1,0:T(8,128)(2,1)S(1)}, u32[]{:S(2)}, u32[]{:S(2)}) %all-to-all-start.4) | async-done | bytes 1245216 | tf_op jit(solution)/shard_map/all_to_all | solution.py:25
  190.3 0.8 pad_maximum_fusion.1
  191.1 5.9 %all-to-all-start.5 = ((bf16[64,24,128]{2,1,0:T(8,128)(2,1)}), bf16[64,24,128]{2,1,0:T(8,128)(2,1)S(1)}, u32[]{:S(2)}, u32[]{:S(2)}) async-start(bf16[64,24,128]{2,1,0:T(8,128)(2,1)} %pad_maximum_fusion.1), calls=%async_computation.5 | async-start | bytes 786432 | tf_op jit(solution)/shard_map/all_to_all | solution.py:25
  197.4 28.4 %all-to-all-done.5 = bf16[64,24,128]{2,1,0:T(8,128)(2,1)S(1)} async-done(((bf16[64,24,128]{2,1,0:T(8,128)(2,1)}), bf16[64,24,128]{2,1,0:T(8,128)(2,1)S(1)}, u32[]{:S(2)}, u32[]{:S(2)}) %all-to-all-start.5) | async-done | bytes 393248 | tf_op jit(solution)/shard_map/all_to_all | solution.py:25
  226.6 3.4 all-to-all-start.6
  230.2 5.2 %all-to-all-done.6 = bf16[8,64,128]{2,1,0:T(8,128)(2,1)S(1)} async-done(((bf16[8,64,128]{2,1,0:T(8,128)(2,1)}), bf16[8,64,128]{2,1,0:T(8,128)(2,1)S(1)}, u32[]{:S(2)}, u32[]{:S(2)}) %all-to-all-start.6) | async-done | bytes 131104 | tf_op jit(solution)/shard_map/all_to_all | solution.py:25
  236.4 1.9 add_convert_fusion
  238.4 10.4 %backward_first.1 = (bf16[8,672,128]{2,1,0:T(8,128)(2,1)}, bf16[64,2048]{1,0:T(8,128)(2,1)}) custom-call(s32[1]{0:T(128)} %bitcast.own_ref.class_ref, bf16[8,640,128]{2,1,0:T(8,128)(2,1)} %place_pieces.1.rows_ref, bf16[8,64,128]{2,1,0:T(8,128)(2,1)} %get-tuple-element.71.grad_ref, bf16[128,128]{1,0:T(8,128)(2,1)} %get-tuple-element.81.wq_ref, ...), custom_call_target="tpu_custom_call" | custom-call | tf_op jit(solution)/shard_map/backward_first/pallas_call | solution.py:383
  248.8 3.7 %all-to-all-start.7 = ((bf16[8,672,128]{2,1,0:T(8,128)(2,1)}), bf16[8,672,128]{2,1,0:T(8,128)(2,1)S(1)}, u32[]{:S(2)}, u32[]{:S(2)}) async-start(bf16[8,672,128]{2,1,0:T(8,128)(2,1)} %get-tuple-element.53), calls=%async_computation.7 | async-start | bytes 2752512 | tf_op jit(solution)/shard_map/all_to_all | solution.py:25
  252.7 21.8 %all-to-all-done.7 = bf16[8,672,128]{2,1,0:T(8,128)(2,1)S(1)} async-done(((bf16[8,672,128]{2,1,0:T(8,128)(2,1)}), bf16[8,672,128]{2,1,0:T(8,128)(2,1)S(1)}, u32[]{:S(2)}, u32[]{:S(2)}) %all-to-all-start.7) | async-done | bytes 1376288 | tf_op jit(solution)/shard_map/all_to_all | solution.py:25
  274.6 0.8 pad_maximum_fusion.2
  275.4 4.9 %all-to-all-start.8 = ((bf16[64,24,128]{2,1,0:T(8,128)(2,1)}), bf16[64,24,128]{2,1,0:T(8,128)(2,1)S(1)}, u32[]{:S(2)}, u32[]{:S(2)}) async-start(bf16[64,24,128]{2,1,0:T(8,128)(2,1)} %pad_maximum_fusion.2), calls=%async_computation.8 | async-start | bytes 786432 | tf_op jit(solution)/shard_map/all_to_all | solution.py:25
  280.5 28.8 %all-to-all-done.8 = bf16[64,24,128]{2,1,0:T(8,128)(2,1)S(1)} async-done(((bf16[64,24,128]{2,1,0:T(8,128)(2,1)}), bf16[64,24,128]{2,1,0:T(8,128)(2,1)S(1)}, u32[]{:S(2)}, u32[]{:S(2)}) %all-to-all-start.8) | async-done | bytes 393248 | tf_op jit(solution)/shard_map/all_to_all | solution.py:25
  310.8 4.6 %all-to-all-start.9 = ((bf16[64,16,128]{2,1,0:T(8,128)(2,1)}), bf16[64,16,128]{2,1,0:T(8,128)(2,1)S(1)}, u32[]{:S(2)}, u32[]{:S(2)}) async-start(bf16[64,16,128]{2,1,0:T(8,128)(2,1)} %broadcast_in_dim.52), calls=%async_computation.9 | async-start | bytes 524288 | tf_op jit(solution)/shard_map/all_to_all | solution.py:25
  315.9 23.3 %all-to-all-done.9 = bf16[64,16,128]{2,1,0:T(8,128)(2,1)S(1)} async-done(((bf16[64,16,128]{2,1,0:T(8,128)(2,1)}), bf16[64,16,128]{2,1,0:T(8,128)(2,1)S(1)}, u32[]{:S(2)}, u32[]{:S(2)}) %all-to-all-start.9) | async-done | bytes 262176 | tf_op jit(solution)/shard_map/all_to_all | solution.py:25
  339.3 0.8 broadcast_in_dim.53
  340.1 3.5 all-to-all-start.10
  343.6 0.9 bitcast_add_fusion
  344.4 7.8 %all-to-all-done.10.arrived_ref = bf16[8,200,128]{2,1,0:T(8,128)(2,1)S(1)} async-done(((bf16[8,200,128]{2,1,0:T(8,128)(2,1)}), bf16[8,200,128]{2,1,0:T(8,128)(2,1)S(1)}, u32[]{:S(2)}, u32[]{:S(2)}) %all-to-all-start.10) | async-done | bytes 409632 | tf_op jit(solution)/shard_map/all_to_all | solution.py:25
  352.2 0.7 copy-done.1
  352.9 1.9 finish_weights.1
  (114 shorter events, 12.6 us)
Async XLA Ops:
  0.6 46.2 %copy-start.18 = (bf16[2,128,128]{2,1,0:T(8,128)(2,1)S(1)}, bf16[2,128,128]{2,1,0:T(8,128)(2,1)}, u32[]{:S(2)}) copy-start(bf16[2,128,128]{2,1,0:T(8,128)(2,1)} %param.16) | copy-start | bytes 196612
  0.6 46.8 %copy-start.7 = (bf16[2,4,128,128]{3,2,1,0:T(8,128)(2,1)S(1)}, bf16[2,4,128,128]{3,2,1,0:T(8,128)(2,1)}, u32[]{:S(2)}) copy-start(bf16[2,4,128,128]{3,2,1,0:T(8,128)(2,1)} %param.14) | copy-start | bytes 786436
  0.7 47.5 %copy-start.20 = (s32[512]{0:T(512)S(1)}, s32[512]{0:T(512)}, u32[]{:S(2)}) copy-start(s32[512]{0:T(512)} %param.11) | copy-start | bytes 6148
  0.7 53.0 %copy-start.21 = (f32[2,128]{1,0:T(2,128)S(1)}, f32[2,128]{1,0:T(2,128)}, u32[]{:S(2)}) copy-start(f32[2,128]{1,0:T(2,128)} %param.15) | copy-start | bytes 3076
  9.4 38.8 %copy-start.23 = (bf16[640,128]{1,0:T(8,128)(2,1)S(1)}, bf16[640,128]{1,0:T(8,128)(2,1)}, u32[]{:S(2)}) copy-start(bf16[640,128]{1,0:T(8,128)(2,1)} %get-tuple-element.41) | copy-start | bytes 491524
  9.4 41.8 %copy-start.22 = (bf16[640,128]{1,0:T(8,128)(2,1)S(1)}, bf16[640,128]{1,0:T(8,128)(2,1)}, u32[]{:S(2)}) copy-start(bf16[640,128]{1,0:T(8,128)(2,1)} %get-tuple-element.42) | copy-start | bytes 491524
  9.4 51.5 %all-to-all-start = ((bf16[64,24,128]{2,1,0:T(8,128)(2,1)}), bf16[64,24,128]{2,1,0:T(8,128)(2,1)S(1)}, u32[]{:S(2)}, u32[]{:S(2)}) async-start(bf16[64,24,128]{2,1,0:T(8,128)(2,1)} %get-tuple-element.43), calls=%async_computation | async-start | bytes 786432 | tf_op jit(solution)/shard_map/all_to_all | solution.py:25
  29.3 18.8 %collective-permute-start = (bf16[640,128]{1,0:T(8,128)(2,1)}, bf16[640,128]{1,0:T(8,128)(2,1)S(1)}, u32[]{:S(2)}, u32[]{:S(2)}) collective-permute-start(bf16[640,128]{1,0:T(8,128)(2,1)} %get-tuple-element.36), channel_id=1, source_target_pairs={{0,1},{1,2},{2,3},{3,4},{4,5},{5,6},{6,7},{7,0},{8,9},{9,10},{10,1... | collective-permute-start | bytes 491528 | tf_op jit(solution)/shard_map/ppermute | solution.py:33
  31.6 19.6 %collective-permute-start.1 = (bf16[640,128]{1,0:T(8,128)(2,1)}, bf16[640,128]{1,0:T(8,128)(2,1)S(1)}, u32[]{:S(2)}, u32[]{:S(2)}) collective-permute-start(bf16[640,128]{1,0:T(8,128)(2,1)} %get-tuple-element.37), channel_id=1, source_target_pairs={{0,2},{1,3},{2,4},{3,5},{4,6},{5,7},{6,0},{7,1},{8,10},{9,11},{10,... | collective-permute-start | bytes 491528 | tf_op jit(solution)/shard_map/ppermute | solution.py:33
  34.8 20.9 %collective-permute-start.2 = (bf16[640,128]{1,0:T(8,128)(2,1)}, bf16[640,128]{1,0:T(8,128)(2,1)S(1)}, u32[]{:S(2)}, u32[]{:S(2)}) collective-permute-start(bf16[640,128]{1,0:T(8,128)(2,1)} %get-tuple-element.38), channel_id=1, source_target_pairs={{0,3},{1,4},{2,5},{3,6},{4,7},{5,0},{6,1},{7,2},{8,11},{9,12},{10,... | collective-permute-start | bytes 491528 | tf_op jit(solution)/shard_map/ppermute | solution.py:33
  39.3 16.4 %collective-permute-start.3 = (bf16[640,128]{1,0:T(8,128)(2,1)}, bf16[640,128]{1,0:T(8,128)(2,1)S(1)}, u32[]{:S(2)}, u32[]{:S(2)}) collective-permute-start(bf16[640,128]{1,0:T(8,128)(2,1)} %get-tuple-element.39), channel_id=1, source_target_pairs={{0,4},{1,5},{2,6},{3,7},{4,0},{5,1},{6,2},{7,3},{8,12},{9,13},{10,... | collective-permute-start | bytes 491528 | tf_op jit(solution)/shard_map/ppermute | solution.py:33
  43.0 12.7 %collective-permute-start.4 = (bf16[640,128]{1,0:T(8,128)(2,1)}, bf16[640,128]{1,0:T(8,128)(2,1)S(1)}, u32[]{:S(2)}, u32[]{:S(2)}) collective-permute-start(bf16[640,128]{1,0:T(8,128)(2,1)} %get-tuple-element.40), channel_id=1, source_target_pairs={{0,5},{1,6},{2,7},{3,0},{4,1},{5,2},{6,3},{7,4},{8,13},{9,14},{10,... | collective-permute-start | bytes 491528 | tf_op jit(solution)/shard_map/ppermute | solution.py:33
  48.1 9.5 %copy-start.11 = (bf16[640,128]{1,0:T(8,128)(2,1)}, bf16[640,128]{1,0:T(8,128)(2,1)S(1)}, u32[]{:S(2)}) copy-start(bf16[640,128]{1,0:T(8,128)(2,1)S(1)} %collective-permute-done.refs_1_) | copy-start | bytes 491524
  48.2 7.6 %collective-permute-start.5 = (bf16[640,128]{1,0:T(8,128)(2,1)S(1)}, bf16[640,128]{1,0:T(8,128)(2,1)S(1)}, u32[]{:S(2)}, u32[]{:S(2)}) collective-permute-start(bf16[640,128]{1,0:T(8,128)(2,1)S(1)} %copy-done.23), channel_id=1, source_target_pairs={{0,6},{1,7},{2,0},{3,1},{4,2},{5,3},{6,4},{7,5},{8,14},{9,15},{10,... | collective-permute-start | bytes 491528 | tf_op jit(solution)/shard_map/ppermute | solution.py:33
  51.2 6.4 %copy-start.12 = (bf16[640,128]{1,0:T(8,128)(2,1)}, bf16[640,128]{1,0:T(8,128)(2,1)S(1)}, u32[]{:S(2)}) copy-start(bf16[640,128]{1,0:T(8,128)(2,1)S(1)} %collective-permute-done.1.refs_2_) | copy-start | bytes 491524
  51.3 6.4 %collective-permute-start.6 = (bf16[640,128]{1,0:T(8,128)(2,1)S(1)}, bf16[640,128]{1,0:T(8,128)(2,1)S(1)}, u32[]{:S(2)}, u32[]{:S(2)}) collective-permute-start(bf16[640,128]{1,0:T(8,128)(2,1)S(1)} %copy-done.22), channel_id=1, source_target_pairs={{0,7},{1,0},{2,1},{3,2},{4,3},{5,4},{6,5},{7,6},{8,15},{9,8},{10,9... | collective-permute-start | bytes 491528 | tf_op jit(solution)/shard_map/ppermute | solution.py:33
  55.7 1.9 copy-start.13
  55.7 1.9 copy-start.14
  55.7 1.9 copy-start.15
  55.7 1.9 copy-start.16
  57.6 0.7 copy-start.17
  61.0 16.4 %copy-start.19 = (bf16[2,128,4]{1,2,0:T(4,128)(2,1)S(1)}, bf16[2,128,4]{1,2,0:T(4,128)(2,1)}, u32[]{:S(2)}) copy-start(bf16[2,128,4]{1,2,0:T(4,128)(2,1)} %param.17) | copy-start | bytes 6148
  71.8 10.9 %all-to-all-start.1 = ((bf16[8,64,128]{2,1,0:T(8,128)(2,1)}), bf16[8,64,128]{2,1,0:T(8,128)(2,1)S(1)}, u32[]{:S(2)}, u32[]{:S(2)}) async-start(bf16[8,64,128]{2,1,0:T(8,128)(2,1)} %get-tuple-element.45), calls=%async_computation.1 | async-start | bytes 262144 | tf_op jit(solution)/shard_map/all_to_all | solution.py:25
  131.2 19.5 %all-to-all-start.3 = ((bf16[8,8,64,128]{3,2,1,0:T(8,128)(2,1)}), bf16[8,8,64,128]{3,2,1,0:T(8,128)(2,1)S(1)}, u32[]{:S(2)}, u32[]{:S(2)}) async-start(bf16[8,8,64,128]{3,2,1,0:T(8,128)(2,1)} %broadcast_in_dim.22), calls=%async_computation.3 | async-start | bytes 2097152 | tf_op jit(solution)/shard_map/all_to_all | solution.py:25
  150.7 1.0 copy-start
  166.4 3.9 %copy-start.10 = (bf16[512,256]{1,0:T(8,128)(2,1)S(1)}, bf16[512,256]{1,0:T(8,128)(2,1)}, u32[]{:S(2)}) copy-start(bf16[512,256]{1,0:T(8,128)(2,1)} %get-tuple-element.46) | copy-start | bytes 786436
  166.4 23.6 %all-to-all-start.4 = ((bf16[8,608,128]{2,1,0:T(8,128)(2,1)}), bf16[8,608,128]{2,1,0:T(8,128)(2,1)S(1)}, u32[]{:S(2)}, u32[]{:S(2)}) async-start(bf16[8,608,128]{2,1,0:T(8,128)(2,1)} %get-tuple-element.47), calls=%async_computation.4 | async-start | bytes 2490368 | tf_op jit(solution)/shard_map/all_to_all | solution.py:25
  170.6 26.4 %copy-start.4 = (bf16[8,64,128]{2,1,0:T(8,128)(2,1)S(1)}, bf16[8,64,128]{2,1,0:T(8,128)(2,1)}, u32[]{:S(2)}) copy-start(bf16[8,64,128]{2,1,0:T(8,128)(2,1)} %get-tuple-element.44) | copy-start | bytes 393220
  190.3 39.7 %copy-start.3 = (bf16[8,64,128]{2,1,0:T(8,128)(2,1)S(1)}, bf16[8,64,128]{2,1,0:T(8,128)(2,1)}, u32[]{:S(2)}) copy-start(bf16[8,64,128]{2,1,0:T(8,128)(2,1)} %get-tuple-element.45) | copy-start | bytes 393220
  191.1 34.7 %all-to-all-start.5 = ((bf16[64,24,128]{2,1,0:T(8,128)(2,1)}), bf16[64,24,128]{2,1,0:T(8,128)(2,1)S(1)}, u32[]{:S(2)}, u32[]{:S(2)}) async-start(bf16[64,24,128]{2,1,0:T(8,128)(2,1)} %pad_maximum_fusion.1), calls=%async_computation.5 | async-start | bytes 786432 | tf_op jit(solution)/shard_map/all_to_all | solution.py:25
  226.6 8.7 %all-to-all-start.6 = ((bf16[8,64,128]{2,1,0:T(8,128)(2,1)}), bf16[8,64,128]{2,1,0:T(8,128)(2,1)S(1)}, u32[]{:S(2)}, u32[]{:S(2)}) async-start(bf16[8,64,128]{2,1,0:T(8,128)(2,1)} %bitcast.97), calls=%async_computation.6 | async-start | bytes 262144 | tf_op jit(solution)/shard_map/all_to_all | solution.py:25
  248.8 3.8 %copy-start.9 = (bf16[64,2048]{1,0:T(8,128)(2,1)S(1)}, bf16[64,2048]{1,0:T(8,128)(2,1)}, u32[]{:S(2)}) copy-start(bf16[64,2048]{1,0:T(8,128)(2,1)} %get-tuple-element.55) | copy-start | bytes 786436
  248.8 25.7 %all-to-all-start.7 = ((bf16[8,672,128]{2,1,0:T(8,128)(2,1)}), bf16[8,672,128]{2,1,0:T(8,128)(2,1)S(1)}, u32[]{:S(2)}, u32[]{:S(2)}) async-start(bf16[8,672,128]{2,1,0:T(8,128)(2,1)} %get-tuple-element.53), calls=%async_computation.7 | async-start | bytes 2752512 | tf_op jit(solution)/shard_map/all_to_all | solution.py:25
  275.4 33.9 %copy-start.6 = (bf16[640,128]{1,0:T(8,128)(2,1)S(1)}, bf16[640,128]{1,0:T(8,128)(2,1)}, u32[]{:S(2)}) copy-start(bf16[640,128]{1,0:T(8,128)(2,1)} %get-tuple-element.35.refs_0_) | copy-start | bytes 491524
  275.4 34.1 %copy-start.5 = (f32[512,128]{1,0:T(8,128)S(1)}, f32[512,128]{1,0:T(8,128)}, u32[]{:S(2)}) copy-start(f32[512,128]{1,0:T(8,128)} %get-tuple-element.56) | copy-start | bytes 786436
  275.4 33.9 %all-to-all-start.8 = ((bf16[64,24,128]{2,1,0:T(8,128)(2,1)}), bf16[64,24,128]{2,1,0:T(8,128)(2,1)S(1)}, u32[]{:S(2)}, u32[]{:S(2)}) async-start(bf16[64,24,128]{2,1,0:T(8,128)(2,1)} %pad_maximum_fusion.2), calls=%async_computation.8 | async-start | bytes 786432 | tf_op jit(solution)/shard_map/all_to_all | solution.py:25
  280.4 35.0 %copy-start.8 = (f32[512,1]{1,0:T(8,128)S(1)}, f32[512,1]{1,0:T(8,128)}, u32[]{:S(2)}) copy-start(f32[512,1]{1,0:T(8,128)} %get-tuple-element.54) | copy-start | bytes 6148
  310.8 28.3 %all-to-all-start.9 = ((bf16[64,16,128]{2,1,0:T(8,128)(2,1)}), bf16[64,16,128]{2,1,0:T(8,128)(2,1)S(1)}, u32[]{:S(2)}, u32[]{:S(2)}) async-start(bf16[64,16,128]{2,1,0:T(8,128)(2,1)} %broadcast_in_dim.52), calls=%async_computation.9 | async-start | bytes 524288 | tf_op jit(solution)/shard_map/all_to_all | solution.py:25
  315.6 28.0 %copy-start.2 = (bf16[1,512,128]{2,1,0:T(8,128)(2,1)S(1)}, bf16[1,512,128]{2,1,0:T(8,128)(2,1)}, u32[]{:S(2)}) copy-start(bf16[1,512,128]{2,1,0:T(8,128)(2,1)} %param.10) | copy-start | bytes 393220
  340.1 12.1 %all-to-all-start.10 = ((bf16[8,200,128]{2,1,0:T(8,128)(2,1)}), bf16[8,200,128]{2,1,0:T(8,128)(2,1)S(1)}, u32[]{:S(2)}, u32[]{:S(2)}) async-start(bf16[8,200,128]{2,1,0:T(8,128)(2,1)} %broadcast_in_dim.53), calls=%async_computation.10 | async-start | bytes 819200 | tf_op jit(solution)/shard_map/all_to_all | solution.py:25
  352.2 0.7 copy-start.1

commit v7 on v6

--- a/solution.py
+++ b/solution.py
@@ -266,11 +266,19 @@
     return (projection[0], joined, projection[3], out_proj, gate_offset[None])
 
 
-def start_kernel(heads, own_ref, pair_ref, class_cot_ref, cot_ref, gain_ref, shift_ref, wb_ref,
-                 row_ref, normed_ref, inverse_ref, *piece_refs):
-    classes, groups, channels = pair_ref.shape
-    positions = classes * groups
-    pair = pair_ref[...].reshape(positions, channels)
+def start_kernel(heads, own_ref, pair_ref, cot_ref, gain_ref, shift_ref, wb_ref,
+                 row_ref, normed_ref, inverse_ref, *refs):
+    piece_refs, plain, ordered = refs[:-2], refs[-2], refs[-1]
+    classes = len(piece_refs)
+    positions, channels = pair_ref.shape
+    groups = positions // classes
+    for which, ref in enumerate((pair_ref, cot_ref)):
+        first = which * positions
+        plain[first : first + positions] = ref[...].astype(jnp.float32)
+        for peer in range(classes):
+            place = first + peer * groups
+            ordered[place : place + groups] = plain[pl.ds(first + peer, groups, stride=classes)]
+    pair = ordered[:positions]
     normed, inverse, normal = layer_norm(pair, gain_ref[...], shift_ref[...])
     normed_ref[...] = normed
     inverse_ref[...] = inverse
@@ -287,17 +295,19 @@
     packed = jnp.concatenate(lines, axis=0).astype(jnp.bfloat16)
     rows = packed.shape[0]
     row_ref[:, :rows] = jnp.broadcast_to(packed[None], (groups, *packed.shape))
-    row_ref[:, rows:] = cot_ref[...]
+    row_ref[:, rows:] = plain[positions:].reshape(groups, classes, channels).astype(jnp.bfloat16)
     for shift, piece_ref in enumerate(piece_refs):
         peer = lax.rem(own_ref[0] + shift, classes)
         piece_ref[:positions] = normal
-        piece_ref[positions : positions + groups] = pair_ref[pl.ds(peer, 1)][0]
-        piece_ref[positions + groups :] = class_cot_ref[pl.ds(peer, 1)][0]
-
-
-def start_call(own_class, pair, class_cot, cot, params, heads):
-    classes, groups, channels = pair.shape
-    positions = classes * groups
+        place = pl.ds(pl.multiple_of(peer * groups, groups), groups)
+        piece_ref[positions : positions + groups] = ordered[place].astype(jnp.bfloat16)
+        place = pl.ds(pl.multiple_of(positions + peer * groups, groups), groups)
+        piece_ref[positions + groups :] = ordered[place].astype(jnp.bfloat16)
+
+
+def start_call(own_class, pair, cot, params, heads, classes):
+    positions, channels = pair.shape
+    groups = positions // classes
     rows = heads * positions // LANES + classes
     half = jnp.bfloat16
     vmem = pl.BlockSpec(memory_space=pltpu.VMEM)
@@ -309,12 +319,13 @@
     results += [jax.ShapeDtypeStruct((positions + 2 * groups, channels), half)] * classes
     return pl.pallas_call(
         functools.partial(start_kernel, heads),
-        in_specs=[pl.BlockSpec(memory_space=pltpu.SMEM)] + [vmem] * 6,
+        in_specs=[pl.BlockSpec(memory_space=pltpu.SMEM)] + [vmem] * 5,
         out_specs=[vmem] * len(results),
         out_shape=results,
+        scratch_shapes=[pltpu.VMEM((2 * positions, channels), jnp.float32)] * 2,
         interpret=INTERPRET,
         name="start_row",
-    )(own_class, pair, class_cot, cot, params[0][None], params[1][None], params[5])
+    )(own_class, pair, cot, params[0][None], params[1][None], params[5])
 
 
 def step_spec(shape):
@@ -479,15 +490,8 @@
         for which in range(2)
     ]
 
-    own_pair = pair_input.reshape(groups, classes, channels).transpose(1, 0, 2)
-    own_cotangent = cotangent.reshape(groups, classes, channels)
     row_parts, normed_flat, inverse_flat, *parts = start_call(
-        own_class,
-        own_pair,
-        own_cotangent.transpose(1, 0, 2),
-        own_cotangent,
-        params[0],
-        head_total,
+        own_class, pair_input[0], cotangent[0], params[0], head_total, classes
     )
     normal_flat = parts[0][:positions]
     pieces = shifted_exchange(parts)

time: 356 us -> 354 us (level)
  no operation moved by 1% of the time
where the time goes in v7:
time: 354 us; the launch traced here: 352 us
  waiting for transfers between devices  154 us (44%)
  starting transfers between devices  81.7 us (23%)
  blocking collectives  47.1 us (13%)
  Pallas kernels  42.4 us (12%)
  local copies, waits for them, and re-layouts  15.3 us (4%)
  other arithmetic  7.9 us (2%)
    all_to_all x10, waiting for transfers between devices, exchanged(): return lax.all_to_all(parts, axis, split_axis=0, concat_axis=0, tiled=True)  152 us
    all_to_all x10, starting transfers between devices, exchanged(): return lax.all_to_all(parts, axis, split_axis=0, concat_axis=0, tiled=True)  58.8 us
    all_to_all x1, blocking collectives, exchanged(): return lax.all_to_all(parts, axis, split_axis=0, concat_axis=0, tiled=True)  47.1 us
    pallas_call x2, Pallas kernels, backward_call(): pl.pallas_call(functools.partial(backward_kernel, heads, positions, secon...  25.2 us
    ppermute x7, starting transfers between devices, shifted_exchange(): pieces.append(lax.ppermute(parts[shift], HEAD, pairs))  22.9 us
    pallas_call x1, Pallas kernels, forward_call(): pl.pallas_call(functools.partial(forward_kernel, heads, positions), grid=...  10 us
  transfers between devices with their start and end apart: 17, of which 10 were waited for; matrix products, arithmetic and copies ran while one was open for 3% of the time, Pallas kernels for 1%

profile of v7, /device:TPU:1, one launch (start us, length us, event | category | flops | bytes accessed | tf_op | source)
XLA Modules:
  0.0 352.4 jit_solution(3676970515474653743)
XLA Ops:
  2.1 1.3 slice_bitcast_fusion.12
  3.5 2.7 start_row.1
  6.2 19.9 %all-to-all-start = ((bf16[64,24,128]{2,1,0:T(8,128)(2,1)}), bf16[64,24,128]{2,1,0:T(8,128)(2,1)S(1)}, u32[]{:S(2)}, u32[]{:S(2)}) async-start(bf16[64,24,128]{2,1,0:T(8,128)(2,1)} %get-tuple-element.43), calls=%async_computation | async-start | bytes 786432 | tf_op jit(solution)/shard_map/all_to_all | solution.py:25
  26.1 2.3 collective-permute-start
  28.4 3.1 collective-permute-start.1
  31.5 4.5 %collective-permute-start.2 = (bf16[640,128]{1,0:T(8,128)(2,1)}, bf16[640,128]{1,0:T(8,128)(2,1)S(1)}, u32[]{:S(2)}, u32[]{:S(2)}) collective-permute-start(bf16[640,128]{1,0:T(8,128)(2,1)} %get-tuple-element.38), channel_id=1, source_target_pairs={{0,3},{1,4},{2,5},{3,6},{4,7},{5,0},{6,1},{7,2},{8,11},{9,12},{10,... | collective-permute-start | bytes 491528 | tf_op jit(solution)/shard_map/ppermute | solution.py:33
  36.1 3.6 %collective-permute-start.3 = (bf16[640,128]{1,0:T(8,128)(2,1)}, bf16[640,128]{1,0:T(8,128)(2,1)S(1)}, u32[]{:S(2)}, u32[]{:S(2)}) collective-permute-start(bf16[640,128]{1,0:T(8,128)(2,1)} %get-tuple-element.39), channel_id=1, source_target_pairs={{0,4},{1,5},{2,6},{3,7},{4,0},{5,1},{6,2},{7,3},{8,12},{9,13},{10,... | collective-permute-start | bytes 491528 | tf_op jit(solution)/shard_map/ppermute | solution.py:33
  39.7 3.9 %collective-permute-start.4 = (bf16[640,128]{1,0:T(8,128)(2,1)}, bf16[640,128]{1,0:T(8,128)(2,1)S(1)}, u32[]{:S(2)}, u32[]{:S(2)}) collective-permute-start(bf16[640,128]{1,0:T(8,128)(2,1)} %get-tuple-element.40), channel_id=1, source_target_pairs={{0,5},{1,6},{2,7},{3,0},{4,1},{5,2},{6,3},{7,4},{8,13},{9,14},{10,... | collective-permute-start | bytes 491528 | tf_op jit(solution)/shard_map/ppermute | solution.py:33
  43.6 1.4 slice_bitcast_fusion.1
  45.7 3.1 collective-permute-start.5
  48.8 2.4 collective-permute-start.6
  53.3 1.9 collective-permute-done.6.refs_7_
  55.9 2.6 place_pieces.1.rows_ref
  58.5 0.8 copy.58
  59.3 10.0 %forward_rows.1 = (bf16[8,64,128]{2,1,0:T(8,128)(2,1)}, bf16[8,64,128]{2,1,0:T(8,128)(2,1)}, bf16[8,256,128]{2,1,0:T(8,128)(2,1)}, bf16[8,512,256]{2,1,0:T(8,128...) custom-call(s32[1]{0:T(128)} %bitcast.own_ref.class_ref, ...), custom_call_target="tpu_custom_call" | custom-call | tf_op jit(solution)/shard_map/forward_rows/pallas_call | solution.py:356
  69.3 5.6 %all-to-all-start.1 = ((bf16[8,64,128]{2,1,0:T(8,128)(2,1)}), bf16[8,64,128]{2,1,0:T(8,128)(2,1)S(1)}, u32[]{:S(2)}, u32[]{:S(2)}) async-start(bf16[8,64,128]{2,1,0:T(8,128)(2,1)} %get-tuple-element.45), calls=%async_computation.1 | async-start | bytes 262144 | tf_op jit(solution)/shard_map/all_to_all | solution.py:25
  74.9 1.1 fusion
  76.1 4.0 %all-to-all-done.1 = bf16[8,64,128]{2,1,0:T(8,128)(2,1)S(1)} async-done(((bf16[8,64,128]{2,1,0:T(8,128)(2,1)}), bf16[8,64,128]{2,1,0:T(8,128)(2,1)S(1)}, u32[]{:S(2)}, u32[]{:S(2)}) %all-to-all-start.1) | async-done | bytes 131104 | tf_op jit(solution)/shard_map/all_to_all | solution.py:25
  80.4 47.1 %all_to_all.55 = bf16[64,24,128]{2,1,0:T(8,128)(2,1)S(1)} all-to-all(bf16[64,24,128]{2,1,0:T(8,128)(2,1)S(1)} %pad_maximum_fusion), channel_id=1, replica_groups=mesh['row'=64,'head_0'=4,'head_1'=2] {'row'}, dimensions={0} | all-to-all | bytes 786432 | tf_op jit(solution)/shard_map/all_to_all | solution.py:25
  127.6 1.3 broadcast_in_dim.22
  128.8 3.6 %all-to-all-start.3 = ((bf16[8,8,64,128]{3,2,1,0:T(8,128)(2,1)}), bf16[8,8,64,128]{3,2,1,0:T(8,128)(2,1)S(1)}, u32[]{:S(2)}, u32[]{:S(2)}) async-start(bf16[8,8,64,128]{3,2,1,0:T(8,128)(2,1)} %broadcast_in_dim.22), calls=%async_computation.3 | async-start | bytes 2097152 | tf_op jit(solution)/shard_map/all_to_all | solution.py:25
  133.8 0.8 copy.42
  134.6 13.7 %all-to-all-done.3.rows_ref = bf16[8,8,64,128]{3,2,1,0:T(8,128)(2,1)S(1)} async-done(((bf16[8,8,64,128]{3,2,1,0:T(8,128)(2,1)}), bf16[8,8,64,128]{3,2,1,0:T(8,128)(2,1)S(1)}, u32[]{:S(2)}, u32[]{:S(2)}) %all-to-all-start.3) | async-done | bytes 1048608 | tf_op jit(solution)/shard_map/all_to_all | solution.py:25
  148.3 1.0 copy-done
  149.2 14.7 %backward_second.1 = (bf16[8,608,128]{2,1,0:T(8,128)(2,1)}, bf16[512,256]{1,0:T(8,128)(2,1)}) custom-call(s32[1]{0:T(128)} %bitcast.own_ref.class_ref, bf16[8,8,64,128]{3,2,1,0:T(8,128)(2,1)} %copy-done, bf16[8,64,128]{2,1,0:T(8,128)(2,1)} %bitcast.107, bf16[128,128]{1,0:T(8,128)(2,1)} %get-tuple-element.77.wq_ref, ...), custom_call_target="tpu_custom_call" | custom-call | tf_op jit(solution)/shard_map/backward_second/pallas_call | solution.py:394
  164.0 3.9 %all-to-all-start.4 = ((bf16[8,608,128]{2,1,0:T(8,128)(2,1)}), bf16[8,608,128]{2,1,0:T(8,128)(2,1)S(1)}, u32[]{:S(2)}, u32[]{:S(2)}) async-start(bf16[8,608,128]{2,1,0:T(8,128)(2,1)} %get-tuple-element.47), calls=%async_computation.4 | async-start | bytes 2490368 | tf_op jit(solution)/shard_map/all_to_all | solution.py:25
  168.2 19.5 %all-to-all-done.4 = bf16[8,608,128]{2,1,0:T(8,128)(2,1)S(1)} async-done(((bf16[8,608,128]{2,1,0:T(8,128)(2,1)}), bf16[8,608,128]{2,1,0:T(8,128)(2,1)S(1)}, u32[]{:S(2)}, u32[]{:S(2)}) %all-to-all-start.4) | async-done | bytes 1245216 | tf_op jit(solution)/shard_map/all_to_all | solution.py:25
  187.9 0.8 pad_maximum_fusion.1
  188.7 5.9 %all-to-all-start.5 = ((bf16[64,24,128]{2,1,0:T(8,128)(2,1)}), bf16[64,24,128]{2,1,0:T(8,128)(2,1)S(1)}, u32[]{:S(2)}, u32[]{:S(2)}) async-start(bf16[64,24,128]{2,1,0:T(8,128)(2,1)} %pad_maximum_fusion.1), calls=%async_computation.5 | async-start | bytes 786432 | tf_op jit(solution)/shard_map/all_to_all | solution.py:25
  195.0 28.4 %all-to-all-done.5 = bf16[64,24,128]{2,1,0:T(8,128)(2,1)S(1)} async-done(((bf16[64,24,128]{2,1,0:T(8,128)(2,1)}), bf16[64,24,128]{2,1,0:T(8,128)(2,1)S(1)}, u32[]{:S(2)}, u32[]{:S(2)}) %all-to-all-start.5) | async-done | bytes 393248 | tf_op jit(solution)/shard_map/all_to_all | solution.py:25
  224.2 3.4 all-to-all-start.6
  227.8 5.2 %all-to-all-done.6 = bf16[8,64,128]{2,1,0:T(8,128)(2,1)S(1)} async-done(((bf16[8,64,128]{2,1,0:T(8,128)(2,1)}), bf16[8,64,128]{2,1,0:T(8,128)(2,1)S(1)}, u32[]{:S(2)}, u32[]{:S(2)}) %all-to-all-start.6) | async-done | bytes 131104 | tf_op jit(solution)/shard_map/all_to_all | solution.py:25
  234.0 1.9 add_convert_fusion
  236.0 10.5 %backward_first.1 = (bf16[8,672,128]{2,1,0:T(8,128)(2,1)}, bf16[64,2048]{1,0:T(8,128)(2,1)}) custom-call(s32[1]{0:T(128)} %bitcast.own_ref.class_ref, bf16[8,640,128]{2,1,0:T(8,128)(2,1)} %place_pieces.1.rows_ref, bf16[8,64,128]{2,1,0:T(8,128)(2,1)} %get-tuple-element.71.grad_ref, bf16[128,128]{1,0:T(8,128)(2,1)} %get-tuple-element.81.wq_ref, ...), custom_call_target="tpu_custom_call" | custom-call | tf_op jit(solution)/shard_map/backward_first/pallas_call | solution.py:394
  246.4 3.7 %all-to-all-start.7 = ((bf16[8,672,128]{2,1,0:T(8,128)(2,1)}), bf16[8,672,128]{2,1,0:T(8,128)(2,1)S(1)}, u32[]{:S(2)}, u32[]{:S(2)}) async-start(bf16[8,672,128]{2,1,0:T(8,128)(2,1)} %get-tuple-element.53), calls=%async_computation.7 | async-start | bytes 2752512 | tf_op jit(solution)/shard_map/all_to_all | solution.py:25
  250.2 21.9 %all-to-all-done.7 = bf16[8,672,128]{2,1,0:T(8,128)(2,1)S(1)} async-done(((bf16[8,672,128]{2,1,0:T(8,128)(2,1)}), bf16[8,672,128]{2,1,0:T(8,128)(2,1)S(1)}, u32[]{:S(2)}, u32[]{:S(2)}) %all-to-all-start.7) | async-done | bytes 1376288 | tf_op jit(solution)/shard_map/all_to_all | solution.py:25
  272.3 0.8 pad_maximum_fusion.2
  273.1 4.9 %all-to-all-start.8 = ((bf16[64,24,128]{2,1,0:T(8,128)(2,1)}), bf16[64,24,128]{2,1,0:T(8,128)(2,1)S(1)}, u32[]{:S(2)}, u32[]{:S(2)}) async-start(bf16[64,24,128]{2,1,0:T(8,128)(2,1)} %pad_maximum_fusion.2), calls=%async_computation.8 | async-start | bytes 786432 | tf_op jit(solution)/shard_map/all_to_all | solution.py:25
  278.1 28.8 %all-to-all-done.8 = bf16[64,24,128]{2,1,0:T(8,128)(2,1)S(1)} async-done(((bf16[64,24,128]{2,1,0:T(8,128)(2,1)}), bf16[64,24,128]{2,1,0:T(8,128)(2,1)S(1)}, u32[]{:S(2)}, u32[]{:S(2)}) %all-to-all-start.8) | async-done | bytes 393248 | tf_op jit(solution)/shard_map/all_to_all | solution.py:25
  307.6 0.7 broadcast_in_dim.52
  308.4 4.6 %all-to-all-start.9 = ((bf16[64,16,128]{2,1,0:T(8,128)(2,1)}), bf16[64,16,128]{2,1,0:T(8,128)(2,1)S(1)}, u32[]{:S(2)}, u32[]{:S(2)}) async-start(bf16[64,16,128]{2,1,0:T(8,128)(2,1)} %broadcast_in_dim.52), calls=%async_computation.9 | async-start | bytes 524288 | tf_op jit(solution)/shard_map/all_to_all | solution.py:25
  313.4 23.3 %all-to-all-done.9 = bf16[64,16,128]{2,1,0:T(8,128)(2,1)S(1)} async-done(((bf16[64,16,128]{2,1,0:T(8,128)(2,1)}), bf16[64,16,128]{2,1,0:T(8,128)(2,1)S(1)}, u32[]{:S(2)}, u32[]{:S(2)}) %all-to-all-start.9) | async-done | bytes 262176 | tf_op jit(solution)/shard_map/all_to_all | solution.py:25
  336.8 0.8 broadcast_in_dim.53
  337.6 3.5 all-to-all-start.10
  341.2 0.9 bitcast_add_fusion
  342.0 7.8 %all-to-all-done.10.arrived_ref = bf16[8,200,128]{2,1,0:T(8,128)(2,1)S(1)} async-done(((bf16[8,200,128]{2,1,0:T(8,128)(2,1)}), bf16[8,200,128]{2,1,0:T(8,128)(2,1)S(1)}, u32[]{:S(2)}, u32[]{:S(2)}) %all-to-all-start.10) | async-done | bytes 409632 | tf_op jit(solution)/shard_map/all_to_all | solution.py:25
  349.8 0.8 copy-done.1
  350.5 1.9 finish_weights.1
  (110 shorter events, 11.2 us)
Async XLA Ops:
  0.6 44.4 %copy-start.7 = (bf16[2,4,128,128]{3,2,1,0:T(8,128)(2,1)S(1)}, bf16[2,4,128,128]{3,2,1,0:T(8,128)(2,1)}, u32[]{:S(2)}) copy-start(bf16[2,4,128,128]{3,2,1,0:T(8,128)(2,1)} %param.14) | copy-start | bytes 786436
  0.6 45.0 %copy-start.19 = (s32[512]{0:T(512)S(1)}, s32[512]{0:T(512)}, u32[]{:S(2)}) copy-start(s32[512]{0:T(512)} %param.11) | copy-start | bytes 6148
  0.7 50.5 %copy-start.20 = (f32[2,128]{1,0:T(2,128)S(1)}, f32[2,128]{1,0:T(2,128)}, u32[]{:S(2)}) copy-start(f32[2,128]{1,0:T(2,128)} %param.15) | copy-start | bytes 3076
  6.2 39.5 %copy-start.22 = (bf16[640,128]{1,0:T(8,128)(2,1)S(1)}, bf16[640,128]{1,0:T(8,128)(2,1)}, u32[]{:S(2)}) copy-start(bf16[640,128]{1,0:T(8,128)(2,1)} %get-tuple-element.41) | copy-start | bytes 491524
  6.2 42.6 %copy-start.21 = (bf16[640,128]{1,0:T(8,128)(2,1)S(1)}, bf16[640,128]{1,0:T(8,128)(2,1)}, u32[]{:S(2)}) copy-start(bf16[640,128]{1,0:T(8,128)(2,1)} %get-tuple-element.42) | copy-start | bytes 491524
  6.2 52.3 %all-to-all-start = ((bf16[64,24,128]{2,1,0:T(8,128)(2,1)}), bf16[64,24,128]{2,1,0:T(8,128)(2,1)S(1)}, u32[]{:S(2)}, u32[]{:S(2)}) async-start(bf16[64,24,128]{2,1,0:T(8,128)(2,1)} %get-tuple-element.43), calls=%async_computation | async-start | bytes 786432 | tf_op jit(solution)/shard_map/all_to_all | solution.py:25
  26.1 19.6 %collective-permute-start = (bf16[640,128]{1,0:T(8,128)(2,1)}, bf16[640,128]{1,0:T(8,128)(2,1)S(1)}, u32[]{:S(2)}, u32[]{:S(2)}) collective-permute-start(bf16[640,128]{1,0:T(8,128)(2,1)} %get-tuple-element.36), channel_id=1, source_target_pairs={{0,1},{1,2},{2,3},{3,4},{4,5},{5,6},{6,7},{7,0},{8,9},{9,10},{10,1... | collective-permute-start | bytes 491528 | tf_op jit(solution)/shard_map/ppermute | solution.py:33
  28.4 20.4 %collective-permute-start.1 = (bf16[640,128]{1,0:T(8,128)(2,1)}, bf16[640,128]{1,0:T(8,128)(2,1)S(1)}, u32[]{:S(2)}, u32[]{:S(2)}) collective-permute-start(bf16[640,128]{1,0:T(8,128)(2,1)} %get-tuple-element.37), channel_id=1, source_target_pairs={{0,2},{1,3},{2,4},{3,5},{4,6},{5,7},{6,0},{7,1},{8,10},{9,11},{10,... | collective-permute-start | bytes 491528 | tf_op jit(solution)/shard_map/ppermute | solution.py:33
  31.5 21.7 %collective-permute-start.2 = (bf16[640,128]{1,0:T(8,128)(2,1)}, bf16[640,128]{1,0:T(8,128)(2,1)S(1)}, u32[]{:S(2)}, u32[]{:S(2)}) collective-permute-start(bf16[640,128]{1,0:T(8,128)(2,1)} %get-tuple-element.38), channel_id=1, source_target_pairs={{0,3},{1,4},{2,5},{3,6},{4,7},{5,0},{6,1},{7,2},{8,11},{9,12},{10,... | collective-permute-start | bytes 491528 | tf_op jit(solution)/shard_map/ppermute | solution.py:33
  36.1 17.2 %collective-permute-start.3 = (bf16[640,128]{1,0:T(8,128)(2,1)}, bf16[640,128]{1,0:T(8,128)(2,1)S(1)}, u32[]{:S(2)}, u32[]{:S(2)}) collective-permute-start(bf16[640,128]{1,0:T(8,128)(2,1)} %get-tuple-element.39), channel_id=1, source_target_pairs={{0,4},{1,5},{2,6},{3,7},{4,0},{5,1},{6,2},{7,3},{8,12},{9,13},{10,... | collective-permute-start | bytes 491528 | tf_op jit(solution)/shard_map/ppermute | solution.py:33
  39.7 13.5 %collective-permute-start.4 = (bf16[640,128]{1,0:T(8,128)(2,1)}, bf16[640,128]{1,0:T(8,128)(2,1)S(1)}, u32[]{:S(2)}, u32[]{:S(2)}) collective-permute-start(bf16[640,128]{1,0:T(8,128)(2,1)} %get-tuple-element.40), channel_id=1, source_target_pairs={{0,5},{1,6},{2,7},{3,0},{4,1},{5,2},{6,3},{7,4},{8,13},{9,14},{10,... | collective-permute-start | bytes 491528 | tf_op jit(solution)/shard_map/ppermute | solution.py:33
  45.7 9.5 %copy-start.11 = (bf16[640,128]{1,0:T(8,128)(2,1)}, bf16[640,128]{1,0:T(8,128)(2,1)S(1)}, u32[]{:S(2)}) copy-start(bf16[640,128]{1,0:T(8,128)(2,1)S(1)} %collective-permute-done.refs_1_) | copy-start | bytes 491524
  45.7 7.6 %collective-permute-start.5 = (bf16[640,128]{1,0:T(8,128)(2,1)S(1)}, bf16[640,128]{1,0:T(8,128)(2,1)S(1)}, u32[]{:S(2)}, u32[]{:S(2)}) collective-permute-start(bf16[640,128]{1,0:T(8,128)(2,1)S(1)} %copy-done.22), channel_id=1, source_target_pairs={{0,6},{1,7},{2,0},{3,1},{4,2},{5,3},{6,4},{7,5},{8,14},{9,15},{10,... | collective-permute-start | bytes 491528 | tf_op jit(solution)/shard_map/ppermute | solution.py:33
  48.8 6.4 %copy-start.12 = (bf16[640,128]{1,0:T(8,128)(2,1)}, bf16[640,128]{1,0:T(8,128)(2,1)S(1)}, u32[]{:S(2)}) copy-start(bf16[640,128]{1,0:T(8,128)(2,1)S(1)} %collective-permute-done.1.refs_2_) | copy-start | bytes 491524
  48.8 6.4 %collective-permute-start.6 = (bf16[640,128]{1,0:T(8,128)(2,1)S(1)}, bf16[640,128]{1,0:T(8,128)(2,1)S(1)}, u32[]{:S(2)}, u32[]{:S(2)}) collective-permute-start(bf16[640,128]{1,0:T(8,128)(2,1)S(1)} %copy-done.21), channel_id=1, source_target_pairs={{0,7},{1,0},{2,1},{3,2},{4,3},{5,4},{6,5},{7,6},{8,15},{9,8},{10,9... | collective-permute-start | bytes 491528 | tf_op jit(solution)/shard_map/ppermute | solution.py:33
  53.2 2.0 copy-start.13
  53.2 2.0 copy-start.14
  53.3 1.9 copy-start.15
  53.3 1.9 copy-start.16
  55.2 0.7 copy-start.17
  58.5 16.4 %copy-start.18 = (bf16[2,128,4]{1,2,0:T(4,128)(2,1)S(1)}, bf16[2,128,4]{1,2,0:T(4,128)(2,1)}, u32[]{:S(2)}) copy-start(bf16[2,128,4]{1,2,0:T(4,128)(2,1)} %param.17) | copy-start | bytes 6148
  69.3 10.9 %all-to-all-start.1 = ((bf16[8,64,128]{2,1,0:T(8,128)(2,1)}), bf16[8,64,128]{2,1,0:T(8,128)(2,1)S(1)}, u32[]{:S(2)}, u32[]{:S(2)}) async-start(bf16[8,64,128]{2,1,0:T(8,128)(2,1)} %get-tuple-element.45), calls=%async_computation.1 | async-start | bytes 262144 | tf_op jit(solution)/shard_map/all_to_all | solution.py:25
  128.8 19.5 %all-to-all-start.3 = ((bf16[8,8,64,128]{3,2,1,0:T(8,128)(2,1)}), bf16[8,8,64,128]{3,2,1,0:T(8,128)(2,1)S(1)}, u32[]{:S(2)}, u32[]{:S(2)}) async-start(bf16[8,8,64,128]{3,2,1,0:T(8,128)(2,1)} %broadcast_in_dim.22), calls=%async_computation.3 | async-start | bytes 2097152 | tf_op jit(solution)/shard_map/all_to_all | solution.py:25
  148.3 1.0 copy-start
  164.0 3.9 %copy-start.10 = (bf16[512,256]{1,0:T(8,128)(2,1)S(1)}, bf16[512,256]{1,0:T(8,128)(2,1)}, u32[]{:S(2)}) copy-start(bf16[512,256]{1,0:T(8,128)(2,1)} %get-tuple-element.46) | copy-start | bytes 786436
  164.0 23.6 %all-to-all-start.4 = ((bf16[8,608,128]{2,1,0:T(8,128)(2,1)}), bf16[8,608,128]{2,1,0:T(8,128)(2,1)S(1)}, u32[]{:S(2)}, u32[]{:S(2)}) async-start(bf16[8,608,128]{2,1,0:T(8,128)(2,1)} %get-tuple-element.47), calls=%async_computation.4 | async-start | bytes 2490368 | tf_op jit(solution)/shard_map/all_to_all | solution.py:25
  168.1 26.4 %copy-start.3 = (bf16[8,64,128]{2,1,0:T(8,128)(2,1)S(1)}, bf16[8,64,128]{2,1,0:T(8,128)(2,1)}, u32[]{:S(2)}) copy-start(bf16[8,64,128]{2,1,0:T(8,128)(2,1)} %get-tuple-element.44) | copy-start | bytes 393220
  187.9 39.7 %copy-start.2 = (bf16[8,64,128]{2,1,0:T(8,128)(2,1)S(1)}, bf16[8,64,128]{2,1,0:T(8,128)(2,1)}, u32[]{:S(2)}) copy-start(bf16[8,64,128]{2,1,0:T(8,128)(2,1)} %get-tuple-element.45) | copy-start | bytes 393220
  188.7 34.7 %all-to-all-start.5 = ((bf16[64,24,128]{2,1,0:T(8,128)(2,1)}), bf16[64,24,128]{2,1,0:T(8,128)(2,1)S(1)}, u32[]{:S(2)}, u32[]{:S(2)}) async-start(bf16[64,24,128]{2,1,0:T(8,128)(2,1)} %pad_maximum_fusion.1), calls=%async_computation.5 | async-start | bytes 786432 | tf_op jit(solution)/shard_map/all_to_all | solution.py:25
  224.2 8.7 %all-to-all-start.6 = ((bf16[8,64,128]{2,1,0:T(8,128)(2,1)}), bf16[8,64,128]{2,1,0:T(8,128)(2,1)S(1)}, u32[]{:S(2)}, u32[]{:S(2)}) async-start(bf16[8,64,128]{2,1,0:T(8,128)(2,1)} %bitcast.93), calls=%async_computation.6 | async-start | bytes 262144 | tf_op jit(solution)/shard_map/all_to_all | solution.py:25
  246.4 3.8 %copy-start.9 = (bf16[64,2048]{1,0:T(8,128)(2,1)S(1)}, bf16[64,2048]{1,0:T(8,128)(2,1)}, u32[]{:S(2)}) copy-start(bf16[64,2048]{1,0:T(8,128)(2,1)} %get-tuple-element.55) | copy-start | bytes 786436
  246.4 25.7 %all-to-all-start.7 = ((bf16[8,672,128]{2,1,0:T(8,128)(2,1)}), bf16[8,672,128]{2,1,0:T(8,128)(2,1)S(1)}, u32[]{:S(2)}, u32[]{:S(2)}) async-start(bf16[8,672,128]{2,1,0:T(8,128)(2,1)} %get-tuple-element.53), calls=%async_computation.7 | async-start | bytes 2752512 | tf_op jit(solution)/shard_map/all_to_all | solution.py:25
  273.1 33.9 %copy-start.5 = (bf16[640,128]{1,0:T(8,128)(2,1)S(1)}, bf16[640,128]{1,0:T(8,128)(2,1)}, u32[]{:S(2)}) copy-start(bf16[640,128]{1,0:T(8,128)(2,1)} %get-tuple-element.35.refs_0_) | copy-start | bytes 491524
  273.1 34.0 %copy-start.4 = (f32[512,128]{1,0:T(8,128)S(1)}, f32[512,128]{1,0:T(8,128)}, u32[]{:S(2)}) copy-start(f32[512,128]{1,0:T(8,128)} %get-tuple-element.56) | copy-start | bytes 786436
  273.1 33.8 %all-to-all-start.8 = ((bf16[64,24,128]{2,1,0:T(8,128)(2,1)}), bf16[64,24,128]{2,1,0:T(8,128)(2,1)S(1)}, u32[]{:S(2)}, u32[]{:S(2)}) async-start(bf16[64,24,128]{2,1,0:T(8,128)(2,1)} %pad_maximum_fusion.2), calls=%async_computation.8 | async-start | bytes 786432 | tf_op jit(solution)/shard_map/all_to_all | solution.py:25
  277.9 35.0 %copy-start.8 = (f32[512,1]{1,0:T(8,128)S(1)}, f32[512,1]{1,0:T(8,128)}, u32[]{:S(2)}) copy-start(f32[512,1]{1,0:T(8,128)} %get-tuple-element.54) | copy-start | bytes 6148
  308.4 28.3 %all-to-all-start.9 = ((bf16[64,16,128]{2,1,0:T(8,128)(2,1)}), bf16[64,16,128]{2,1,0:T(8,128)(2,1)S(1)}, u32[]{:S(2)}, u32[]{:S(2)}) async-start(bf16[64,16,128]{2,1,0:T(8,128)(2,1)} %broadcast_in_dim.52), calls=%async_computation.9 | async-start | bytes 524288 | tf_op jit(solution)/shard_map/all_to_all | solution.py:25
  313.1 28.0 %copy-start.6 = (bf16[1,512,128]{2,1,0:T(8,128)(2,1)S(1)}, bf16[1,512,128]{2,1,0:T(8,128)(2,1)}, u32[]{:S(2)}) copy-start(bf16[1,512,128]{2,1,0:T(8,128)(2,1)} %param.10) | copy-start | bytes 393220
  337.6 12.1 %all-to-all-start.10 = ((bf16[8,200,128]{2,1,0:T(8,128)(2,1)}), bf16[8,200,128]{2,1,0:T(8,128)(2,1)S(1)}, u32[]{:S(2)}, u32[]{:S(2)}) async-start(bf16[8,200,128]{2,1,0:T(8,128)(2,1)} %broadcast_in_dim.53), calls=%async_computation.10 | async-start | bytes 819200 | tf_op jit(solution)/shard_map/all_to_all | solution.py:25
  349.8 0.8 copy-start.1
